TPU v7x, 32 devices: a whole 2x2x4 slice. The times are simulated.
32 devices in a mesh: gx: 4 (over x, core), gy: 4 (over z), row: 2 (over y).
Axes of the slice: x: 2, y: 2, z: 4, core: 2. Of those that a mesh axis runs over, the one named last changes fastest.
Arguments:
- concentrations: float32 [2, 64, 128, 256], P(None, 'gx', 'gy', 'row'), may hold values from 0 to 1
- diffusivity: float32 [64, 128, 256], P('gx', 'gy', 'row'), may hold values from 0.25 to 1
- weight_first: bfloat16 [512, 1024], replicated, may hold values from -0.25 to 0.25
- weight_middle: bfloat16 [1024, 1024], replicated, may hold values from -0.1875 to 0.1875
- weight_last: bfloat16 [1024, 512], replicated, may hold values from -0.1875 to 0.1875
Outputs:
- concentrations_out: float32 [2, 64, 128, 256], P(None, 'gx', 'gy', 'row')
- grad_first: float32 [512, 1024], P(('gx', 'gy', 'row'))
- grad_middle: float32 [1024, 1024], P(('gx', 'gy', 'row'))
- grad_last: float32 [1024, 512], P(('gx', 'gy', 'row'))
All inputs are finite; a program needn't handle non-finite values.
Results may differ from a plain program's by a relative error of at most 0.00035.
Values may be sent and summed in bfloat16 or wider, within the bound.
No kernel may reach another device: no remote copies, remote signals or barrier semaphores. Data moves between devices by JAX's collectives and lax.ppermute only.
A program may use at most 128 MiB of HBM per device.

v0:
```python
import functools
import math

import jax
import jax.numpy as jnp
from jax import lax
from jax.experimental import pallas as pl
from jax.experimental.pallas import tpu as pltpu
from jax.sharding import PartitionSpec as P

STEPS = 6
PATCH = 8
HALO = STEPS // 2
EDGE = 4
VMEM_LIMIT = 20 << 20


def ring(array, axis, distance):
    size = lax.axis_size(axis)
    return lax.ppermute(array, axis, [(i, (i + distance) % size) for i in range(size)])


def react(activator, inhibitor, diffusivity, lap_activator, lap_inhibitor, forcing):
    product = activator * inhibitor * inhibitor
    inner = diffusivity * lap_activator - product + 0.04 * (1.0 - activator)
    new_activator = activator + 0.1 * (inner if forcing is None else inner + forcing)
    new_inhibitor = inhibitor + 0.1 * (
        0.5 * diffusivity * lap_inhibitor + product - 0.1 * inhibitor
    )
    return (new_activator, new_inhibitor)


def fields(state, third):
    return ((lambda x, rows: state[0, x, rows, :], HALO), (lambda x, rows: state[1, x, rows, :], HALO),
            (lambda x, rows: third[x, rows, :], HALO - 1))


def plane_of(state, third, before, after, kind, plane, rows):
    read, depth = fields(state, third)[kind]
    length = state.shape[1]
    x = plane - HALO
    if x < -depth or x >= length + depth:
        return None
    if x < 0:
        return before[kind * HALO + depth + x, rows, :]
    if x >= length:
        return after[kind * HALO + x - length, rows, :]
    return read(x, rows)


def edge_rows_body(state, third, before, after, leading_ref, trailing_ref):
    length, height = state.shape[1:3]
    for plane in range(length + 2 * HALO):
        for kind, depth in enumerate((HALO, HALO, HALO - 1)):
            for out_ref, start in ((leading_ref, 0), (trailing_ref, height - depth)):
                value = plane_of(state, third, before, after, kind, plane, slice(start, start + depth))
                if value is None:
                    value = jnp.zeros((depth, state.shape[3]), jnp.float32)
                out_ref[plane, kind * HALO:kind * HALO + depth, :] = value


def strips_of(planes, width):
    each = width // (2 * HALO)
    places = {}
    for kind in range(3):
        for plane in range(kind // 2, planes - kind // 2):
            number = len(places)
            places[kind, plane] = (number // each, (number % each) * 2 * HALO)
    return places, -(-len(places) // each)


def assemble_body(state, third, before, after, below, above, whole_ref, strips_ref):
    length, height, width = state.shape[1:]
    planes = length + 2 * HALO
    places, _ = strips_of(planes, width)
    lanes = lax.broadcasted_iota(jnp.int32, whole_ref.shape[2:], 1)
    tiles = {}
    for kind, depth in enumerate((HALO, HALO, HALO - 1)):
        for plane in range(planes):
            value = plane_of(state, third, before, after, kind, plane, slice(0, height))
            if value is None:
                continue
            held = slice(kind * HALO, kind * HALO + depth)
            whole_ref[kind, plane, EDGE:EDGE + height, :] = value
            whole_ref[kind, plane, EDGE - depth:EDGE, :] = below[plane, held, :]
            whole_ref[kind, plane, EDGE + height:EDGE + height + depth, :] = above[plane, held, :]
            tile, shift = places[kind, plane]
            turned = pltpu.roll(whole_ref[kind, plane], (shift + HALO) % width, axis=1)
            here = (lanes >= shift) & (lanes < shift + 2 * HALO)
            tiles[tile] = jnp.where(here, turned, tiles[tile]) if tile in tiles else turned
    for tile, value in tiles.items():
        strips_ref[tile] = value


def load_wide(whole, earlier, later, kind, target, places):
    rows, width = whole.shape[2:]
    lanes = lax.broadcasted_iota(jnp.int32, (rows, width), 1)
    for plane in range(whole.shape[1]):
        if (kind, plane) not in places:
            continue
        tile, shift = places[kind, plane]
        back = (2 * width - shift - HALO) % width
        beside = later[tile] if later is earlier else jnp.where(
            (lanes >= shift + HALO) & (lanes < shift + 2 * HALO), later[tile], earlier[tile])
        target[plane, 8:8 + rows, :width] = whole[kind, plane]
        target[plane, 8:8 + rows, width:] = pltpu.roll(beside, back, axis=1)


def one_step(source, target, diffusivity, forcing, planes, rows):
    first, last = rows

    def one_plane(plane, carry):
        laps = []
        for field in source:
            center = field[plane, first:last, :]
            width = center.shape[1]
            summed = -6.0 * center + field[plane + 1, first:last, :] + field[plane - 1, first:last, :]
            summed = summed + field[plane, first + 1:last + 1, :] + field[plane, first - 1:last - 1, :]
            laps.append(summed + pltpu.roll(center, 1, axis=1) + pltpu.roll(center, width - 1, axis=1))
        extra = None if forcing is None else forcing[plane, first:last, :]
        new = react(source[0][plane, first:last, :], source[1][plane, first:last, :],
                    diffusivity[plane, first:last, :], *laps, extra)
        for field, value in zip(target, new):
            field[plane, first:last, :] = value
        return carry

    lax.fori_loop(planes[0], planes[1], one_plane, 0)


def run_steps(now, then, diffusivity, forcing, rows):
    planes = now[0].shape[0]
    for step in range(HALO):
        one_step(now, then, diffusivity, forcing, (step + 1, planes - step - 1), (8, 8 + rows))
        now, then = then, now
    return now


def move_order(patches_z, edge):
    lanes = patches_z * edge
    row = lax.broadcasted_iota(jnp.int32, (lanes, lanes), 0)
    column = lax.broadcasted_iota(jnp.int32, (lanes, lanes), 1)
    return jnp.where((row % patches_z) * edge + row // patches_z == column, 1.0, 0.0).astype(jnp.bfloat16)


def cell_order(edge):
    cells = edge ** 3
    row = lax.broadcasted_iota(jnp.int32, (cells, cells), 0)
    column = lax.broadcasted_iota(jnp.int32, (cells, cells), 1)
    return jnp.where((row % (edge * edge)) * edge + row // (edge * edge) == column, 1.0, 0.0).astype(jnp.bfloat16)


def half_tiles(source, count, rows, by_lane):
    half = by_lane // 2
    lanes = lax.broadcasted_iota(jnp.int32, (rows, by_lane), 1)
    out = []
    for b in range(count[1]):
        tiles = []
        for a in range(0, count[0], 2):
            low, high = [source[n * rows:(n + 1) * rows, (b // 2) * by_lane:(b // 2 + 1) * by_lane] for n in (a, a + 1)]
            if b % 2 == 0:
                high = pltpu.roll(high, half, axis=1)
            else:
                low = pltpu.roll(low, half, axis=1)
            tiles.append(jnp.where(lanes < half, low, high))
        out.append(jnp.concatenate(tiles, axis=1))
    return jnp.concatenate(out, axis=0)


def cube_starts(shape, edge):
    extent_x, extent_y = shape
    return [(px * edge + ix, py * edge) for px in range(extent_x // edge) for py in range(extent_y // edge)
            for ix in range(edge)]


def exact_product(left, right):
    high = left.astype(jnp.bfloat16)
    low = (left - high.astype(jnp.float32)).astype(jnp.bfloat16)
    return product(high, right) + product(low, right)


def first_steps_body(edge, whole, earlier, later, state_ref, own_ref, wide_ref, u0, v0, u1, v1, wide, column_ref, semaphores):
    length, height, width = state_ref.shape[1:]
    places, _ = strips_of(whole.shape[1], width)
    for kind, target in enumerate((u0, v0, wide)):
        load_wide(whole, earlier, later, kind, target, places)
    (copy,) = start_copies([(wide, wide_ref)], semaphores)
    now = run_steps((u0, v0), (u1, v1), wide, None, whole.shape[2])
    move, order = (move_order(width // edge, edge), cell_order(edge))
    count = own_ref.shape[0] // 2
    for species, field in enumerate(now):
        for x in range(length):
            state_ref[species, x] = field[x + HALO, 8 + EDGE:8 + EDGE + height, :width]
        for number, (x, y) in enumerate(cube_starts((length, height), edge)):
            column_ref[number * edge:(number + 1) * edge, :] = state_ref[species, x, y:y + edge, :]
        turned = product_transposed(move, column_ref[...].astype(jnp.bfloat16))
        columns = length * height // (edge * edge)
        cubes = half_tiles(turned, (edge, columns), width // edge, 2 * edge * edge)
        own_ref[species * count:(species + 1) * count, :] = product(cubes.astype(jnp.bfloat16), order).astype(jnp.bfloat16)
    copy.wait()


def own_forward_body(edge, own_ref, first_ref, middle_ref, last_ref, field_ref):
    length, height, width = field_ref.shape
    count = own_ref.shape[0] // 2
    h1 = gelu_value(product(own_ref[:count, :], first_ref[...])).astype(jnp.bfloat16)
    h2 = gelu_value(product(h1, middle_ref[...])).astype(jnp.bfloat16)
    forcing = product(h2, last_ref[...])
    cells = lax.broadcasted_iota(jnp.int32, (edge ** 3, edge ** 3), 1)
    row = lax.broadcasted_iota(jnp.int32, (edge ** 3, edge ** 3), 0)
    square = edge * edge
    order = jnp.where((cells % square) * edge + cells // square == row, 1.0, 0.0).astype(jnp.bfloat16)
    columns = length * height // square
    turned = half_tiles(exact_product(forcing, order), (columns, edge), width // edge, 2 * square)
    moved = exact_product(turned.T, move_order(width // edge, edge))
    for number, (x, y) in enumerate(cube_starts((length, height), edge)):
        field_ref[x, y:y + edge, :] = moved[number * edge:(number + 1) * edge, :]


def last_steps_body(whole, earlier, later, wide, state_ref, u0, v0, u1, v1, force):
    length, height, width = state_ref.shape[1:]
    places, _ = strips_of(whole.shape[1], width)
    for kind, target in enumerate((u0, v0, force)):
        load_wide(whole, earlier, later, kind, target, places)
    now = run_steps((u0, v0), (u1, v1), wide, force, whole.shape[2])
    for species, field in enumerate(now):
        for x in range(length):
            state_ref[species, x] = field[x + HALO, 8 + EDGE:8 + EDGE + height, :width]


def start_copies(pairs, semaphores):
    copies = [pltpu.make_async_copy(*pair, semaphores.at[number]) for number, pair in enumerate(pairs)]
    for copy in copies:
        copy.start()
    return copies


def store_faces(state, third, leading_ref, trailing_ref):
    length = third.shape[0]
    for kind, depth in enumerate((HALO, HALO, HALO - 1)):
        read = fields(state, third)[kind][0]
        for plane in range(depth):
            leading_ref[kind * HALO + plane] = read(plane, slice(None))
            trailing_ref[kind * HALO + plane] = read(length - depth + plane, slice(None))


def first_faces_body(state_ref, third_ref, leading_ref, trailing_ref, state_out, third_out, semaphores):
    for copy in start_copies(((state_ref, state_out), (third_ref, third_out)), semaphores):
        copy.wait()
    store_faces(state_out, third_out, leading_ref, trailing_ref)


def x_halos(leading, trailing):
    return ring(trailing, "gx", 1), ring(leading, "gx", -1)


def edge_rows(state, third, before, after):
    planes = state.shape[1] + 2 * HALO
    return kernel_call(edge_rows_body, [((planes, 3 * HALO - 1, state.shape[3]), jnp.float32)] * 2)(
        state, third, before, after
    )


def y_halos(leading, trailing):
    return ring(trailing, "gy", 1), ring(leading, "gy", -1)


def assemble(state, third, before, after, below, above):
    length, height, width = state.shape[1:]
    planes, rows = (length + 2 * HALO, height + 2 * EDGE)
    outputs = [(3, planes, rows, width), (strips_of(planes, width)[1], rows, width)]
    return kernel_call(assemble_body, [(shape, jnp.float32) for shape in outputs])(
        state, third, before, after, below, above
    )


def z_strips(strips):
    earlier = ring(strips, "row", 1)
    return earlier, (earlier if lax.axis_size("row") == 2 else ring(strips, "row", -1))


def exchange(array, mesh_sizes, flips):
    size_x, size_y, size_r = mesh_sizes
    route = []
    for i in range(size_x):
        for j in range(size_y):
            for k in range(size_r):
                here = (i * size_y + j) * size_r + k
                there = ((i ^ flips[0]) * size_y + (j ^ flips[1])) * size_r + (k ^ flips[2])
                route.append((here, there))
    return lax.ppermute(array, ("gx", "gy", "row"), route)


def reduction_stages(mesh_sizes):
    size_x, size_y, _ = mesh_sizes
    stages = []
    bit = 1
    while bit < size_x:
        stages.append((bit, 0, 0))
        bit *= 2
    bit = 2
    while bit < size_y:
        stages.append((0, bit, 0))
        bit *= 2
    return stages


def chosen_rows(total, mesh_sizes):
    size_x, size_y, size_r = mesh_sizes
    stages = reduction_stages(mesh_sizes)
    unit = total // (size_x * size_y * size_r)
    blocks = 1 << len(stages)
    position = jnp.arange(blocks * unit, dtype=jnp.int32)
    place, inner = (position // unit, position % unit)
    x = jnp.zeros_like(position) + lax.axis_index("gx")
    y = jnp.zeros_like(position) + lax.axis_index("gy")
    for number, (bit_x, bit_y, _) in enumerate(stages):
        leaves = 1 - (place >> (len(stages) - 1 - number)) % 2
        x = x ^ (leaves * bit_x)
        y = y ^ (leaves * bit_y)
    block = (x * size_y + y) * size_r + lax.axis_index("row")
    return (block * unit + inner)[:, None]


def halved(leaving, staying, flips, mesh_sizes):
    arrived = exchange(leaving, mesh_sizes, flips)
    half = staying.shape[0] // 2
    return staying[:half] + arrived[:half], staying[half:] + arrived[half:]


def rest_halved(leaving, staying, stages, done, mesh_sizes):
    for number in range(done, len(stages) - 1):
        leaving, staying = halved(leaving, staying, stages[number], mesh_sizes)
    return staying + exchange(leaving, mesh_sizes, stages[-1])


def gelu_pair(values):
    root = math.sqrt(2.0 / math.pi)
    square = values * values
    bend = jnp.tanh(values * (root + (root * 0.044715) * square))
    cdf = 0.5 + 0.5 * bend
    slope = cdf + (0.5 * values) * (1.0 - bend * bend) * (root + (3.0 * root * 0.044715) * square)
    return values * cdf, slope


def gelu_value(values):
    root = math.sqrt(2.0 / math.pi)
    return values * (0.5 + 0.5 * jnp.tanh(values * (root + (root * 0.044715) * (values * values))))


def product(left, right):
    return jnp.dot(left, right, preferred_element_type=jnp.float32)


def product_transposed(left, right):
    return lax.dot_general(left, right, (((1,), (1,)), ((), ())), preferred_element_type=jnp.float32)


def transposed_choice(rows, source):
    columns = lax.broadcasted_iota(jnp.int32, (rows.shape[0], source.shape[1]), 1)
    choice = jnp.where(columns == rows, 1.0, 0.0).astype(jnp.bfloat16)
    return product_transposed(choice, source).astype(jnp.bfloat16)


def column_tiles(width):
    tile = 256 if width % 256 == 0 else width
    return [slice(start, start + tile) for start in range(0, width, tile)]


def store_halves(value, columns, leaving_ref, staying_ref):
    half = value.shape[0] // 2
    leaving_ref[:, columns] = value[:half]
    staying_ref[:, columns] = value[half:]


def forward_body(scale, own_ref, a_ref, b_ref, c_ref, first_ref, middle_ref, last_ref, rows_ref,
                 x_ref, h1_ref, s1_ref, h2_ref, s2_ref, error_ref, leaving_ref, staying_ref, first_near, last_near, semaphores):
    first_copy, last_copy = start_copies(((first_ref, first_near), (last_ref, last_near)), semaphores)
    count = own_ref.shape[0] // 2
    parts = (own_ref, a_ref, b_ref, c_ref)
    for number, part in enumerate(parts):
        x_ref[number * count:(number + 1) * count, :] = part[:count, :]
    x = x_ref[...]
    first_copy.wait()
    for columns in column_tiles(h1_ref.shape[1]):
        value, slope = gelu_pair(product(x, first_near[:, columns]))
        h1_ref[:, columns] = value.astype(jnp.bfloat16)
        s1_ref[:, columns] = slope
    h1 = h1_ref[...]
    for columns in column_tiles(h2_ref.shape[1]):
        value, slope = gelu_pair(product(h1, middle_ref[:, columns]))
        h2_ref[:, columns] = value.astype(jnp.bfloat16)
        s2_ref[:, columns] = slope
    h2 = h2_ref[...]
    last_copy.wait()
    for columns in column_tiles(error_ref.shape[1]):
        forcing = product(h2, last_near[:, columns])
        for number, part in enumerate(parts):
            block = slice(number * count, (number + 1) * count)
            target = part[count:, columns].astype(jnp.float32)
            error_ref[block, columns] = ((forcing[block] - target) * scale).astype(jnp.bfloat16)
    chosen = transposed_choice(rows_ref[...], h2)
    for columns in column_tiles(error_ref.shape[1]):
        store_halves(product(chosen, error_ref[:, columns]), columns, leaving_ref, staying_ref)


def backward_body(carried_ref, weight_ref, slope_ref, source_ref, rows_ref, back_ref, leaving_ref, staying_ref):
    carried = carried_ref[...]
    for columns in column_tiles(back_ref.shape[1]):
        value = product_transposed(carried, weight_ref[columns, :]) * slope_ref[:, columns]
        back_ref[:, columns] = value.astype(jnp.bfloat16)
    chosen = transposed_choice(rows_ref[...], source_ref[...])
    for columns in column_tiles(back_ref.shape[1]):
        store_halves(product(chosen, back_ref[:, columns]), columns, leaving_ref, staying_ref)


def tied(value, *others):
    return lax.optimization_barrier((value, *others))[0]


def kernel_call(body, outputs, scratch=(), flops=1 << 24, far=(), far_outputs=(), copies=0):
    def call(*inputs):
        near, away = (pl.BlockSpec(memory_space=pltpu.VMEM), pl.BlockSpec(memory_space=pltpu.HBM))
        result = pl.pallas_call(
            body,
            cost_estimate=pl.CostEstimate(flops=flops, transcendentals=0, bytes_accessed=0),
            in_specs=[away if number in far else near for number in range(len(inputs))],
            out_specs=[away if number in far_outputs else near for number in range(len(outputs))],
            out_shape=[(pltpu.HBM if number in far_outputs else jax.ShapeDtypeStruct)(shape, dtype)
                       for number, (shape, dtype) in enumerate(outputs)],
            scratch_shapes=[pltpu.VMEM(shape, dtype) for shape, dtype in scratch]
            + [pltpu.SemaphoreType.DMA((copies,))] * (copies > 0),
            compiler_params=pltpu.CompilerParams(vmem_limit_bytes=VMEM_LIMIT),
        )(*(pltpu.with_memory_space_constraint(array, pltpu.HBM) if number in far else array
            for number, array in enumerate(inputs)))
        return result

    return call


def all_steps(concentrations, diffusivity, weight_first, weight_middle, weight_last):
    mesh_sizes = tuple(lax.axis_size(axis) for axis in ("gx", "gy", "row"))
    length, height, width = diffusivity.shape
    f32, bf16 = (jnp.float32, jnp.bfloat16)
    planes, rows = (length + 2 * HALO, height + 2 * EDGE)
    wide = ((planes, 8 + rows + 8, 2 * width), f32)
    count = length * height * width // PATCH ** 3
    cells, hidden = weight_first.shape
    hidden_second = weight_middle.shape[1]
    total = 4 * count
    rows_first, rows_middle, rows_last = [chosen_rows(size, mesh_sizes) for size in (cells, hidden, hidden_second)]
    half_of = lambda chosen, width: ((chosen.shape[0] // 2, width), f32)
    stages = reduction_stages(mesh_sizes)
    big = 1 << 32

    layers = ((3 * HALO - 1, height, width), f32)
    weights = (weight_first, weight_middle, weight_last)
    leading, trailing, near_state, near_third = kernel_call(
        first_faces_body, [layers, layers, (concentrations.shape, f32), (diffusivity.shape, f32)],
        far=(0, 1), copies=2,
    )(concentrations, diffusivity)
    before, after = x_halos(leading, trailing)
    leading, trailing = edge_rows(near_state, near_third, before, after)
    below, above = y_halos(leading, trailing)
    whole, strips = assemble(near_state, near_third, before, after, below, above)
    state, own, wide_diffusivity = kernel_call(
        functools.partial(first_steps_body, PATCH),
        [(concentrations.shape, f32), ((2 * count, cells), bf16), wide],
        scratch=[wide] * 5 + [((length * height, width), f32)],
        far_outputs=(2,), copies=1,
    )(whole, *z_strips(strips))

    others = [exchange(own, mesh_sizes, flips) for flips in ((0, 0, 1), (0, 1, 0), (0, 1, 1))]
    (field,) = kernel_call(functools.partial(own_forward_body, PATCH), [(diffusivity.shape, f32)], flops=big // 4)(
        own, *weights
    )
    leading, trailing = kernel_call(store_faces, [layers, layers])(state, field)
    before, after = x_halos(leading, trailing)
    leading, trailing = edge_rows(state, field, before, after)
    below, above = y_halos(leading, trailing)
    x, h1, s1, h2, s2, error, *last = kernel_call(
        functools.partial(forward_body, 1.0 / count),
        [((total, cells), bf16), ((total, hidden), bf16), ((total, hidden), f32), ((total, hidden_second), bf16),
         ((total, hidden_second), f32), ((total, cells), bf16),
         half_of(rows_last, cells), half_of(rows_last, cells)],
        scratch=[(weight_first.shape, bf16), (weight_last.shape, bf16)],
        flops=big, far=(4, 6), copies=2,
    )(tied(own, leading, trailing), *others, *weights, rows_last)
    last = halved(*last, stages[0], mesh_sizes)
    whole, strips = assemble(state, field, before, after, tied(below, error), above)
    back_second, *middle = kernel_call(
        backward_body,
        [((total, hidden_second), bf16), half_of(rows_middle, hidden_second), half_of(rows_middle, hidden_second)],
        flops=big // 2,
    )(tied(error, strips, last[0]), weights[2], s2, h1, rows_middle)
    middle = halved(*middle, stages[0], mesh_sizes)
    last = halved(*last, stages[1], mesh_sizes)
    back_first, *first = kernel_call(
        backward_body,
        [((total, hidden), bf16), half_of(rows_first, hidden), half_of(rows_first, hidden)],
        flops=big // 2,
    )(tied(back_second, last[0], middle[0]), weights[1], s1, x, rows_first)
    first = halved(*first, stages[0], mesh_sizes)
    middle = halved(*middle, stages[1], mesh_sizes)
    (state,) = kernel_call(last_steps_body, [(state.shape, f32)], scratch=[wide] * 5, flops=big)(
        tied(whole, first[0], middle[0], last[0]), *z_strips(strips), wide_diffusivity
    )
    grads = [rest_halved(*part, stages, done, mesh_sizes) for part, done in ((first, 1), (middle, 2), (last, 2))]
    return (state, *grads)


def solution(mesh):
    in_specs = (P(None, "gx", "gy", "row"), P("gx", "gy", "row"), P(), P(), P())
    out_specs = (
        P(None, "gx", "gy", "row"),
        P(("gx", "gy", "row"), None),
        P(("gx", "gy", "row"), None),
        P(("gx", "gy", "row"), None),
    )
    return jax.shard_map(all_steps, mesh=mesh, in_specs=in_specs, out_specs=out_specs, check_vma=False)
```

profile of v0, /device:TPU:0, one launch (start us, length us, event | category | flops | bytes accessed | tf_op | source)
XLA Modules:
  0.0 94.3 jit_solution(17566918834208028171)
XLA Ops:
  2.4 2.0 %collective-permute-start.1 = (f32[8,32,128]{2,1,0:T(8,128)S(1)}, f32[8,32,128]{2,1,0:T(8,128)S(1)}, u32[]{:S(2)}, u32[]{:S(2)}) collective-permute-start(f32[8,32,128]{2,1,0:T(8,128)S(1)} %get-tuple-element.41), channel_id=1, source_target_pairs={{0,24},{8,0},{16,8},{24,16},{1,25},{9,1},{17,9},{25,17},{2,26},{10... | collective-permute-start | bytes 393224 | tf_op jit(solution)/shard_map/ppermute | solution.py:20
  4.4 2.6 %collective-permute-done.before = f32[8,32,128]{2,1,0:T(8,128)S(1)} collective-permute-done((f32[8,32,128]{2,1,0:T(8,128)S(1)}, f32[8,32,128]{2,1,0:T(8,128)S(1)}, u32[]{:S(2)}, u32[]{:S(2)}) %collective-permute-start) | collective-permute-done | bytes 131104 | tf_op jit(solution)/shard_map/ppermute | solution.py:20
  8.3 1.6 %collective-permute-start.2 = (f32[22,8,128]{2,1,0:T(8,128)S(1)}, f32[22,8,128]{2,1,0:T(8,128)S(1)}, u32[]{:S(2)}, u32[]{:S(2)}) collective-permute-start(f32[22,8,128]{2,1,0:T(8,128)S(1)} %get-tuple-element.42), channel_id=1, source_target_pairs={{0,2},{2,4},{4,6},{6,0},{1,3},{3,5},{5,7},{7,1},{8,10},{10,12},{12... | collective-permute-start | bytes 270344 | tf_op jit(solution)/shard_map/ppermute | solution.py:20
  9.9 2.2 %collective-permute-start.3 = (f32[22,8,128]{2,1,0:T(8,128)S(1)}, f32[22,8,128]{2,1,0:T(8,128)S(1)}, u32[]{:S(2)}, u32[]{:S(2)}) collective-permute-start(f32[22,8,128]{2,1,0:T(8,128)S(1)} %get-tuple-element.43), channel_id=1, source_target_pairs={{0,6},{2,0},{4,2},{6,4},{1,7},{3,1},{5,3},{7,5},{8,14},{10,8},{12,... | collective-permute-start | bytes 270344 | tf_op jit(solution)/shard_map/ppermute | solution.py:20
  12.2 3.3 %collective-permute-done.2.below = f32[22,8,128]{2,1,0:T(8,128)S(1)} collective-permute-done((f32[22,8,128]{2,1,0:T(8,128)S(1)}, f32[22,8,128]{2,1,0:T(8,128)S(1)}, u32[]{:S(2)}, u32[]{:S(2)}) %collective-permute-start.2) | collective-permute-done | bytes 90144 | tf_op jit(solution)/shard_map/ppermute | solution.py:20
  15.4 1.8 %collective-permute-done.3.above = f32[22,8,128]{2,1,0:T(8,128)S(1)} collective-permute-done((f32[22,8,128]{2,1,0:T(8,128)S(1)}, f32[22,8,128]{2,1,0:T(8,128)S(1)}, u32[]{:S(2)}, u32[]{:S(2)}) %collective-permute-start.3) | collective-permute-done | bytes 90144 | tf_op jit(solution)/shard_map/ppermute | solution.py:20
  17.7 1.6 %collective-permute-start.4 = (f32[4,40,128]{2,1,0:T(8,128)S(1)}, f32[4,40,128]{2,1,0:T(8,128)S(1)}, u32[]{:S(2)}, u32[]{:S(2)}) collective-permute-start(f32[4,40,128]{2,1,0:T(8,128)S(1)} %get-tuple-element.45), channel_id=1, source_target_pairs={{0,1},{1,0},{2,3},{3,2},{4,5},{5,4},{6,7},{7,6},{8,9},{9,8},{10,11... | collective-permute-start | bytes 245768 | tf_op jit(solution)/shard_map/ppermute | solution.py:20
  19.3 2.9 %collective-permute-done.4.earlier.later = f32[4,40,128]{2,1,0:T(8,128)S(1)} collective-permute-done((f32[4,40,128]{2,1,0:T(8,128)S(1)}, f32[4,40,128]{2,1,0:T(8,128)S(1)}, u32[]{:S(2)}, u32[]{:S(2)}) %collective-permute-start.4) | collective-permute-done | bytes 81952 | tf_op jit(solution)/shard_map/ppermute | solution.py:20
  22.2 8.1 %shard_map.87 = (f32[2,16,32,128]{3,2,1,0:T(8,128)S(1)}, bf16[256,512]{1,0:T(8,128)(2,1)S(1)}, f32[22,56,256]{2,1,0:T(8,128)}) custom-call(f32[3,22,40,128]{3,2,1,0:T(8,128)S(1)} %get-tuple-element.44.whole, f32[4,40,128]{2,1,0:T(8,128)S(1)} %collective-permute-done.4.earlier.later, f32[4,40,128]{2,1,0:T(8,128)S(1)} %collective-permute-done.4.earlier.later), custom_call_target="tpu_custom_call" | custom-call | flops 16777216 | tf_op jit(solution)/shard_map/pallas_call | solution.py:423
  30.3 1.9 %collective-permute-start.10 = (bf16[256,512]{1,0:T(8,128)(2,1)S(1)}, bf16[256,512]{1,0:T(8,128)(2,1)}, u32[]{:S(2)}, u32[]{:S(2)}) collective-permute-start(bf16[256,512]{1,0:T(8,128)(2,1)S(1)} %get-tuple-element.52.own_ref), channel_id=1, source_target_pairs={{0,3},{1,2},{2,1},{3,0},{4,7},{5,6},{6,5},{7,4},{8,11},{9,10},{10,... | collective-permute-start | bytes 786440 | tf_op jit(solution)/shard_map/ppermute | solution.py:290
  33.9 1.5 %shard_map.88.third = f32[16,32,128]{2,1,0:T(8,128)S(1)} custom-call(bf16[256,512]{1,0:T(8,128)(2,1)S(1)} %get-tuple-element.52.own_ref, bf16[512,1024]{1,0:T(8,128)(2,1)S(1)} %copy-done.1, bf16[1024,1024]{1,0:T(8,128)(2,1)S(1)} %copy-done, bf16[1024,512]{1,0:T(8,128)(2,1)S(1)} %copy-done.2), custom_call_target="tpu_custom_call" | custom-call | flops 1073741824 | tf_op jit(solution)/shard_map/pallas_call | solution.py:423
  36.1 1.7 %collective-permute-start.6 = (f32[8,32,128]{2,1,0:T(8,128)S(1)}, f32[8,32,128]{2,1,0:T(8,128)S(1)}, u32[]{:S(2)}, u32[]{:S(2)}) collective-permute-start(f32[8,32,128]{2,1,0:T(8,128)S(1)} %get-tuple-element.49), channel_id=1, source_target_pairs={{0,24},{8,0},{16,8},{24,16},{1,25},{9,1},{17,9},{25,17},{2,26},{10... | collective-permute-start | bytes 393224 | tf_op jit(solution)/shard_map/ppermute | solution.py:20
  38.1 2.9 %collective-permute-done.5.before = f32[8,32,128]{2,1,0:T(8,128)S(1)} collective-permute-done((f32[8,32,128]{2,1,0:T(8,128)}, f32[8,32,128]{2,1,0:T(8,128)S(1)}, u32[]{:S(2)}, u32[]{:S(2)}) %collective-permute-start.5) | collective-permute-done | bytes 131104 | tf_op jit(solution)/shard_map/ppermute | solution.py:20
  41.0 3.1 %collective-permute-done.8.a_ref = bf16[256,512]{1,0:T(8,128)(2,1)} collective-permute-done((bf16[256,512]{1,0:T(8,128)(2,1)S(1)}, bf16[256,512]{1,0:T(8,128)(2,1)}, u32[]{:S(2)}, u32[]{:S(2)}) %collective-permute-start.8) | collective-permute-done | bytes 262176 | tf_op jit(solution)/shard_map/ppermute | solution.py:290
  44.2 7.9 %shard_map.91 = (bf16[512,512]{1,0:T(8,128)(2,1)S(1)}, bf16[512,1024]{1,0:T(8,128)(2,1)S(1)}, f32[512,1024]{1,0:T(8,128)S(1)}, bf16[512,1024]{1,0:T(8,128)(2,1)}...) custom-call(bf16[256,512]{1,0:T(8,128)(2,1)S(1)} %get-tuple-element.5, ...), custom_call_target="tpu_custom_call" | custom-call | flops 4294967296 | tf_op jit(solution)/shard_map/pallas_call | solution.py:423
  53.5 2.6 %collective-permute-start.11 = (f32[22,8,128]{2,1,0:T(8,128)S(1)}, f32[22,8,128]{2,1,0:T(8,128)S(1)}, u32[]{:S(2)}, u32[]{:S(2)}) collective-permute-start(f32[22,8,128]{2,1,0:T(8,128)S(1)} %get-tuple-element.51), channel_id=1, source_target_pairs={{0,6},{2,0},{4,2},{6,4},{1,7},{3,1},{5,3},{7,5},{8,14},{10,8},{12,... | collective-permute-start | bytes 270344 | tf_op jit(solution)/shard_map/ppermute | solution.py:20
  56.1 3.5 %collective-permute-done.7.below = f32[22,8,128]{2,1,0:T(8,128)S(1)} collective-permute-done((f32[22,8,128]{2,1,0:T(8,128)S(1)}, f32[22,8,128]{2,1,0:T(8,128)S(1)}, u32[]{:S(2)}, u32[]{:S(2)}) %collective-permute-start.7) | collective-permute-done | bytes 90144 | tf_op jit(solution)/shard_map/ppermute | solution.py:20
  64.0 4.0 %collective-permute-done.13 = f32[64,512]{1,0:T(8,128)S(1)} collective-permute-done((f32[64,512]{1,0:T(8,128)S(1)}, f32[64,512]{1,0:T(8,128)S(1)}, u32[]{:S(2)}, u32[]{:S(2)}) %collective-permute-start.13) | collective-permute-done | bytes 131104 | tf_op jit(solution)/shard_map/ppermute | solution.py:290
  68.0 1.5 %collective-permute-start.21 = (f32[32,512]{1,0:T(8,128)S(1)}, f32[32,512]{1,0:T(8,128)S(1)}, u32[]{:S(2)}, u32[]{:S(2)}) collective-permute-start(f32[32,512]{1,0:T(8,128)S(1)} %slice_add_fusion.11), channel_id=1, source_target_pairs={{0,4},{1,5},{2,6},{3,7},{4,0},{5,1},{6,2},{7,3},{8,12},{9,13},{10,... | collective-permute-start | bytes 196616 | tf_op jit(solution)/shard_map/ppermute | solution.py:290
  70.3 2.3 %shard_map.94 = (bf16[512,1024]{1,0:T(8,128)(2,1)}, f32[64,1024]{1,0:T(8,128)S(1)}, f32[64,1024]{1,0:T(8,128)S(1)}) custom-call(bf16[512,1024]{1,0:T(8,128)(2,1)S(1)} %get-tuple-element.65.carried_ref, bf16[1024,1024]{1,0:T(8,128)(2,1)S(1)} %copy-done, f32[512,1024]{1,0:T(8,128)S(1)} %get-tuple-element.66.slope_ref, ...), custom_call_target="tpu_custom_call" | custom-call | flops 2147483648 | tf_op jit(solution)/shard_map/pallas_call | solution.py:423
  74.6 2.6 %collective-permute-done.16 = f32[64,1024]{1,0:T(8,128)S(1)} collective-permute-done((f32[64,1024]{1,0:T(8,128)S(1)}, f32[64,1024]{1,0:T(8,128)S(1)}, u32[]{:S(2)}, u32[]{:S(2)}) %collective-permute-start.16) | collective-permute-done | bytes 262176 | tf_op jit(solution)/shard_map/ppermute | solution.py:290
  77.2 1.5 %collective-permute-start.20 = (f32[32,1024]{1,0:T(8,128)S(1)}, f32[32,1024]{1,0:T(8,128)S(1)}, u32[]{:S(2)}, u32[]{:S(2)}) collective-permute-start(f32[32,1024]{1,0:T(8,128)S(1)} %slice_add_fusion.4), channel_id=1, source_target_pairs={{0,4},{1,5},{2,6},{3,7},{4,0},{5,1},{6,2},{7,3},{8,12},{9,13},{10,... | collective-permute-start | bytes 393224 | tf_op jit(solution)/shard_map/ppermute | solution.py:290
  79.9 8.1 %shard_map.95 = f32[2,16,32,128]{3,2,1,0:T(8,128)} custom-call(f32[3,22,40,128]{3,2,1,0:T(8,128)S(1)} %get-tuple-element.70.whole, f32[4,40,128]{2,1,0:T(8,128)S(1)} %collective-permute-done.17.earlier.later, f32[4,40,128]{2,1,0:T(8,128)S(1)} %collective-permute-done.17.earlier.later, f32[22,56,256]{2,1,0:T(8,128)S(1)} %copy-done.4), custom_call_target="tpu_custom_call" | custom-call | flops 4294967296 | tf_op jit(solution)/shard_map/pallas_call | solution.py:423
  89.7 4.0 %collective-permute-done.19 = f32[16,1024]{1,0:T(8,128)S(1)} collective-permute-done((f32[16,1024]{1,0:T(8,128)S(1)}, f32[16,1024]{1,0:T(8,128)S(1)}, u32[]{:S(2)}, u32[]{:S(2)}) %collective-permute-start.19) | collective-permute-done | bytes 65568 | tf_op jit(solution)/shard_map/ppermute | solution.py:290
  (53 shorter events, 18.2 us)
Async XLA Ops:
  0.6 33.3 %copy-start.2 = (bf16[1024,512]{1,0:T(8,128)(2,1)S(1)}, bf16[1024,512]{1,0:T(8,128)(2,1)}, u32[]{:S(2)}) copy-start(bf16[1024,512]{1,0:T(8,128)(2,1)} %weight_ref.2) | copy-start | bytes 3145732
  1.9 32.0 %copy-start = (bf16[1024,1024]{1,0:T(8,128)(2,1)S(1)}, bf16[1024,1024]{1,0:T(8,128)(2,1)}, u32[]{:S(2)}) copy-start(bf16[1024,1024]{1,0:T(8,128)(2,1)} %weight_ref.3) | copy-start | bytes 6291460
  1.9 5.1 %collective-permute-start = (f32[8,32,128]{2,1,0:T(8,128)S(1)}, f32[8,32,128]{2,1,0:T(8,128)S(1)}, u32[]{:S(2)}, u32[]{:S(2)}) collective-permute-start(f32[8,32,128]{2,1,0:T(8,128)S(1)} %get-tuple-element.40), channel_id=1, source_target_pairs={{0,8},{8,16},{16,24},{24,0},{1,9},{9,17},{17,25},{25,1},{2,10},{10... | collective-permute-start | bytes 393224 | tf_op jit(solution)/shard_map/ppermute | solution.py:20
  2.4 5.8 %collective-permute-start.1 = (f32[8,32,128]{2,1,0:T(8,128)S(1)}, f32[8,32,128]{2,1,0:T(8,128)S(1)}, u32[]{:S(2)}, u32[]{:S(2)}) collective-permute-start(f32[8,32,128]{2,1,0:T(8,128)S(1)} %get-tuple-element.41), channel_id=1, source_target_pairs={{0,24},{8,0},{16,8},{24,16},{1,25},{9,1},{17,9},{25,17},{2,26},{10... | collective-permute-start | bytes 393224 | tf_op jit(solution)/shard_map/ppermute | solution.py:20
  8.3 7.2 %collective-permute-start.2 = (f32[22,8,128]{2,1,0:T(8,128)S(1)}, f32[22,8,128]{2,1,0:T(8,128)S(1)}, u32[]{:S(2)}, u32[]{:S(2)}) collective-permute-start(f32[22,8,128]{2,1,0:T(8,128)S(1)} %get-tuple-element.42), channel_id=1, source_target_pairs={{0,2},{2,4},{4,6},{6,0},{1,3},{3,5},{5,7},{7,1},{8,10},{10,12},{12... | collective-permute-start | bytes 270344 | tf_op jit(solution)/shard_map/ppermute | solution.py:20
  9.9 7.4 %collective-permute-start.3 = (f32[22,8,128]{2,1,0:T(8,128)S(1)}, f32[22,8,128]{2,1,0:T(8,128)S(1)}, u32[]{:S(2)}, u32[]{:S(2)}) collective-permute-start(f32[22,8,128]{2,1,0:T(8,128)S(1)} %get-tuple-element.43), channel_id=1, source_target_pairs={{0,6},{2,0},{4,2},{6,4},{1,7},{3,1},{5,3},{7,5},{8,14},{10,8},{12,... | collective-permute-start | bytes 270344 | tf_op jit(solution)/shard_map/ppermute | solution.py:20
  17.7 4.5 %collective-permute-start.4 = (f32[4,40,128]{2,1,0:T(8,128)S(1)}, f32[4,40,128]{2,1,0:T(8,128)S(1)}, u32[]{:S(2)}, u32[]{:S(2)}) collective-permute-start(f32[4,40,128]{2,1,0:T(8,128)S(1)} %get-tuple-element.45), channel_id=1, source_target_pairs={{0,1},{1,0},{2,3},{3,2},{4,5},{5,4},{6,7},{7,6},{8,9},{9,8},{10,11... | collective-permute-start | bytes 245768 | tf_op jit(solution)/shard_map/ppermute | solution.py:20
  30.3 10.7 %collective-permute-start.10 = (bf16[256,512]{1,0:T(8,128)(2,1)S(1)}, bf16[256,512]{1,0:T(8,128)(2,1)}, u32[]{:S(2)}, u32[]{:S(2)}) collective-permute-start(bf16[256,512]{1,0:T(8,128)(2,1)S(1)} %get-tuple-element.52.own_ref), channel_id=1, source_target_pairs={{0,3},{1,2},{2,1},{3,0},{4,7},{5,6},{6,5},{7,4},{8,11},{9,10},{10,... | collective-permute-start | bytes 786440 | tf_op jit(solution)/shard_map/ppermute | solution.py:290
  32.2 11.9 %collective-permute-start.8 = (bf16[256,512]{1,0:T(8,128)(2,1)S(1)}, bf16[256,512]{1,0:T(8,128)(2,1)}, u32[]{:S(2)}, u32[]{:S(2)}) collective-permute-start(bf16[256,512]{1,0:T(8,128)(2,1)S(1)} %get-tuple-element.52.own_ref), channel_id=1, source_target_pairs={{0,1},{1,0},{2,3},{3,2},{4,5},{5,4},{6,7},{7,6},{8,9},{9,8},{10,11... | collective-permute-start | bytes 786440 | tf_op jit(solution)/shard_map/ppermute | solution.py:290
  32.7 11.5 %collective-permute-start.9 = (bf16[256,512]{1,0:T(8,128)(2,1)S(1)}, bf16[256,512]{1,0:T(8,128)(2,1)}, u32[]{:S(2)}, u32[]{:S(2)}) collective-permute-start(bf16[256,512]{1,0:T(8,128)(2,1)S(1)} %get-tuple-element.52.own_ref), channel_id=1, source_target_pairs={{0,2},{1,3},{2,0},{3,1},{4,6},{5,7},{6,4},{7,5},{8,10},{9,11},{10,... | collective-permute-start | bytes 786440 | tf_op jit(solution)/shard_map/ppermute | solution.py:290
  36.1 4.8 %collective-permute-start.5 = (f32[8,32,128]{2,1,0:T(8,128)}, f32[8,32,128]{2,1,0:T(8,128)S(1)}, u32[]{:S(2)}, u32[]{:S(2)}) collective-permute-start(f32[8,32,128]{2,1,0:T(8,128)} %get-tuple-element.48), channel_id=1, source_target_pairs={{0,8},{8,16},{16,24},{24,0},{1,9},{9,17},{17,25},{25,1},{2,10},{10... | collective-permute-start | bytes 393224 | tf_op jit(solution)/shard_map/ppermute | solution.py:20
  36.1 4.8 %collective-permute-start.6 = (f32[8,32,128]{2,1,0:T(8,128)S(1)}, f32[8,32,128]{2,1,0:T(8,128)S(1)}, u32[]{:S(2)}, u32[]{:S(2)}) collective-permute-start(f32[8,32,128]{2,1,0:T(8,128)S(1)} %get-tuple-element.49), channel_id=1, source_target_pairs={{0,24},{8,0},{16,8},{24,16},{1,25},{9,1},{17,9},{25,17},{2,26},{10... | collective-permute-start | bytes 393224 | tf_op jit(solution)/shard_map/ppermute | solution.py:20
  52.2 8.4 %collective-permute-start.12 = (f32[128,512]{1,0:T(8,128)S(1)}, f32[128,512]{1,0:T(8,128)S(1)}, u32[]{:S(2)}, u32[]{:S(2)}) collective-permute-start(f32[128,512]{1,0:T(8,128)S(1)} %get-tuple-element.58), channel_id=1, source_target_pairs={{0,8},{1,9},{2,10},{3,11},{4,12},{5,13},{6,14},{7,15},{8,0},{9,1},... | collective-permute-start | bytes 786440 | tf_op jit(solution)/shard_map/ppermute | solution.py:290
  52.3 7.4 %collective-permute-start.7 = (f32[22,8,128]{2,1,0:T(8,128)S(1)}, f32[22,8,128]{2,1,0:T(8,128)S(1)}, u32[]{:S(2)}, u32[]{:S(2)}) collective-permute-start(f32[22,8,128]{2,1,0:T(8,128)S(1)} %get-tuple-element.50), channel_id=1, source_target_pairs={{0,2},{2,4},{4,6},{6,0},{1,3},{3,5},{5,7},{7,1},{8,10},{10,12},{12... | collective-permute-start | bytes 270344 | tf_op jit(solution)/shard_map/ppermute | solution.py:20
  53.5 6.6 %collective-permute-start.11 = (f32[22,8,128]{2,1,0:T(8,128)S(1)}, f32[22,8,128]{2,1,0:T(8,128)S(1)}, u32[]{:S(2)}, u32[]{:S(2)}) collective-permute-start(f32[22,8,128]{2,1,0:T(8,128)S(1)} %get-tuple-element.51), channel_id=1, source_target_pairs={{0,6},{2,0},{4,2},{6,4},{1,7},{3,1},{5,3},{7,5},{8,14},{10,8},{12,... | collective-permute-start | bytes 270344 | tf_op jit(solution)/shard_map/ppermute | solution.py:20
  62.0 7.5 %collective-permute-start.14 = (f32[128,1024]{1,0:T(8,128)S(1)}, f32[128,1024]{1,0:T(8,128)S(1)}, u32[]{:S(2)}, u32[]{:S(2)}) collective-permute-start(f32[128,1024]{1,0:T(8,128)S(1)} %get-tuple-element.64), channel_id=1, source_target_pairs={{0,8},{1,9},{2,10},{3,11},{4,12},{5,13},{6,14},{7,15},{8,0},{9,1},... | collective-permute-start | bytes 1572872 | tf_op jit(solution)/shard_map/ppermute | solution.py:290
  62.1 5.9 %collective-permute-start.13 = (f32[64,512]{1,0:T(8,128)S(1)}, f32[64,512]{1,0:T(8,128)S(1)}, u32[]{:S(2)}, u32[]{:S(2)}) collective-permute-start(f32[64,512]{1,0:T(8,128)S(1)} %get-tuple-element.77), channel_id=1, source_target_pairs={{0,16},{1,17},{2,18},{3,19},{4,20},{5,21},{6,22},{7,23},{8,24},{9,... | collective-permute-start | bytes 393224 | tf_op jit(solution)/shard_map/ppermute | solution.py:290
  63.3 16.6 %collective-permute-start.17 = (f32[4,40,128]{2,1,0:T(8,128)S(1)}, f32[4,40,128]{2,1,0:T(8,128)S(1)}, u32[]{:S(2)}, u32[]{:S(2)}) collective-permute-start(f32[4,40,128]{2,1,0:T(8,128)S(1)} %get-tuple-element.56), channel_id=1, source_target_pairs={{0,1},{1,0},{2,3},{3,2},{4,5},{5,4},{6,7},{7,6},{8,9},{9,8},{10,11... | collective-permute-start | bytes 245768 | tf_op jit(solution)/shard_map/ppermute | solution.py:20
  68.0 5.9 %collective-permute-start.21 = (f32[32,512]{1,0:T(8,128)S(1)}, f32[32,512]{1,0:T(8,128)S(1)}, u32[]{:S(2)}, u32[]{:S(2)}) collective-permute-start(f32[32,512]{1,0:T(8,128)S(1)} %slice_add_fusion.11), channel_id=1, source_target_pairs={{0,4},{1,5},{2,6},{3,7},{4,0},{5,1},{6,2},{7,3},{8,12},{9,13},{10,... | collective-permute-start | bytes 196616 | tf_op jit(solution)/shard_map/ppermute | solution.py:290
  69.6 7.6 %collective-permute-start.16 = (f32[64,1024]{1,0:T(8,128)S(1)}, f32[64,1024]{1,0:T(8,128)S(1)}, u32[]{:S(2)}, u32[]{:S(2)}) collective-permute-start(f32[64,1024]{1,0:T(8,128)S(1)} %get-tuple-element.73), channel_id=1, source_target_pairs={{0,16},{1,17},{2,18},{3,19},{4,20},{5,21},{6,22},{7,23},{8,24},{9,... | collective-permute-start | bytes 786440 | tf_op jit(solution)/shard_map/ppermute | solution.py:290
  72.6 6.2 %collective-permute-start.15 = (f32[64,1024]{1,0:T(8,128)S(1)}, f32[64,1024]{1,0:T(8,128)S(1)}, u32[]{:S(2)}, u32[]{:S(2)}) collective-permute-start(f32[64,1024]{1,0:T(8,128)S(1)} %get-tuple-element.69), channel_id=1, source_target_pairs={{0,8},{1,9},{2,10},{3,11},{4,12},{5,13},{6,14},{7,15},{8,0},{9,1},... | collective-permute-start | bytes 786440 | tf_op jit(solution)/shard_map/ppermute | solution.py:290
  77.2 11.8 %collective-permute-start.20 = (f32[32,1024]{1,0:T(8,128)S(1)}, f32[32,1024]{1,0:T(8,128)S(1)}, u32[]{:S(2)}, u32[]{:S(2)}) collective-permute-start(f32[32,1024]{1,0:T(8,128)S(1)} %slice_add_fusion.4), channel_id=1, source_target_pairs={{0,4},{1,5},{2,6},{3,7},{4,0},{5,1},{6,2},{7,3},{8,12},{9,13},{10,... | collective-permute-start | bytes 393224 | tf_op jit(solution)/shard_map/ppermute | solution.py:290
  78.8 9.2 %collective-permute-start.18 = (f32[32,1024]{1,0:T(8,128)S(1)}, f32[32,1024]{1,0:T(8,128)S(1)}, u32[]{:S(2)}, u32[]{:S(2)}) collective-permute-start(f32[32,1024]{1,0:T(8,128)S(1)} %get-tuple-element.75), channel_id=1, source_target_pairs={{0,16},{1,17},{2,18},{3,19},{4,20},{5,21},{6,22},{7,23},{8,24},{9,... | collective-permute-start | bytes 393224 | tf_op jit(solution)/shard_map/ppermute | solution.py:290
  88.0 5.7 %collective-permute-start.19 = (f32[16,1024]{1,0:T(8,128)S(1)}, f32[16,1024]{1,0:T(8,128)S(1)}, u32[]{:S(2)}, u32[]{:S(2)}) collective-permute-start(f32[16,1024]{1,0:T(8,128)S(1)} %slice_add_fusion.9), channel_id=1, source_target_pairs={{0,4},{1,5},{2,6},{3,7},{4,0},{5,1},{6,2},{7,3},{8,12},{9,13},{10,... | collective-permute-start | bytes 196616 | tf_op jit(solution)/shard_map/ppermute | solution.py:290
  (3 other events, 61.3 us)
where the time goes:
time: 94.5 us; the launch traced here: 94.3 us
  waiting for transfers between devices  33.9 us (36%)
  Pallas kernels  32.1 us (34%)
  starting transfers between devices  25 us (26%)
  other arithmetic  2.44 us (3%)
    pallas_call x12, Pallas kernels, call(): pl.pallas_call(body, cost_estimate=pl.CostEstimate(flops=flops, transcend...  32.1 us
    ppermute x10, waiting for transfers between devices, ring(): lax.ppermute(array, axis, [(i, (i + distance) % size) for i in range(size)])  18.7 us
    ppermute x12, waiting for transfers between devices, exchange(): return lax.ppermute(array, ('gx', 'gy', 'row'), route)  15.2 us
    ppermute x10, starting transfers between devices, ring(): lax.ppermute(array, axis, [(i, (i + distance) % size) for i in range(size)])  14.3 us
    ppermute x12, starting transfers between devices, exchange(): return lax.ppermute(array, ('gx', 'gy', 'row'), route)  10.7 us
    add x3, other arithmetic, rest_halved(): return staying + exchange(leaving, mesh_sizes, stages[-1])  1.97 us
  transfers between devices with their start and end apart: 22, of which 14 were waited for; matrix products, arithmetic and copies ran while one was open for 2% of the time, Pallas kernels for 14%

commit v1 on v0

--- a/solution.py
+++ b/solution.py
@@ -92,7 +92,7 @@
         strips_ref[tile] = value
 
 
-def load_wide(whole, earlier, later, kind, target, places):
+def load_sides(whole, earlier, later, kind, target, places, first):
     rows, width = whole.shape[2:]
     lanes = lax.broadcasted_iota(jnp.int32, (rows, width), 1)
     for plane in range(whole.shape[1]):
@@ -102,37 +102,52 @@
         back = (2 * width - shift - HALO) % width
         beside = later[tile] if later is earlier else jnp.where(
             (lanes >= shift + HALO) & (lanes < shift + 2 * HALO), later[tile], earlier[tile])
-        target[plane, 8:8 + rows, :width] = whole[kind, plane]
-        target[plane, 8:8 + rows, width:] = pltpu.roll(beside, back, axis=1)
-
-
-def one_step(source, target, diffusivity, forcing, planes, rows):
-    first, last = rows
+        target[plane, first:first + rows, :] = pltpu.roll(beside, back, axis=1)
+
+
+def one_step(source, target, fixed, planes, rows, sides):
+    def some_rows(plane, first):
+        held, here = (slice(8 + first, 16 + first), slice(first, first + 8))
+        around, centers = ([], [])
+        for pair in source:
+            summed, center = ([], [])
+            for field in pair:
+                middle = field[plane, held, :]
+                total = -6.0 * middle + field[plane + 1, held, :] + field[plane - 1, held, :]
+                summed.append(total + field[plane, 9 + first:17 + first, :] + field[plane, 7 + first:15 + first, :])
+                center.append(middle)
+            width = center[0].shape[1]
+            lanes = lax.broadcasted_iota(jnp.int32, center[0].shape, 1)
+            up = [pltpu.roll(value, 1, axis=1) for value in center]
+            down = [pltpu.roll(value, width - 1, axis=1) for value in center]
+            around.append([summed[n] + jnp.where(lanes == 0, up[1 - n], up[n])
+                           + jnp.where(lanes == width - 1, down[1 - n], down[n]) for n in range(2)])
+            centers.append(center)
+        for n in range(2 if sides else 1):
+            still = [pair[n][plane, here, :] for pair in fixed] + [None]
+            new = react(centers[0][n], centers[1][n], still[0], around[0][n], around[1][n], still[1])
+            for pair, value in zip(target, new):
+                pair[n][plane, held, :] = value
 
     def one_plane(plane, carry):
-        laps = []
-        for field in source:
-            center = field[plane, first:last, :]
-            width = center.shape[1]
-            summed = -6.0 * center + field[plane + 1, first:last, :] + field[plane - 1, first:last, :]
-            summed = summed + field[plane, first + 1:last + 1, :] + field[plane, first - 1:last - 1, :]
-            laps.append(summed + pltpu.roll(center, 1, axis=1) + pltpu.roll(center, width - 1, axis=1))
-        extra = None if forcing is None else forcing[plane, first:last, :]
-        new = react(source[0][plane, first:last, :], source[1][plane, first:last, :],
-                    diffusivity[plane, first:last, :], *laps, extra)
-        for field, value in zip(target, new):
-            field[plane, first:last, :] = value
+        for first in range(0, rows, 8):
+            some_rows(plane, first)
         return carry
 
-    lax.fori_loop(planes[0], planes[1], one_plane, 0)
-
-
-def run_steps(now, then, diffusivity, forcing, rows):
-    planes = now[0].shape[0]
+    lax.fori_loop(planes[0], planes[1], one_plane, 0, unroll=True)
+
+
+def run_steps(whole, earlier, later, fixed, now, then):
+    places, _ = strips_of(whole.shape[1], whole.shape[3])
+    planes, rows = whole.shape[1:3]
+    for kind, pair in enumerate(now):
+        load_sides(whole, earlier, later, kind, pair[1], places, 8)
+        for plane in range(planes):
+            pair[0][plane, 8:8 + rows, :] = whole[kind, plane]
     for step in range(HALO):
-        one_step(now, then, diffusivity, forcing, (step + 1, planes - step - 1), (8, 8 + rows))
+        one_step(now, then, fixed, (step + 1, planes - step - 1), rows, step < HALO - 1)
         now, then = then, now
-    return now
+    return now[0][0], now[1][0]
 
 
 def move_order(patches_z, edge):
@@ -178,25 +193,30 @@
     return product(high, right) + product(low, right)
 
 
-def first_steps_body(edge, whole, earlier, later, state_ref, own_ref, wide_ref, u0, v0, u1, v1, wide, column_ref, semaphores):
+def paired(refs):
+    pairs = list(zip(refs[::2], refs[1::2]))
+    return pairs[:2], pairs[2:]
+
+
+def first_steps_body(edge, whole, earlier, later, state_ref, own_ref, fixed_ref, *scratch):
+    *fields_now, side, column_ref, semaphores = scratch
     length, height, width = state_ref.shape[1:]
-    places, _ = strips_of(whole.shape[1], width)
-    for kind, target in enumerate((u0, v0, wide)):
-        load_wide(whole, earlier, later, kind, target, places)
-    (copy,) = start_copies([(wide, wide_ref)], semaphores)
-    now = run_steps((u0, v0), (u1, v1), wide, None, whole.shape[2])
+    load_sides(whole, earlier, later, 2, side, strips_of(whole.shape[1], width)[0], 0)
+    copies = start_copies([(whole.at[2], fixed_ref.at[0]), (side, fixed_ref.at[1])], semaphores)
+    now = run_steps(whole, earlier, later, [(whole.at[2], side)], *paired(fields_now))
     move, order = (move_order(width // edge, edge), cell_order(edge))
     count = own_ref.shape[0] // 2
     for species, field in enumerate(now):
         for x in range(length):
-            state_ref[species, x] = field[x + HALO, 8 + EDGE:8 + EDGE + height, :width]
+            state_ref[species, x] = field[x + HALO, 8 + EDGE:8 + EDGE + height, :]
         for number, (x, y) in enumerate(cube_starts((length, height), edge)):
             column_ref[number * edge:(number + 1) * edge, :] = state_ref[species, x, y:y + edge, :]
         turned = product_transposed(move, column_ref[...].astype(jnp.bfloat16))
         columns = length * height // (edge * edge)
         cubes = half_tiles(turned, (edge, columns), width // edge, 2 * edge * edge)
         own_ref[species * count:(species + 1) * count, :] = product(cubes.astype(jnp.bfloat16), order).astype(jnp.bfloat16)
-    copy.wait()
+    for copy in copies:
+        copy.wait()
 
 
 def own_forward_body(edge, own_ref, first_ref, middle_ref, last_ref, field_ref):
@@ -216,15 +236,15 @@
         field_ref[x, y:y + edge, :] = moved[number * edge:(number + 1) * edge, :]
 
 
-def last_steps_body(whole, earlier, later, wide, state_ref, u0, v0, u1, v1, force):
+def last_steps_body(whole, earlier, later, fixed, state_ref, *scratch):
+    *fields_now, side = scratch
     length, height, width = state_ref.shape[1:]
-    places, _ = strips_of(whole.shape[1], width)
-    for kind, target in enumerate((u0, v0, force)):
-        load_wide(whole, earlier, later, kind, target, places)
-    now = run_steps((u0, v0), (u1, v1), wide, force, whole.shape[2])
+    load_sides(whole, earlier, later, 2, side, strips_of(whole.shape[1], width)[0], 0)
+    both = [(fixed.at[0], fixed.at[1]), (whole.at[2], side)]
+    now = run_steps(whole, earlier, later, both, *paired(fields_now))
     for species, field in enumerate(now):
         for x in range(length):
-            state_ref[species, x] = field[x + HALO, 8 + EDGE:8 + EDGE + height, :width]
+            state_ref[species, x] = field[x + HALO, 8 + EDGE:8 + EDGE + height, :]
 
 
 def start_copies(pairs, semaphores):
@@ -442,7 +462,8 @@
     length, height, width = diffusivity.shape
     f32, bf16 = (jnp.float32, jnp.bfloat16)
     planes, rows = (length + 2 * HALO, height + 2 * EDGE)
-    wide = ((planes, 8 + rows + 8, 2 * width), f32)
+    fixed = ((2, planes, rows, width), f32)
+    buffers = [((planes, 8 + rows + 8, width), f32)] * 8 + [((planes, rows, width), f32)]
     count = length * height * width // PATCH ** 3
     cells, hidden = weight_first.shape
     hidden_second = weight_middle.shape[1]
@@ -462,11 +483,11 @@
     leading, trailing = edge_rows(near_state, near_third, before, after)
     below, above = y_halos(leading, trailing)
     whole, strips = assemble(near_state, near_third, before, after, below, above)
-    state, own, wide_diffusivity = kernel_call(
+    state, own, diffusivity_fixed = kernel_call(
         functools.partial(first_steps_body, PATCH),
-        [(concentrations.shape, f32), ((2 * count, cells), bf16), wide],
-        scratch=[wide] * 5 + [((length * height, width), f32)],
-        far_outputs=(2,), copies=1,
+        [(concentrations.shape, f32), ((2 * count, cells), bf16), fixed],
+        scratch=buffers + [((length * height, width), f32)],
+        far_outputs=(2,), copies=2,
     )(whole, *z_strips(strips))
 
     others = [exchange(own, mesh_sizes, flips) for flips in ((0, 0, 1), (0, 1, 0), (0, 1, 1))]
@@ -501,8 +522,8 @@
     )(tied(back_second, last[0], middle[0]), weights[1], s1, x, rows_first)
     first = halved(*first, stages[0], mesh_sizes)
     middle = halved(*middle, stages[1], mesh_sizes)
-    (state,) = kernel_call(last_steps_body, [(state.shape, f32)], scratch=[wide] * 5, flops=big)(
-        tied(whole, first[0], middle[0], last[0]), *z_strips(strips), wide_diffusivity
+    (state,) = kernel_call(last_steps_body, [(state.shape, f32)], scratch=buffers, flops=big)(
+        tied(whole, first[0], middle[0], last[0]), *z_strips(strips), diffusivity_fixed
     )
     grads = [rest_halved(*part, stages, done, mesh_sizes) for part, done in ((first, 1), (middle, 2), (last, 2))]
     return (state, *grads)

time: 94.5 us -> 86.5 us (0.915)
  Pallas kernels: 32.1 us -> 23.7 us
    pallas_call x12, Pallas kernels: 32.1 us -> 23.7 us  [call(): pl.pallas_call(body, cost_estimate=pl.CostEstimate(flops=flops, transcend...]
  transfers between devices with their start and end apart: 22 -> 22, of which waited for: 14 -> 15; matrix products, arithmetic and copies ran while one was open for 2% -> 2% of each run, Pallas kernels for 14% -> 10%
where the time goes in v1:
time: 86.5 us; the launch traced here: 86.3 us
  waiting for transfers between devices  33.8 us (39%)
  starting transfers between devices  25.5 us (29%)
  Pallas kernels  23.7 us (27%)
  other arithmetic  2.44 us (3%)
    pallas_call x12, Pallas kernels, call(): pl.pallas_call(body, cost_estimate=pl.CostEstimate(flops=flops, transcend...  23.7 us
    ppermute x10, waiting for transfers between devices, ring(): lax.ppermute(array, axis, [(i, (i + distance) % size) for i in range(size)])  18.7 us
    ppermute x12, waiting for transfers between devices, exchange(): return lax.ppermute(array, ('gx', 'gy', 'row'), route)  15.1 us
    ppermute x10, starting transfers between devices, ring(): lax.ppermute(array, axis, [(i, (i + distance) % size) for i in range(size)])  14.3 us
    ppermute x12, starting transfers between devices, exchange(): return lax.ppermute(array, ('gx', 'gy', 'row'), route)  11.2 us
    add x3, other arithmetic, rest_halved(): return staying + exchange(leaving, mesh_sizes, stages[-1])  1.97 us
  transfers between devices with their start and end apart: 22, of which 15 were waited for; matrix products, arithmetic and copies ran while one was open for 2% of the time, Pallas kernels for 10%

profile of v1, /device:TPU:0, one launch (start us, length us, event | category | flops | bytes accessed | tf_op | source)
XLA Modules:
  0.0 86.3 jit_solution(5907205407817061711)
XLA Ops:
  2.4 2.0 %collective-permute-start.1 = (f32[8,32,128]{2,1,0:T(8,128)S(1)}, f32[8,32,128]{2,1,0:T(8,128)S(1)}, u32[]{:S(2)}, u32[]{:S(2)}) collective-permute-start(f32[8,32,128]{2,1,0:T(8,128)S(1)} %get-tuple-element.41), channel_id=1, source_target_pairs={{0,24},{8,0},{16,8},{24,16},{1,25},{9,1},{17,9},{25,17},{2,26},{10... | collective-permute-start | bytes 393224 | tf_op jit(solution)/shard_map/ppermute | solution.py:20
  4.4 2.6 %collective-permute-done.before = f32[8,32,128]{2,1,0:T(8,128)S(1)} collective-permute-done((f32[8,32,128]{2,1,0:T(8,128)S(1)}, f32[8,32,128]{2,1,0:T(8,128)S(1)}, u32[]{:S(2)}, u32[]{:S(2)}) %collective-permute-start) | collective-permute-done | bytes 131104 | tf_op jit(solution)/shard_map/ppermute | solution.py:20
  8.3 1.6 %collective-permute-start.2 = (f32[22,8,128]{2,1,0:T(8,128)S(1)}, f32[22,8,128]{2,1,0:T(8,128)S(1)}, u32[]{:S(2)}, u32[]{:S(2)}) collective-permute-start(f32[22,8,128]{2,1,0:T(8,128)S(1)} %get-tuple-element.42), channel_id=1, source_target_pairs={{0,2},{2,4},{4,6},{6,0},{1,3},{3,5},{5,7},{7,1},{8,10},{10,12},{12... | collective-permute-start | bytes 270344 | tf_op jit(solution)/shard_map/ppermute | solution.py:20
  9.9 2.2 %collective-permute-start.3 = (f32[22,8,128]{2,1,0:T(8,128)S(1)}, f32[22,8,128]{2,1,0:T(8,128)S(1)}, u32[]{:S(2)}, u32[]{:S(2)}) collective-permute-start(f32[22,8,128]{2,1,0:T(8,128)S(1)} %get-tuple-element.43), channel_id=1, source_target_pairs={{0,6},{2,0},{4,2},{6,4},{1,7},{3,1},{5,3},{7,5},{8,14},{10,8},{12,... | collective-permute-start | bytes 270344 | tf_op jit(solution)/shard_map/ppermute | solution.py:20
  12.2 3.3 %collective-permute-done.2.below = f32[22,8,128]{2,1,0:T(8,128)S(1)} collective-permute-done((f32[22,8,128]{2,1,0:T(8,128)S(1)}, f32[22,8,128]{2,1,0:T(8,128)S(1)}, u32[]{:S(2)}, u32[]{:S(2)}) %collective-permute-start.2) | collective-permute-done | bytes 90144 | tf_op jit(solution)/shard_map/ppermute | solution.py:20
  15.4 1.8 %collective-permute-done.3.above = f32[22,8,128]{2,1,0:T(8,128)S(1)} collective-permute-done((f32[22,8,128]{2,1,0:T(8,128)S(1)}, f32[22,8,128]{2,1,0:T(8,128)S(1)}, u32[]{:S(2)}, u32[]{:S(2)}) %collective-permute-start.3) | collective-permute-done | bytes 90144 | tf_op jit(solution)/shard_map/ppermute | solution.py:20
  17.7 1.6 %collective-permute-start.4 = (f32[4,40,128]{2,1,0:T(8,128)S(1)}, f32[4,40,128]{2,1,0:T(8,128)S(1)}, u32[]{:S(2)}, u32[]{:S(2)}) collective-permute-start(f32[4,40,128]{2,1,0:T(8,128)S(1)} %get-tuple-element.45), channel_id=1, source_target_pairs={{0,1},{1,0},{2,3},{3,2},{4,5},{5,4},{6,7},{7,6},{8,9},{9,8},{10,11... | collective-permute-start | bytes 245768 | tf_op jit(solution)/shard_map/ppermute | solution.py:20
  19.3 2.9 %collective-permute-done.4.earlier.later = f32[4,40,128]{2,1,0:T(8,128)S(1)} collective-permute-done((f32[4,40,128]{2,1,0:T(8,128)S(1)}, f32[4,40,128]{2,1,0:T(8,128)S(1)}, u32[]{:S(2)}, u32[]{:S(2)}) %collective-permute-start.4) | collective-permute-done | bytes 81952 | tf_op jit(solution)/shard_map/ppermute | solution.py:20
  22.2 4.0 %shard_map.87 = (f32[2,16,32,128]{3,2,1,0:T(8,128)S(1)}, bf16[256,512]{1,0:T(8,128)(2,1)S(1)}, f32[2,22,40,128]{3,2,1,0:T(8,128)}) custom-call(f32[3,22,40,128]{3,2,1,0:T(8,128)S(1)} %get-tuple-element.44.whole, f32[4,40,128]{2,1,0:T(8,128)S(1)} %collective-permute-done.4.earlier.later, f32[4,40,128]{2,1,0:T(8,128)S(1)} %collective-permute-done.4.earlier.later), custom_call_target="tpu_custom_call" | custom-call | flops 16777216 | tf_op jit(solution)/shard_map/pallas_call | solution.py:443
  26.2 1.9 %collective-permute-start.10 = (bf16[256,512]{1,0:T(8,128)(2,1)S(1)}, bf16[256,512]{1,0:T(8,128)(2,1)}, u32[]{:S(2)}, u32[]{:S(2)}) collective-permute-start(bf16[256,512]{1,0:T(8,128)(2,1)S(1)} %get-tuple-element.52.own_ref), channel_id=1, source_target_pairs={{0,3},{1,2},{2,1},{3,0},{4,7},{5,6},{6,5},{7,4},{8,11},{9,10},{10,... | collective-permute-start | bytes 786440 | tf_op jit(solution)/shard_map/ppermute | solution.py:310
  29.8 1.5 %shard_map.88.third = f32[16,32,128]{2,1,0:T(8,128)S(1)} custom-call(bf16[256,512]{1,0:T(8,128)(2,1)S(1)} %get-tuple-element.52.own_ref, bf16[512,1024]{1,0:T(8,128)(2,1)S(1)} %copy-done.1, bf16[1024,1024]{1,0:T(8,128)(2,1)S(1)} %copy-done, bf16[1024,512]{1,0:T(8,128)(2,1)S(1)} %copy-done.2), custom_call_target="tpu_custom_call" | custom-call | flops 1073741824 | tf_op jit(solution)/shard_map/pallas_call | solution.py:443
  32.0 1.7 %collective-permute-start.6 = (f32[8,32,128]{2,1,0:T(8,128)S(1)}, f32[8,32,128]{2,1,0:T(8,128)S(1)}, u32[]{:S(2)}, u32[]{:S(2)}) collective-permute-start(f32[8,32,128]{2,1,0:T(8,128)S(1)} %get-tuple-element.49), channel_id=1, source_target_pairs={{0,24},{8,0},{16,8},{24,16},{1,25},{9,1},{17,9},{25,17},{2,26},{10... | collective-permute-start | bytes 393224 | tf_op jit(solution)/shard_map/ppermute | solution.py:20
  34.0 2.9 %collective-permute-done.5.before = f32[8,32,128]{2,1,0:T(8,128)S(1)} collective-permute-done((f32[8,32,128]{2,1,0:T(8,128)}, f32[8,32,128]{2,1,0:T(8,128)S(1)}, u32[]{:S(2)}, u32[]{:S(2)}) %collective-permute-start.5) | collective-permute-done | bytes 131104 | tf_op jit(solution)/shard_map/ppermute | solution.py:20
  36.9 3.1 %collective-permute-done.8.a_ref = bf16[256,512]{1,0:T(8,128)(2,1)} collective-permute-done((bf16[256,512]{1,0:T(8,128)(2,1)S(1)}, bf16[256,512]{1,0:T(8,128)(2,1)}, u32[]{:S(2)}, u32[]{:S(2)}) %collective-permute-start.8) | collective-permute-done | bytes 262176 | tf_op jit(solution)/shard_map/ppermute | solution.py:310
  40.1 7.9 %shard_map.91 = (bf16[512,512]{1,0:T(8,128)(2,1)S(1)}, bf16[512,1024]{1,0:T(8,128)(2,1)S(1)}, f32[512,1024]{1,0:T(8,128)S(1)}, bf16[512,1024]{1,0:T(8,128)(2,1)}...) custom-call(bf16[256,512]{1,0:T(8,128)(2,1)S(1)} %get-tuple-element.5, ...), custom_call_target="tpu_custom_call" | custom-call | flops 4294967296 | tf_op jit(solution)/shard_map/pallas_call | solution.py:443
  49.4 2.6 %collective-permute-start.11 = (f32[22,8,128]{2,1,0:T(8,128)S(1)}, f32[22,8,128]{2,1,0:T(8,128)S(1)}, u32[]{:S(2)}, u32[]{:S(2)}) collective-permute-start(f32[22,8,128]{2,1,0:T(8,128)S(1)} %get-tuple-element.51), channel_id=1, source_target_pairs={{0,6},{2,0},{4,2},{6,4},{1,7},{3,1},{5,3},{7,5},{8,14},{10,8},{12,... | collective-permute-start | bytes 270344 | tf_op jit(solution)/shard_map/ppermute | solution.py:20
  52.0 3.5 %collective-permute-done.7.below = f32[22,8,128]{2,1,0:T(8,128)S(1)} collective-permute-done((f32[22,8,128]{2,1,0:T(8,128)S(1)}, f32[22,8,128]{2,1,0:T(8,128)S(1)}, u32[]{:S(2)}, u32[]{:S(2)}) %collective-permute-start.7) | collective-permute-done | bytes 90144 | tf_op jit(solution)/shard_map/ppermute | solution.py:20
  59.9 4.0 %collective-permute-done.13 = f32[64,512]{1,0:T(8,128)S(1)} collective-permute-done((f32[64,512]{1,0:T(8,128)S(1)}, f32[64,512]{1,0:T(8,128)S(1)}, u32[]{:S(2)}, u32[]{:S(2)}) %collective-permute-start.13) | collective-permute-done | bytes 131104 | tf_op jit(solution)/shard_map/ppermute | solution.py:310
  63.9 1.5 %collective-permute-start.21 = (f32[32,512]{1,0:T(8,128)S(1)}, f32[32,512]{1,0:T(8,128)S(1)}, u32[]{:S(2)}, u32[]{:S(2)}) collective-permute-start(f32[32,512]{1,0:T(8,128)S(1)} %slice_add_fusion.11), channel_id=1, source_target_pairs={{0,4},{1,5},{2,6},{3,7},{4,0},{5,1},{6,2},{7,3},{8,12},{9,13},{10,... | collective-permute-start | bytes 196616 | tf_op jit(solution)/shard_map/ppermute | solution.py:310
  66.2 2.3 %shard_map.94 = (bf16[512,1024]{1,0:T(8,128)(2,1)}, f32[64,1024]{1,0:T(8,128)S(1)}, f32[64,1024]{1,0:T(8,128)S(1)}) custom-call(bf16[512,1024]{1,0:T(8,128)(2,1)S(1)} %get-tuple-element.65.carried_ref, bf16[1024,1024]{1,0:T(8,128)(2,1)S(1)} %copy-done, f32[512,1024]{1,0:T(8,128)S(1)} %get-tuple-element.66.slope_ref, ...), custom_call_target="tpu_custom_call" | custom-call | flops 2147483648 | tf_op jit(solution)/shard_map/pallas_call | solution.py:443
  70.5 2.6 %collective-permute-done.16 = f32[64,1024]{1,0:T(8,128)S(1)} collective-permute-done((f32[64,1024]{1,0:T(8,128)S(1)}, f32[64,1024]{1,0:T(8,128)S(1)}, u32[]{:S(2)}, u32[]{:S(2)}) %collective-permute-start.16) | collective-permute-done | bytes 262176 | tf_op jit(solution)/shard_map/ppermute | solution.py:310
  73.1 1.5 %collective-permute-start.20 = (f32[32,1024]{1,0:T(8,128)S(1)}, f32[32,1024]{1,0:T(8,128)S(1)}, u32[]{:S(2)}, u32[]{:S(2)}) collective-permute-start(f32[32,1024]{1,0:T(8,128)S(1)} %slice_add_fusion.4), channel_id=1, source_target_pairs={{0,4},{1,5},{2,6},{3,7},{4,0},{5,1},{6,2},{7,3},{8,12},{9,13},{10,... | collective-permute-start | bytes 393224 | tf_op jit(solution)/shard_map/ppermute | solution.py:310
  75.8 3.7 %shard_map.95 = f32[2,16,32,128]{3,2,1,0:T(8,128)} custom-call(f32[3,22,40,128]{3,2,1,0:T(8,128)S(1)} %get-tuple-element.70.whole, f32[4,40,128]{2,1,0:T(8,128)S(1)} %collective-permute-done.17.earlier.later, f32[4,40,128]{2,1,0:T(8,128)S(1)} %collective-permute-done.17.earlier.later, f32[2,22,40,128]{3,2,1,0:T(8,128)S(1)} %copy-done.4), custom_call_target="tpu_custom_call" | custom-call | flops 4294967296 | tf_op jit(solution)/shard_map/pallas_call | solution.py:443
  81.9 3.7 %collective-permute-done.19 = f32[16,1024]{1,0:T(8,128)S(1)} collective-permute-done((f32[16,1024]{1,0:T(8,128)S(1)}, f32[16,1024]{1,0:T(8,128)S(1)}, u32[]{:S(2)}, u32[]{:S(2)}) %collective-permute-start.19) | collective-permute-done | bytes 65568 | tf_op jit(solution)/shard_map/ppermute | solution.py:310
  (53 shorter events, 18.8 us)
Async XLA Ops:
  0.6 29.2 %copy-start.2 = (bf16[1024,512]{1,0:T(8,128)(2,1)S(1)}, bf16[1024,512]{1,0:T(8,128)(2,1)}, u32[]{:S(2)}) copy-start(bf16[1024,512]{1,0:T(8,128)(2,1)} %weight_ref.2) | copy-start | bytes 3145732
  1.9 27.9 %copy-start = (bf16[1024,1024]{1,0:T(8,128)(2,1)S(1)}, bf16[1024,1024]{1,0:T(8,128)(2,1)}, u32[]{:S(2)}) copy-start(bf16[1024,1024]{1,0:T(8,128)(2,1)} %weight_ref.3) | copy-start | bytes 6291460
  1.9 5.1 %collective-permute-start = (f32[8,32,128]{2,1,0:T(8,128)S(1)}, f32[8,32,128]{2,1,0:T(8,128)S(1)}, u32[]{:S(2)}, u32[]{:S(2)}) collective-permute-start(f32[8,32,128]{2,1,0:T(8,128)S(1)} %get-tuple-element.40), channel_id=1, source_target_pairs={{0,8},{8,16},{16,24},{24,0},{1,9},{9,17},{17,25},{25,1},{2,10},{10... | collective-permute-start | bytes 393224 | tf_op jit(solution)/shard_map/ppermute | solution.py:20
  2.4 5.8 %collective-permute-start.1 = (f32[8,32,128]{2,1,0:T(8,128)S(1)}, f32[8,32,128]{2,1,0:T(8,128)S(1)}, u32[]{:S(2)}, u32[]{:S(2)}) collective-permute-start(f32[8,32,128]{2,1,0:T(8,128)S(1)} %get-tuple-element.41), channel_id=1, source_target_pairs={{0,24},{8,0},{16,8},{24,16},{1,25},{9,1},{17,9},{25,17},{2,26},{10... | collective-permute-start | bytes 393224 | tf_op jit(solution)/shard_map/ppermute | solution.py:20
  8.3 7.2 %collective-permute-start.2 = (f32[22,8,128]{2,1,0:T(8,128)S(1)}, f32[22,8,128]{2,1,0:T(8,128)S(1)}, u32[]{:S(2)}, u32[]{:S(2)}) collective-permute-start(f32[22,8,128]{2,1,0:T(8,128)S(1)} %get-tuple-element.42), channel_id=1, source_target_pairs={{0,2},{2,4},{4,6},{6,0},{1,3},{3,5},{5,7},{7,1},{8,10},{10,12},{12... | collective-permute-start | bytes 270344 | tf_op jit(solution)/shard_map/ppermute | solution.py:20
  9.9 7.4 %collective-permute-start.3 = (f32[22,8,128]{2,1,0:T(8,128)S(1)}, f32[22,8,128]{2,1,0:T(8,128)S(1)}, u32[]{:S(2)}, u32[]{:S(2)}) collective-permute-start(f32[22,8,128]{2,1,0:T(8,128)S(1)} %get-tuple-element.43), channel_id=1, source_target_pairs={{0,6},{2,0},{4,2},{6,4},{1,7},{3,1},{5,3},{7,5},{8,14},{10,8},{12,... | collective-permute-start | bytes 270344 | tf_op jit(solution)/shard_map/ppermute | solution.py:20
  17.7 4.5 %collective-permute-start.4 = (f32[4,40,128]{2,1,0:T(8,128)S(1)}, f32[4,40,128]{2,1,0:T(8,128)S(1)}, u32[]{:S(2)}, u32[]{:S(2)}) collective-permute-start(f32[4,40,128]{2,1,0:T(8,128)S(1)} %get-tuple-element.45), channel_id=1, source_target_pairs={{0,1},{1,0},{2,3},{3,2},{4,5},{5,4},{6,7},{7,6},{8,9},{9,8},{10,11... | collective-permute-start | bytes 245768 | tf_op jit(solution)/shard_map/ppermute | solution.py:20
  26.2 10.7 %collective-permute-start.10 = (bf16[256,512]{1,0:T(8,128)(2,1)S(1)}, bf16[256,512]{1,0:T(8,128)(2,1)}, u32[]{:S(2)}, u32[]{:S(2)}) collective-permute-start(bf16[256,512]{1,0:T(8,128)(2,1)S(1)} %get-tuple-element.52.own_ref), channel_id=1, source_target_pairs={{0,3},{1,2},{2,1},{3,0},{4,7},{5,6},{6,5},{7,4},{8,11},{9,10},{10,... | collective-permute-start | bytes 786440 | tf_op jit(solution)/shard_map/ppermute | solution.py:310
  28.1 11.9 %collective-permute-start.8 = (bf16[256,512]{1,0:T(8,128)(2,1)S(1)}, bf16[256,512]{1,0:T(8,128)(2,1)}, u32[]{:S(2)}, u32[]{:S(2)}) collective-permute-start(bf16[256,512]{1,0:T(8,128)(2,1)S(1)} %get-tuple-element.52.own_ref), channel_id=1, source_target_pairs={{0,1},{1,0},{2,3},{3,2},{4,5},{5,4},{6,7},{7,6},{8,9},{9,8},{10,11... | collective-permute-start | bytes 786440 | tf_op jit(solution)/shard_map/ppermute | solution.py:310
  28.6 11.5 %collective-permute-start.9 = (bf16[256,512]{1,0:T(8,128)(2,1)S(1)}, bf16[256,512]{1,0:T(8,128)(2,1)}, u32[]{:S(2)}, u32[]{:S(2)}) collective-permute-start(bf16[256,512]{1,0:T(8,128)(2,1)S(1)} %get-tuple-element.52.own_ref), channel_id=1, source_target_pairs={{0,2},{1,3},{2,0},{3,1},{4,6},{5,7},{6,4},{7,5},{8,10},{9,11},{10,... | collective-permute-start | bytes 786440 | tf_op jit(solution)/shard_map/ppermute | solution.py:310
  32.0 4.8 %collective-permute-start.5 = (f32[8,32,128]{2,1,0:T(8,128)}, f32[8,32,128]{2,1,0:T(8,128)S(1)}, u32[]{:S(2)}, u32[]{:S(2)}) collective-permute-start(f32[8,32,128]{2,1,0:T(8,128)} %get-tuple-element.48), channel_id=1, source_target_pairs={{0,8},{8,16},{16,24},{24,0},{1,9},{9,17},{17,25},{25,1},{2,10},{10... | collective-permute-start | bytes 393224 | tf_op jit(solution)/shard_map/ppermute | solution.py:20
  32.0 4.8 %collective-permute-start.6 = (f32[8,32,128]{2,1,0:T(8,128)S(1)}, f32[8,32,128]{2,1,0:T(8,128)S(1)}, u32[]{:S(2)}, u32[]{:S(2)}) collective-permute-start(f32[8,32,128]{2,1,0:T(8,128)S(1)} %get-tuple-element.49), channel_id=1, source_target_pairs={{0,24},{8,0},{16,8},{24,16},{1,25},{9,1},{17,9},{25,17},{2,26},{10... | collective-permute-start | bytes 393224 | tf_op jit(solution)/shard_map/ppermute | solution.py:20
  48.1 8.4 %collective-permute-start.12 = (f32[128,512]{1,0:T(8,128)S(1)}, f32[128,512]{1,0:T(8,128)S(1)}, u32[]{:S(2)}, u32[]{:S(2)}) collective-permute-start(f32[128,512]{1,0:T(8,128)S(1)} %get-tuple-element.58), channel_id=1, source_target_pairs={{0,8},{1,9},{2,10},{3,11},{4,12},{5,13},{6,14},{7,15},{8,0},{9,1},... | collective-permute-start | bytes 786440 | tf_op jit(solution)/shard_map/ppermute | solution.py:310
  48.2 7.4 %collective-permute-start.7 = (f32[22,8,128]{2,1,0:T(8,128)S(1)}, f32[22,8,128]{2,1,0:T(8,128)S(1)}, u32[]{:S(2)}, u32[]{:S(2)}) collective-permute-start(f32[22,8,128]{2,1,0:T(8,128)S(1)} %get-tuple-element.50), channel_id=1, source_target_pairs={{0,2},{2,4},{4,6},{6,0},{1,3},{3,5},{5,7},{7,1},{8,10},{10,12},{12... | collective-permute-start | bytes 270344 | tf_op jit(solution)/shard_map/ppermute | solution.py:20
  49.4 6.6 %collective-permute-start.11 = (f32[22,8,128]{2,1,0:T(8,128)S(1)}, f32[22,8,128]{2,1,0:T(8,128)S(1)}, u32[]{:S(2)}, u32[]{:S(2)}) collective-permute-start(f32[22,8,128]{2,1,0:T(8,128)S(1)} %get-tuple-element.51), channel_id=1, source_target_pairs={{0,6},{2,0},{4,2},{6,4},{1,7},{3,1},{5,3},{7,5},{8,14},{10,8},{12,... | collective-permute-start | bytes 270344 | tf_op jit(solution)/shard_map/ppermute | solution.py:20
  57.9 7.5 %collective-permute-start.14 = (f32[128,1024]{1,0:T(8,128)S(1)}, f32[128,1024]{1,0:T(8,128)S(1)}, u32[]{:S(2)}, u32[]{:S(2)}) collective-permute-start(f32[128,1024]{1,0:T(8,128)S(1)} %get-tuple-element.64), channel_id=1, source_target_pairs={{0,8},{1,9},{2,10},{3,11},{4,12},{5,13},{6,14},{7,15},{8,0},{9,1},... | collective-permute-start | bytes 1572872 | tf_op jit(solution)/shard_map/ppermute | solution.py:310
  58.0 5.9 %collective-permute-start.13 = (f32[64,512]{1,0:T(8,128)S(1)}, f32[64,512]{1,0:T(8,128)S(1)}, u32[]{:S(2)}, u32[]{:S(2)}) collective-permute-start(f32[64,512]{1,0:T(8,128)S(1)} %get-tuple-element.77), channel_id=1, source_target_pairs={{0,16},{1,17},{2,18},{3,19},{4,20},{5,21},{6,22},{7,23},{8,24},{9,... | collective-permute-start | bytes 393224 | tf_op jit(solution)/shard_map/ppermute | solution.py:310
  59.2 16.6 %collective-permute-start.17 = (f32[4,40,128]{2,1,0:T(8,128)S(1)}, f32[4,40,128]{2,1,0:T(8,128)S(1)}, u32[]{:S(2)}, u32[]{:S(2)}) collective-permute-start(f32[4,40,128]{2,1,0:T(8,128)S(1)} %get-tuple-element.56), channel_id=1, source_target_pairs={{0,1},{1,0},{2,3},{3,2},{4,5},{5,4},{6,7},{7,6},{8,9},{9,8},{10,11... | collective-permute-start | bytes 245768 | tf_op jit(solution)/shard_map/ppermute | solution.py:20
  63.9 5.9 %collective-permute-start.21 = (f32[32,512]{1,0:T(8,128)S(1)}, f32[32,512]{1,0:T(8,128)S(1)}, u32[]{:S(2)}, u32[]{:S(2)}) collective-permute-start(f32[32,512]{1,0:T(8,128)S(1)} %slice_add_fusion.11), channel_id=1, source_target_pairs={{0,4},{1,5},{2,6},{3,7},{4,0},{5,1},{6,2},{7,3},{8,12},{9,13},{10,... | collective-permute-start | bytes 196616 | tf_op jit(solution)/shard_map/ppermute | solution.py:310
  65.5 7.6 %collective-permute-start.16 = (f32[64,1024]{1,0:T(8,128)S(1)}, f32[64,1024]{1,0:T(8,128)S(1)}, u32[]{:S(2)}, u32[]{:S(2)}) collective-permute-start(f32[64,1024]{1,0:T(8,128)S(1)} %get-tuple-element.73), channel_id=1, source_target_pairs={{0,16},{1,17},{2,18},{3,19},{4,20},{5,21},{6,22},{7,23},{8,24},{9,... | collective-permute-start | bytes 786440 | tf_op jit(solution)/shard_map/ppermute | solution.py:310
  68.5 6.2 %collective-permute-start.15 = (f32[64,1024]{1,0:T(8,128)S(1)}, f32[64,1024]{1,0:T(8,128)S(1)}, u32[]{:S(2)}, u32[]{:S(2)}) collective-permute-start(f32[64,1024]{1,0:T(8,128)S(1)} %get-tuple-element.69), channel_id=1, source_target_pairs={{0,8},{1,9},{2,10},{3,11},{4,12},{5,13},{6,14},{7,15},{8,0},{9,1},... | collective-permute-start | bytes 786440 | tf_op jit(solution)/shard_map/ppermute | solution.py:310
  73.1 8.1 %collective-permute-start.20 = (f32[32,1024]{1,0:T(8,128)S(1)}, f32[32,1024]{1,0:T(8,128)S(1)}, u32[]{:S(2)}, u32[]{:S(2)}) collective-permute-start(f32[32,1024]{1,0:T(8,128)S(1)} %slice_add_fusion.4), channel_id=1, source_target_pairs={{0,4},{1,5},{2,6},{3,7},{4,0},{5,1},{6,2},{7,3},{8,12},{9,13},{10,... | collective-permute-start | bytes 393224 | tf_op jit(solution)/shard_map/ppermute | solution.py:310
  74.7 5.0 %collective-permute-start.18 = (f32[32,1024]{1,0:T(8,128)S(1)}, f32[32,1024]{1,0:T(8,128)S(1)}, u32[]{:S(2)}, u32[]{:S(2)}) collective-permute-start(f32[32,1024]{1,0:T(8,128)S(1)} %get-tuple-element.75), channel_id=1, source_target_pairs={{0,16},{1,17},{2,18},{3,19},{4,20},{5,21},{6,22},{7,23},{8,24},{9,... | collective-permute-start | bytes 393224 | tf_op jit(solution)/shard_map/ppermute | solution.py:310
  79.7 5.9 %collective-permute-start.19 = (f32[16,1024]{1,0:T(8,128)S(1)}, f32[16,1024]{1,0:T(8,128)S(1)}, u32[]{:S(2)}, u32[]{:S(2)}) collective-permute-start(f32[16,1024]{1,0:T(8,128)S(1)} %slice_add_fusion.9), channel_id=1, source_target_pairs={{0,4},{1,5},{2,6},{3,7},{4,0},{5,1},{6,2},{7,3},{8,12},{9,13},{10,... | collective-permute-start | bytes 196616 | tf_op jit(solution)/shard_map/ppermute | solution.py:310
  (3 other events, 57.2 us)

commit v2 on v1

--- a/solution.py
+++ b/solution.py
@@ -198,15 +198,14 @@
     return pairs[:2], pairs[2:]
 
 
-def first_steps_body(edge, whole, earlier, later, state_ref, own_ref, fixed_ref, *scratch):
+def first_steps_body(edge, whole, earlier, later, state_ref, inputs_ref, targets_ref, fixed_ref, *scratch):
     *fields_now, side, column_ref, semaphores = scratch
     length, height, width = state_ref.shape[1:]
     load_sides(whole, earlier, later, 2, side, strips_of(whole.shape[1], width)[0], 0)
     copies = start_copies([(whole.at[2], fixed_ref.at[0]), (side, fixed_ref.at[1])], semaphores)
     now = run_steps(whole, earlier, later, [(whole.at[2], side)], *paired(fields_now))
     move, order = (move_order(width // edge, edge), cell_order(edge))
-    count = own_ref.shape[0] // 2
-    for species, field in enumerate(now):
+    for species, (field, out_ref) in enumerate(zip(now, (inputs_ref, targets_ref))):
         for x in range(length):
             state_ref[species, x] = field[x + HALO, 8 + EDGE:8 + EDGE + height, :]
         for number, (x, y) in enumerate(cube_starts((length, height), edge)):
@@ -214,15 +213,14 @@
         turned = product_transposed(move, column_ref[...].astype(jnp.bfloat16))
         columns = length * height // (edge * edge)
         cubes = half_tiles(turned, (edge, columns), width // edge, 2 * edge * edge)
-        own_ref[species * count:(species + 1) * count, :] = product(cubes.astype(jnp.bfloat16), order).astype(jnp.bfloat16)
+        out_ref[...] = product(cubes.astype(jnp.bfloat16), order).astype(jnp.bfloat16)
     for copy in copies:
         copy.wait()
 
 
-def own_forward_body(edge, own_ref, first_ref, middle_ref, last_ref, field_ref):
+def own_forward_body(edge, inputs_ref, first_ref, middle_ref, last_ref, field_ref):
     length, height, width = field_ref.shape
-    count = own_ref.shape[0] // 2
-    h1 = gelu_value(product(own_ref[:count, :], first_ref[...])).astype(jnp.bfloat16)
+    h1 = gelu_value(product(inputs_ref[...], first_ref[...])).astype(jnp.bfloat16)
     h2 = gelu_value(product(h1, middle_ref[...])).astype(jnp.bfloat16)
     forcing = product(h2, last_ref[...])
     cells = lax.broadcasted_iota(jnp.int32, (edge ** 3, edge ** 3), 1)
@@ -252,6 +250,10 @@
     for copy in copies:
         copy.start()
     return copies
+
+
+def bring_body(far_ref, near_ref, semaphores):
+    start_copies([(far_ref, near_ref)], semaphores)[0].wait()
 
 
 def store_faces(state, third, leading_ref, trailing_ref):
@@ -350,7 +352,8 @@
 def rest_halved(leaving, staying, stages, done, mesh_sizes):
     for number in range(done, len(stages) - 1):
         leaving, staying = halved(leaving, staying, stages[number], mesh_sizes)
-    return staying + exchange(leaving, mesh_sizes, stages[-1])
+    arrived = exchange(leaving, mesh_sizes, stages[-1])
+    return staying + arrived
 
 
 def gelu_pair(values):
@@ -392,31 +395,35 @@
     staying_ref[:, columns] = value[half:]
 
 
-def forward_body(scale, own_ref, a_ref, b_ref, c_ref, first_ref, middle_ref, last_ref, rows_ref,
-                 x_ref, h1_ref, s1_ref, h2_ref, s2_ref, error_ref, leaving_ref, staying_ref, first_near, last_near, semaphores):
-    first_copy, last_copy = start_copies(((first_ref, first_near), (last_ref, last_near)), semaphores)
-    count = own_ref.shape[0] // 2
-    parts = (own_ref, a_ref, b_ref, c_ref)
-    for number, part in enumerate(parts):
-        x_ref[number * count:(number + 1) * count, :] = part[:count, :]
-    x = x_ref[...]
-    first_copy.wait()
-    for columns in column_tiles(h1_ref.shape[1]):
-        value, slope = gelu_pair(product(x, first_near[:, columns]))
-        h1_ref[:, columns] = value.astype(jnp.bfloat16)
-        s1_ref[:, columns] = slope
-    h1 = h1_ref[...]
-    for columns in column_tiles(h2_ref.shape[1]):
-        value, slope = gelu_pair(product(h1, middle_ref[:, columns]))
-        h2_ref[:, columns] = value.astype(jnp.bfloat16)
-        s2_ref[:, columns] = slope
+def activated(left, weight, value_ref, slope_ref):
+    tiles = column_tiles(value_ref.shape[1])
+    ahead = product(left, weight[:, tiles[0]])
+    for number, columns in enumerate(tiles):
+        now = ahead
+        if number + 1 < len(tiles):
+            ahead = product(left, weight[:, tiles[number + 1]])
+        value, slope = gelu_pair(now)
+        value_ref[:, columns] = value.astype(jnp.bfloat16)
+        slope_ref[:, columns] = slope
+
+
+def forward_one_body(own_ref, a_ref, b_ref, c_ref, first_ref, middle_ref,
+                     x_ref, h1_ref, s1_ref, h2_ref, s2_ref):
+    count = own_ref.shape[0]
+    for number, part in enumerate((own_ref, a_ref, b_ref, c_ref)):
+        x_ref[number * count:(number + 1) * count, :] = part[...]
+    activated(x_ref[...], first_ref, h1_ref, s1_ref)
+    activated(h1_ref[...], middle_ref, h2_ref, s2_ref)
+
+
+def forward_two_body(scale, h2_ref, own_ref, a_ref, b_ref, c_ref, last_ref, rows_ref, error_ref, leaving_ref, staying_ref):
+    count = own_ref.shape[0]
     h2 = h2_ref[...]
-    last_copy.wait()
     for columns in column_tiles(error_ref.shape[1]):
-        forcing = product(h2, last_near[:, columns])
-        for number, part in enumerate(parts):
+        forcing = product(h2, last_ref[:, columns])
+        for number, part in enumerate((own_ref, a_ref, b_ref, c_ref)):
             block = slice(number * count, (number + 1) * count)
-            target = part[count:, columns].astype(jnp.float32)
+            target = part[:, columns].astype(jnp.float32)
             error_ref[block, columns] = ((forcing[block] - target) * scale).astype(jnp.bfloat16)
     chosen = transposed_choice(rows_ref[...], h2)
     for columns in column_tiles(error_ref.shape[1]):
@@ -437,7 +444,7 @@
     return lax.optimization_barrier((value, *others))[0]
 
 
-def kernel_call(body, outputs, scratch=(), flops=1 << 24, far=(), far_outputs=(), copies=0):
+def kernel_call(body, outputs, scratch=(), flops=1 << 31, far=(), far_outputs=(), copies=0):
     def call(*inputs):
         near, away = (pl.BlockSpec(memory_space=pltpu.VMEM), pl.BlockSpec(memory_space=pltpu.HBM))
         result = pl.pallas_call(
@@ -474,52 +481,60 @@
     big = 1 << 32
 
     layers = ((3 * HALO - 1, height, width), f32)
-    weights = (weight_first, weight_middle, weight_last)
     leading, trailing, near_state, near_third = kernel_call(
         first_faces_body, [layers, layers, (concentrations.shape, f32), (diffusivity.shape, f32)],
         far=(0, 1), copies=2,
     )(concentrations, diffusivity)
     before, after = x_halos(leading, trailing)
+    (near_last,) = kernel_call(bring_body, [(weight_last.shape, bf16)], far=(0,), copies=1)(weight_last)
     leading, trailing = edge_rows(near_state, near_third, before, after)
     below, above = y_halos(leading, trailing)
     whole, strips = assemble(near_state, near_third, before, after, below, above)
-    state, own, diffusivity_fixed = kernel_call(
+    state, inputs, targets, diffusivity_fixed = kernel_call(
         functools.partial(first_steps_body, PATCH),
-        [(concentrations.shape, f32), ((2 * count, cells), bf16), fixed],
+        [(concentrations.shape, f32), ((count, cells), bf16), ((count, cells), bf16), fixed],
         scratch=buffers + [((length * height, width), f32)],
-        far_outputs=(2,), copies=2,
+        far_outputs=(3,), copies=2,
     )(whole, *z_strips(strips))
 
-    others = [exchange(own, mesh_sizes, flips) for flips in ((0, 0, 1), (0, 1, 0), (0, 1, 1))]
-    (field,) = kernel_call(functools.partial(own_forward_body, PATCH), [(diffusivity.shape, f32)], flops=big // 4)(
-        own, *weights
+    gather = lambda array: [exchange(array, mesh_sizes, flips) for flips in ((0, 0, 1), (0, 1, 0), (0, 1, 1))]
+    all_inputs = gather(inputs)
+    (field,) = kernel_call(functools.partial(own_forward_body, PATCH), [(diffusivity.shape, f32)],
+        flops=big // 4,
+    )(
+        inputs, weight_first, weight_middle, near_last
     )
+    all_targets = gather(tied(targets, field))
     leading, trailing = kernel_call(store_faces, [layers, layers])(state, field)
     before, after = x_halos(leading, trailing)
-    leading, trailing = edge_rows(state, field, before, after)
+    x, h1, s1, h2, s2 = kernel_call(
+        forward_one_body,
+        [((total, cells), bf16), ((total, hidden), bf16), ((total, hidden), f32), ((total, hidden_second), bf16),
+         ((total, hidden_second), f32)],
+        flops=big,
+    )(tied(inputs, leading, trailing), *all_inputs, weight_first, weight_middle)
+    leading, trailing = edge_rows(state, field, tied(before, h2), after)
     below, above = y_halos(leading, trailing)
-    x, h1, s1, h2, s2, error, *last = kernel_call(
-        functools.partial(forward_body, 1.0 / count),
-        [((total, cells), bf16), ((total, hidden), bf16), ((total, hidden), f32), ((total, hidden_second), bf16),
-         ((total, hidden_second), f32), ((total, cells), bf16),
-         half_of(rows_last, cells), half_of(rows_last, cells)],
-        scratch=[(weight_first.shape, bf16), (weight_last.shape, bf16)],
-        flops=big, far=(4, 6), copies=2,
-    )(tied(own, leading, trailing), *others, *weights, rows_last)
+    error, *last = kernel_call(
+        functools.partial(forward_two_body, 1.0 / count),
+        [((total, cells), bf16), half_of(rows_last, cells), half_of(rows_last, cells)],
+        flops=big,
+    )(tied(h2, leading, trailing), targets, *all_targets, weight_last, rows_last)
     last = halved(*last, stages[0], mesh_sizes)
-    whole, strips = assemble(state, field, before, after, tied(below, error), above)
     back_second, *middle = kernel_call(
         backward_body,
         [((total, hidden_second), bf16), half_of(rows_middle, hidden_second), half_of(rows_middle, hidden_second)],
         flops=big // 2,
-    )(tied(error, strips, last[0]), weights[2], s2, h1, rows_middle)
+    )(error, weight_last, s2, h1, rows_middle)
     middle = halved(*middle, stages[0], mesh_sizes)
+    last_leaving = last[0]
+    whole, strips = assemble(state, field, before, after, tied(below, back_second, last_leaving, middle[0]), above)
     last = halved(*last, stages[1], mesh_sizes)
     back_first, *first = kernel_call(
         backward_body,
         [((total, hidden), bf16), half_of(rows_first, hidden), half_of(rows_first, hidden)],
         flops=big // 2,
-    )(tied(back_second, last[0], middle[0]), weights[1], s1, x, rows_first)
+    )(tied(back_second, strips), weight_middle, s1, x, rows_first)
     first = halved(*first, stages[0], mesh_sizes)
     middle = halved(*middle, stages[1], mesh_sizes)
     (state,) = kernel_call(last_steps_body, [(state.shape, f32)], scratch=buffers, flops=big)(

time: 86.5 us -> 72.7 us (0.84)
  waiting for transfers between devices: 33.8 us -> 18.2 us
  starting transfers between devices: 25.5 us -> 29.8 us
  Pallas kernels: 23.7 us -> 21.3 us
    ppermute x10, waiting for transfers between devices: 18.7 us -> 10.4 us  [ring(): lax.ppermute(array, axis, [(i, (i + distance) % size) for i in range(size)])]
    ppermute x12 -> x15, waiting for transfers between devices: 15.1 us -> 7.76 us  [exchange(): return lax.ppermute(array, ('gx', 'gy', 'row'), route)]
    ppermute x12 -> x15, starting transfers between devices: 11.2 us -> 15 us  [exchange(): return lax.ppermute(array, ('gx', 'gy', 'row'), route)]
    pallas_call x12 -> x14, Pallas kernels: 23.7 us -> 21.3 us  [call(): pl.pallas_call(body, cost_estimate=pl.CostEstimate(flops=flops, transcend...]
  transfers between devices with their start and end apart: 22 -> 25, of which waited for: 15 -> 12; matrix products, arithmetic and copies ran while one was open for 2% -> 2% of each run, Pallas kernels for 10% -> 20%
where the time goes in v2:
time: 72.7 us; the launch traced here: 72.6 us
  starting transfers between devices  29.8 us (41%)
  Pallas kernels  21.3 us (29%)
  waiting for transfers between devices  18.2 us (25%)
  other arithmetic  2.42 us (3%)
  between operations  0.83 us (1%)
    pallas_call x14, Pallas kernels, call(): pl.pallas_call(body, cost_estimate=pl.CostEstimate(flops=flops, transcend...  21.3 us
    ppermute x15, starting transfers between devices, exchange(): return lax.ppermute(array, ('gx', 'gy', 'row'), route)  15 us
    ppermute x10, starting transfers between devices, ring(): lax.ppermute(array, axis, [(i, (i + distance) % size) for i in range(size)])  14.8 us
    ppermute x10, waiting for transfers between devices, ring(): lax.ppermute(array, axis, [(i, (i + distance) % size) for i in range(size)])  10.4 us
    ppermute x15, waiting for transfers between devices, exchange(): return lax.ppermute(array, ('gx', 'gy', 'row'), route)  7.76 us
    add x3, other arithmetic, rest_halved(): return staying + arrived  1.97 us
  transfers between devices with their start and end apart: 25, of which 12 were waited for; matrix products, arithmetic and copies ran while one was open for 2% of the time, Pallas kernels for 20%

profile of v2, /device:TPU:0, one launch (start us, length us, event | category | flops | bytes accessed | tf_op | source)
XLA Modules:
  0.0 72.6 jit_solution(5442850003315785773)
XLA Ops:
  2.3 2.0 %collective-permute-start.1 = (f32[8,32,128]{2,1,0:T(8,128)S(1)}, f32[8,32,128]{2,1,0:T(8,128)S(1)}, u32[]{:S(2)}, u32[]{:S(2)}) collective-permute-start(f32[8,32,128]{2,1,0:T(8,128)S(1)} %get-tuple-element.45), channel_id=1, source_target_pairs={{0,24},{8,0},{16,8},{24,16},{1,25},{9,1},{17,9},{25,17},{2,26},{10... | collective-permute-start | bytes 393224 | tf_op jit(solution)/shard_map/ppermute | solution.py:20
  4.3 2.6 %collective-permute-done.before = f32[8,32,128]{2,1,0:T(8,128)S(1)} collective-permute-done((f32[8,32,128]{2,1,0:T(8,128)S(1)}, f32[8,32,128]{2,1,0:T(8,128)S(1)}, u32[]{:S(2)}, u32[]{:S(2)}) %collective-permute-start) | collective-permute-done | bytes 131104 | tf_op jit(solution)/shard_map/ppermute | solution.py:20
  8.2 1.6 %collective-permute-start.2 = (f32[22,8,128]{2,1,0:T(8,128)S(1)}, f32[22,8,128]{2,1,0:T(8,128)S(1)}, u32[]{:S(2)}, u32[]{:S(2)}) collective-permute-start(f32[22,8,128]{2,1,0:T(8,128)S(1)} %get-tuple-element.46), channel_id=1, source_target_pairs={{0,2},{2,4},{4,6},{6,0},{1,3},{3,5},{5,7},{7,1},{8,10},{10,12},{12... | collective-permute-start | bytes 270344 | tf_op jit(solution)/shard_map/ppermute | solution.py:20
  9.8 2.2 %collective-permute-start.3 = (f32[22,8,128]{2,1,0:T(8,128)S(1)}, f32[22,8,128]{2,1,0:T(8,128)S(1)}, u32[]{:S(2)}, u32[]{:S(2)}) collective-permute-start(f32[22,8,128]{2,1,0:T(8,128)S(1)} %get-tuple-element.47), channel_id=1, source_target_pairs={{0,6},{2,0},{4,2},{6,4},{1,7},{3,1},{5,3},{7,5},{8,14},{10,8},{12,... | collective-permute-start | bytes 270344 | tf_op jit(solution)/shard_map/ppermute | solution.py:20
  12.0 1.2 %shard_map.88.last_ref = bf16[1024,512]{1,0:T(8,128)(2,1)S(1)} custom-call(bf16[1024,512]{1,0:T(8,128)(2,1)} %weight_ref.2), custom_call_target="tpu_custom_call" | custom-call | flops 2147483648 | tf_op jit(solution)/shard_map/pallas_call | solution.py:450
  13.3 2.0 %collective-permute-done.2.below = f32[22,8,128]{2,1,0:T(8,128)S(1)} collective-permute-done((f32[22,8,128]{2,1,0:T(8,128)S(1)}, f32[22,8,128]{2,1,0:T(8,128)S(1)}, u32[]{:S(2)}, u32[]{:S(2)}) %collective-permute-start.2) | collective-permute-done | bytes 90144 | tf_op jit(solution)/shard_map/ppermute | solution.py:20
  15.3 1.8 %collective-permute-done.3.above = f32[22,8,128]{2,1,0:T(8,128)S(1)} collective-permute-done((f32[22,8,128]{2,1,0:T(8,128)S(1)}, f32[22,8,128]{2,1,0:T(8,128)S(1)}, u32[]{:S(2)}, u32[]{:S(2)}) %collective-permute-start.3) | collective-permute-done | bytes 90144 | tf_op jit(solution)/shard_map/ppermute | solution.py:20
  17.6 1.6 %collective-permute-start.4 = (f32[4,40,128]{2,1,0:T(8,128)S(1)}, f32[4,40,128]{2,1,0:T(8,128)S(1)}, u32[]{:S(2)}, u32[]{:S(2)}) collective-permute-start(f32[4,40,128]{2,1,0:T(8,128)S(1)} %get-tuple-element.49), channel_id=1, source_target_pairs={{0,1},{1,0},{2,3},{3,2},{4,5},{5,4},{6,7},{7,6},{8,9},{9,8},{10,11... | collective-permute-start | bytes 245768 | tf_op jit(solution)/shard_map/ppermute | solution.py:20
  19.4 2.7 %collective-permute-done.4.earlier.later = f32[4,40,128]{2,1,0:T(8,128)S(1)} collective-permute-done((f32[4,40,128]{2,1,0:T(8,128)S(1)}, f32[4,40,128]{2,1,0:T(8,128)S(1)}, u32[]{:S(2)}, u32[]{:S(2)}) %collective-permute-start.4) | collective-permute-done | bytes 81952 | tf_op jit(solution)/shard_map/ppermute | solution.py:20
  22.1 4.2 %shard_map.87 = (f32[2,16,32,128]{3,2,1,0:T(8,128)S(1)}, bf16[128,512]{1,0:T(8,128)(2,1)S(1)}, bf16[128,512]{1,0:T(8,128)(2,1)S(1)}, f32[2,22,40,128]{3,2,1,0:T(8,128)}) custom-call(f32[3,22,40,128]{3,2,1,0:T(8,128)S(1)} %get-tuple-element.48.whole, f32[4,40,128]{2,1,0:T(8,128)S(1)} %collective-permute-done.4.earlier.later, ...), custom_call_target="tpu_custom_call" | custom-call | flops 2147483648 | tf_op jit(solution)/shard_map/pallas_call | solution.py:450
  26.3 1.6 %collective-permute-start.7 = (bf16[128,512]{1,0:T(8,128)(2,1)S(1)}, bf16[128,512]{1,0:T(8,128)(2,1)S(1)}, u32[]{:S(2)}, u32[]{:S(2)}) collective-permute-start(bf16[128,512]{1,0:T(8,128)(2,1)S(1)} %get-tuple-element.54.inputs_ref.own_ref), channel_id=1, source_target_pairs={{0,1},{1,0},{2,3},{3,2},{4,5},{5,4},{6,7},{7,6},{8,9},{9,8},{10,11... | collective-permute-start | bytes 393224 | tf_op jit(solution)/shard_map/ppermute | solution.py:312
  29.8 1.5 %shard_map.89.third = f32[16,32,128]{2,1,0:T(8,128)S(1)} custom-call(bf16[128,512]{1,0:T(8,128)(2,1)S(1)} %get-tuple-element.54.inputs_ref.own_ref, bf16[512,1024]{1,0:T(8,128)(2,1)S(1)} %copy-done.1, bf16[1024,1024]{1,0:T(8,128)(2,1)S(1)} %copy-done, bf16[1024,512]{1,0:T(8,128)(2,1)S(1)} %shard_map.88.last_ref), custom_call_target="tpu_custom_call" | custom-call | flops 1073741824 | tf_op jit(solution)/shard_map/pallas_call | solution.py:450
  31.5 1.7 %collective-permute-start.6 = (f32[8,32,128]{2,1,0:T(8,128)S(1)}, f32[8,32,128]{2,1,0:T(8,128)S(1)}, u32[]{:S(2)}, u32[]{:S(2)}) collective-permute-start(f32[8,32,128]{2,1,0:T(8,128)S(1)} %get-tuple-element.53), channel_id=1, source_target_pairs={{0,24},{8,0},{16,8},{24,16},{1,25},{9,1},{17,9},{25,17},{2,26},{10... | collective-permute-start | bytes 393224 | tf_op jit(solution)/shard_map/ppermute | solution.py:20
  33.2 1.5 %collective-permute-start.11 = (bf16[128,512]{1,0:T(8,128)(2,1)S(1)}, bf16[128,512]{1,0:T(8,128)(2,1)S(1)}, u32[]{:S(2)}, u32[]{:S(2)}) collective-permute-start(bf16[128,512]{1,0:T(8,128)(2,1)S(1)} %get-tuple-element.61.own_ref), channel_id=1, source_target_pairs={{0,1},{1,0},{2,3},{3,2},{4,5},{5,4},{6,7},{7,6},{8,9},{9,8},{10,11... | collective-permute-start | bytes 393224 | tf_op jit(solution)/shard_map/ppermute | solution.py:312
  36.8 3.6 %shard_map.91 = (bf16[512,512]{1,0:T(8,128)(2,1)S(1)}, bf16[512,1024]{1,0:T(8,128)(2,1)S(1)}, f32[512,1024]{1,0:T(8,128)S(1)}, bf16[512,1024]{1,0:T(8,128)(2,1)S(1)}, f32[512,1024]{1,0:T(8,128)S(1)}) custom-call(bf16[128,512]{1,0:T(8,128)(2,1)S(1)} %get-tuple-element.54.inputs_ref.own_ref, bf16[128,512]{1,0:T(8,128)(2,1)S(1)} %collective-permute-done.7.a_ref, ...), custom_call_target="tpu_custom_call" | custom-call | flops 4294967296 | tf_op jit(solution)/shard_map/pallas_call | solution.py:450
  40.8 1.7 %collective-permute-done.13.c_ref = bf16[128,512]{1,0:T(8,128)(2,1)S(1)} collective-permute-done((bf16[128,512]{1,0:T(8,128)(2,1)S(1)}, bf16[128,512]{1,0:T(8,128)(2,1)S(1)}, u32[]{:S(2)}, u32[]{:S(2)}) %collective-permute-start.13) | collective-permute-done | bytes 131104 | tf_op jit(solution)/shard_map/ppermute | solution.py:312
  43.8 1.4 %shard_map.94 = (bf16[512,1024]{1,0:T(8,128)(2,1)S(1)}, f32[128,1024]{1,0:T(8,128)S(1)}, f32[128,1024]{1,0:T(8,128)S(1)}) custom-call(bf16[512,512]{1,0:T(8,128)(2,1)S(1)} %get-tuple-element.62.carried_ref, bf16[1024,512]{1,0:T(8,128)(2,1)S(1)} %copy-done.2, f32[512,1024]{1,0:T(8,128)S(1)} %get-tuple-element.63.slope_ref, ...), custom_call_target="tpu_custom_call" | custom-call | flops 2147483648 | tf_op jit(solution)/shard_map/pallas_call | solution.py:450
  47.8 2.7 %collective-permute-start.16 = (f32[22,8,128]{2,1,0:T(8,128)S(1)}, f32[22,8,128]{2,1,0:T(8,128)S(1)}, u32[]{:S(2)}, u32[]{:S(2)}) collective-permute-start(f32[22,8,128]{2,1,0:T(8,128)S(1)} %get-tuple-element.58), channel_id=1, source_target_pairs={{0,6},{2,0},{4,2},{6,4},{1,7},{3,1},{5,3},{7,5},{8,14},{10,8},{12,... | collective-permute-start | bytes 270344 | tf_op jit(solution)/shard_map/ppermute | solution.py:20
  52.4 1.4 %collective-permute-start.18 = (f32[64,1024]{1,0:T(8,128)S(1)}, f32[64,1024]{1,0:T(8,128)S(1)}, u32[]{:S(2)}, u32[]{:S(2)}) collective-permute-start(f32[64,1024]{1,0:T(8,128)S(1)} %get-tuple-element.81), channel_id=1, source_target_pairs={{0,16},{1,17},{2,18},{3,19},{4,20},{5,21},{6,22},{7,23},{8,24},{9,... | collective-permute-start | bytes 786440 | tf_op jit(solution)/shard_map/ppermute | solution.py:312
  54.3 2.3 %shard_map.96 = (bf16[512,1024]{1,0:T(8,128)(2,1)}, f32[64,1024]{1,0:T(8,128)S(1)}, f32[64,1024]{1,0:T(8,128)S(1)}) custom-call(bf16[512,1024]{1,0:T(8,128)(2,1)S(1)} %get-tuple-element.73.carried_ref, bf16[1024,1024]{1,0:T(8,128)(2,1)S(1)} %copy-done, f32[512,1024]{1,0:T(8,128)S(1)} %get-tuple-element.74.slope_ref, ...), custom_call_target="tpu_custom_call" | custom-call | flops 2147483648 | tf_op jit(solution)/shard_map/pallas_call | solution.py:450
  59.6 1.9 %collective-permute-start.23 = (f32[32,1024]{1,0:T(8,128)S(1)}, f32[32,1024]{1,0:T(8,128)S(1)}, u32[]{:S(2)}, u32[]{:S(2)}) collective-permute-start(f32[32,1024]{1,0:T(8,128)S(1)} %slice_add_fusion.5), channel_id=1, source_target_pairs={{0,4},{1,5},{2,6},{3,7},{4,0},{5,1},{6,2},{7,3},{8,12},{9,13},{10,... | collective-permute-start | bytes 393224 | tf_op jit(solution)/shard_map/ppermute | solution.py:312
  62.3 3.7 %shard_map.97 = f32[2,16,32,128]{3,2,1,0:T(8,128)} custom-call(f32[3,22,40,128]{3,2,1,0:T(8,128)S(1)} %get-tuple-element.78.whole, f32[4,40,128]{2,1,0:T(8,128)S(1)} %collective-permute-done.20.earlier.later, f32[4,40,128]{2,1,0:T(8,128)S(1)} %collective-permute-done.20.earlier.later, f32[2,22,40,128]{3,2,1,0:T(8,128)S(1)} %copy-done.3), custom_call_target="tpu_custom_call" | custom-call | flops 4294967296 | tf_op jit(solution)/shard_map/pallas_call | solution.py:450
  66.6 1.2 %collective-permute-start.22 = (f32[16,1024]{1,0:T(8,128)S(1)}, f32[16,1024]{1,0:T(8,128)S(1)}, u32[]{:S(2)}, u32[]{:S(2)}) collective-permute-start(f32[16,1024]{1,0:T(8,128)S(1)} %slice_add_fusion.9), channel_id=1, source_target_pairs={{0,4},{1,5},{2,6},{3,7},{4,0},{5,1},{6,2},{7,3},{8,12},{9,13},{10,... | collective-permute-start | bytes 196616 | tf_op jit(solution)/shard_map/ppermute | solution.py:312
  68.6 3.4 %collective-permute-done.22 = f32[16,1024]{1,0:T(8,128)S(1)} collective-permute-done((f32[16,1024]{1,0:T(8,128)S(1)}, f32[16,1024]{1,0:T(8,128)S(1)}, u32[]{:S(2)}, u32[]{:S(2)}) %collective-permute-start.22) | collective-permute-done | bytes 65568 | tf_op jit(solution)/shard_map/ppermute | solution.py:312
  (59 shorter events, 19.9 us)
Async XLA Ops:
  1.8 5.1 %collective-permute-start = (f32[8,32,128]{2,1,0:T(8,128)S(1)}, f32[8,32,128]{2,1,0:T(8,128)S(1)}, u32[]{:S(2)}, u32[]{:S(2)}) collective-permute-start(f32[8,32,128]{2,1,0:T(8,128)S(1)} %get-tuple-element.44), channel_id=1, source_target_pairs={{0,8},{8,16},{16,24},{24,0},{1,9},{9,17},{17,25},{25,1},{2,10},{10... | collective-permute-start | bytes 393224 | tf_op jit(solution)/shard_map/ppermute | solution.py:20
  2.3 5.8 %collective-permute-start.1 = (f32[8,32,128]{2,1,0:T(8,128)S(1)}, f32[8,32,128]{2,1,0:T(8,128)S(1)}, u32[]{:S(2)}, u32[]{:S(2)}) collective-permute-start(f32[8,32,128]{2,1,0:T(8,128)S(1)} %get-tuple-element.45), channel_id=1, source_target_pairs={{0,24},{8,0},{16,8},{24,16},{1,25},{9,1},{17,9},{25,17},{2,26},{10... | collective-permute-start | bytes 393224 | tf_op jit(solution)/shard_map/ppermute | solution.py:20
  8.2 7.2 %collective-permute-start.2 = (f32[22,8,128]{2,1,0:T(8,128)S(1)}, f32[22,8,128]{2,1,0:T(8,128)S(1)}, u32[]{:S(2)}, u32[]{:S(2)}) collective-permute-start(f32[22,8,128]{2,1,0:T(8,128)S(1)} %get-tuple-element.46), channel_id=1, source_target_pairs={{0,2},{2,4},{4,6},{6,0},{1,3},{3,5},{5,7},{7,1},{8,10},{10,12},{12... | collective-permute-start | bytes 270344 | tf_op jit(solution)/shard_map/ppermute | solution.py:20
  9.8 7.4 %collective-permute-start.3 = (f32[22,8,128]{2,1,0:T(8,128)S(1)}, f32[22,8,128]{2,1,0:T(8,128)S(1)}, u32[]{:S(2)}, u32[]{:S(2)}) collective-permute-start(f32[22,8,128]{2,1,0:T(8,128)S(1)} %get-tuple-element.47), channel_id=1, source_target_pairs={{0,6},{2,0},{4,2},{6,4},{1,7},{3,1},{5,3},{7,5},{8,14},{10,8},{12,... | collective-permute-start | bytes 270344 | tf_op jit(solution)/shard_map/ppermute | solution.py:20
  17.6 4.5 %collective-permute-start.4 = (f32[4,40,128]{2,1,0:T(8,128)S(1)}, f32[4,40,128]{2,1,0:T(8,128)S(1)}, u32[]{:S(2)}, u32[]{:S(2)}) collective-permute-start(f32[4,40,128]{2,1,0:T(8,128)S(1)} %get-tuple-element.49), channel_id=1, source_target_pairs={{0,1},{1,0},{2,3},{3,2},{4,5},{5,4},{6,7},{7,6},{8,9},{9,8},{10,11... | collective-permute-start | bytes 245768 | tf_op jit(solution)/shard_map/ppermute | solution.py:20
  26.3 6.9 %collective-permute-start.7 = (bf16[128,512]{1,0:T(8,128)(2,1)S(1)}, bf16[128,512]{1,0:T(8,128)(2,1)S(1)}, u32[]{:S(2)}, u32[]{:S(2)}) collective-permute-start(bf16[128,512]{1,0:T(8,128)(2,1)S(1)} %get-tuple-element.54.inputs_ref.own_ref), channel_id=1, source_target_pairs={{0,1},{1,0},{2,3},{3,2},{4,5},{5,4},{6,7},{7,6},{8,9},{9,8},{10,11... | collective-permute-start | bytes 393224 | tf_op jit(solution)/shard_map/ppermute | solution.py:312
  27.9 6.9 %collective-permute-start.8 = (bf16[128,512]{1,0:T(8,128)(2,1)S(1)}, bf16[128,512]{1,0:T(8,128)(2,1)S(1)}, u32[]{:S(2)}, u32[]{:S(2)}) collective-permute-start(bf16[128,512]{1,0:T(8,128)(2,1)S(1)} %get-tuple-element.54.inputs_ref.own_ref), channel_id=1, source_target_pairs={{0,2},{1,3},{2,0},{3,1},{4,6},{5,7},{6,4},{7,5},{8,10},{9,11},{10,... | collective-permute-start | bytes 393224 | tf_op jit(solution)/shard_map/ppermute | solution.py:312
  28.7 6.9 %collective-permute-start.9 = (bf16[128,512]{1,0:T(8,128)(2,1)S(1)}, bf16[128,512]{1,0:T(8,128)(2,1)S(1)}, u32[]{:S(2)}, u32[]{:S(2)}) collective-permute-start(bf16[128,512]{1,0:T(8,128)(2,1)S(1)} %get-tuple-element.54.inputs_ref.own_ref), channel_id=1, source_target_pairs={{0,3},{1,2},{2,1},{3,0},{4,7},{5,6},{6,5},{7,4},{8,11},{9,10},{10,... | collective-permute-start | bytes 393224 | tf_op jit(solution)/shard_map/ppermute | solution.py:312
  31.4 9.0 %collective-permute-start.5 = (f32[8,32,128]{2,1,0:T(8,128)S(1)}, f32[8,32,128]{2,1,0:T(8,128)S(1)}, u32[]{:S(2)}, u32[]{:S(2)}) collective-permute-start(f32[8,32,128]{2,1,0:T(8,128)S(1)} %get-tuple-element.52), channel_id=1, source_target_pairs={{0,8},{8,16},{16,24},{24,0},{1,9},{9,17},{17,25},{25,1},{2,10},{10... | collective-permute-start | bytes 393224 | tf_op jit(solution)/shard_map/ppermute | solution.py:20
  31.5 9.0 %collective-permute-start.6 = (f32[8,32,128]{2,1,0:T(8,128)S(1)}, f32[8,32,128]{2,1,0:T(8,128)S(1)}, u32[]{:S(2)}, u32[]{:S(2)}) collective-permute-start(f32[8,32,128]{2,1,0:T(8,128)S(1)} %get-tuple-element.53), channel_id=1, source_target_pairs={{0,24},{8,0},{16,8},{24,16},{1,25},{9,1},{17,9},{25,17},{2,26},{10... | collective-permute-start | bytes 393224 | tf_op jit(solution)/shard_map/ppermute | solution.py:20
  33.2 7.3 %collective-permute-start.11 = (bf16[128,512]{1,0:T(8,128)(2,1)S(1)}, bf16[128,512]{1,0:T(8,128)(2,1)S(1)}, u32[]{:S(2)}, u32[]{:S(2)}) collective-permute-start(bf16[128,512]{1,0:T(8,128)(2,1)S(1)} %get-tuple-element.61.own_ref), channel_id=1, source_target_pairs={{0,1},{1,0},{2,3},{3,2},{4,5},{5,4},{6,7},{7,6},{8,9},{9,8},{10,11... | collective-permute-start | bytes 393224 | tf_op jit(solution)/shard_map/ppermute | solution.py:312
  34.8 6.0 %collective-permute-start.12 = (bf16[128,512]{1,0:T(8,128)(2,1)S(1)}, bf16[128,512]{1,0:T(8,128)(2,1)S(1)}, u32[]{:S(2)}, u32[]{:S(2)}) collective-permute-start(bf16[128,512]{1,0:T(8,128)(2,1)S(1)} %get-tuple-element.61.own_ref), channel_id=1, source_target_pairs={{0,2},{1,3},{2,0},{3,1},{4,6},{5,7},{6,4},{7,5},{8,10},{9,11},{10,... | collective-permute-start | bytes 393224 | tf_op jit(solution)/shard_map/ppermute | solution.py:312
  35.6 6.8 %collective-permute-start.13 = (bf16[128,512]{1,0:T(8,128)(2,1)S(1)}, bf16[128,512]{1,0:T(8,128)(2,1)S(1)}, u32[]{:S(2)}, u32[]{:S(2)}) collective-permute-start(bf16[128,512]{1,0:T(8,128)(2,1)S(1)} %get-tuple-element.61.own_ref), channel_id=1, source_target_pairs={{0,3},{1,2},{2,1},{3,0},{4,7},{5,6},{6,5},{7,4},{8,11},{9,10},{10,... | collective-permute-start | bytes 393224 | tf_op jit(solution)/shard_map/ppermute | solution.py:312
  45.1 7.2 %collective-permute-start.15 = (f32[128,1024]{1,0:T(8,128)S(1)}, f32[128,1024]{1,0:T(8,128)S(1)}, u32[]{:S(2)}, u32[]{:S(2)}) collective-permute-start(f32[128,1024]{1,0:T(8,128)S(1)} %get-tuple-element.69), channel_id=1, source_target_pairs={{0,8},{1,9},{2,10},{3,11},{4,12},{5,13},{6,14},{7,15},{8,0},{9,1},... | collective-permute-start | bytes 1572872 | tf_op jit(solution)/shard_map/ppermute | solution.py:312
  45.7 5.5 %collective-permute-start.19 = (f32[64,512]{1,0:T(8,128)S(1)}, f32[64,512]{1,0:T(8,128)S(1)}, u32[]{:S(2)}, u32[]{:S(2)}) collective-permute-start(f32[64,512]{1,0:T(8,128)S(1)} %get-tuple-element.85), channel_id=1, source_target_pairs={{0,16},{1,17},{2,18},{3,19},{4,20},{5,21},{6,22},{7,23},{8,24},{9,... | collective-permute-start | bytes 393224 | tf_op jit(solution)/shard_map/ppermute | solution.py:312
  46.6 7.2 %collective-permute-start.10 = (f32[22,8,128]{2,1,0:T(8,128)S(1)}, f32[22,8,128]{2,1,0:T(8,128)S(1)}, u32[]{:S(2)}, u32[]{:S(2)}) collective-permute-start(f32[22,8,128]{2,1,0:T(8,128)S(1)} %get-tuple-element.57), channel_id=1, source_target_pairs={{0,2},{2,4},{4,6},{6,0},{1,3},{3,5},{5,7},{7,1},{8,10},{10,12},{12... | collective-permute-start | bytes 270344 | tf_op jit(solution)/shard_map/ppermute | solution.py:20
  47.8 6.0 %collective-permute-start.16 = (f32[22,8,128]{2,1,0:T(8,128)S(1)}, f32[22,8,128]{2,1,0:T(8,128)S(1)}, u32[]{:S(2)}, u32[]{:S(2)}) collective-permute-start(f32[22,8,128]{2,1,0:T(8,128)S(1)} %get-tuple-element.58), channel_id=1, source_target_pairs={{0,6},{2,0},{4,2},{6,4},{1,7},{3,1},{5,3},{7,5},{8,14},{10,8},{12,... | collective-permute-start | bytes 270344 | tf_op jit(solution)/shard_map/ppermute | solution.py:20
  51.2 5.9 %collective-permute-start.24 = (f32[32,512]{1,0:T(8,128)S(1)}, f32[32,512]{1,0:T(8,128)S(1)}, u32[]{:S(2)}, u32[]{:S(2)}) collective-permute-start(f32[32,512]{1,0:T(8,128)S(1)} %slice_add_fusion.11), channel_id=1, source_target_pairs={{0,4},{1,5},{2,6},{3,7},{4,0},{5,1},{6,2},{7,3},{8,12},{9,13},{10,... | collective-permute-start | bytes 196616 | tf_op jit(solution)/shard_map/ppermute | solution.py:312
  52.4 7.2 %collective-permute-start.18 = (f32[64,1024]{1,0:T(8,128)S(1)}, f32[64,1024]{1,0:T(8,128)S(1)}, u32[]{:S(2)}, u32[]{:S(2)}) collective-permute-start(f32[64,1024]{1,0:T(8,128)S(1)} %get-tuple-element.81), channel_id=1, source_target_pairs={{0,16},{1,17},{2,18},{3,19},{4,20},{5,21},{6,22},{7,23},{8,24},{9,... | collective-permute-start | bytes 786440 | tf_op jit(solution)/shard_map/ppermute | solution.py:312
  56.6 5.0 %collective-permute-start.17 = (f32[64,1024]{1,0:T(8,128)S(1)}, f32[64,1024]{1,0:T(8,128)S(1)}, u32[]{:S(2)}, u32[]{:S(2)}) collective-permute-start(f32[64,1024]{1,0:T(8,128)S(1)} %get-tuple-element.77), channel_id=1, source_target_pairs={{0,8},{1,9},{2,10},{3,11},{4,12},{5,13},{6,14},{7,15},{8,0},{9,1},... | collective-permute-start | bytes 786440 | tf_op jit(solution)/shard_map/ppermute | solution.py:312
  57.8 4.5 %collective-permute-start.20 = (f32[4,40,128]{2,1,0:T(8,128)S(1)}, f32[4,40,128]{2,1,0:T(8,128)S(1)}, u32[]{:S(2)}, u32[]{:S(2)}) collective-permute-start(f32[4,40,128]{2,1,0:T(8,128)S(1)} %get-tuple-element.72), channel_id=1, source_target_pairs={{0,1},{1,0},{2,3},{3,2},{4,5},{5,4},{6,7},{7,6},{8,9},{9,8},{10,11... | collective-permute-start | bytes 245768 | tf_op jit(solution)/shard_map/ppermute | solution.py:20
  59.6 8.3 %collective-permute-start.23 = (f32[32,1024]{1,0:T(8,128)S(1)}, f32[32,1024]{1,0:T(8,128)S(1)}, u32[]{:S(2)}, u32[]{:S(2)}) collective-permute-start(f32[32,1024]{1,0:T(8,128)S(1)} %slice_add_fusion.5), channel_id=1, source_target_pairs={{0,4},{1,5},{2,6},{3,7},{4,0},{5,1},{6,2},{7,3},{8,12},{9,13},{10,... | collective-permute-start | bytes 393224 | tf_op jit(solution)/shard_map/ppermute | solution.py:312
  61.6 5.0 %collective-permute-start.21 = (f32[32,1024]{1,0:T(8,128)S(1)}, f32[32,1024]{1,0:T(8,128)S(1)}, u32[]{:S(2)}, u32[]{:S(2)}) collective-permute-start(f32[32,1024]{1,0:T(8,128)S(1)} %get-tuple-element.83), channel_id=1, source_target_pairs={{0,16},{1,17},{2,18},{3,19},{4,20},{5,21},{6,22},{7,23},{8,24},{9,... | collective-permute-start | bytes 393224 | tf_op jit(solution)/shard_map/ppermute | solution.py:312
  66.6 5.3 %collective-permute-start.22 = (f32[16,1024]{1,0:T(8,128)S(1)}, f32[16,1024]{1,0:T(8,128)S(1)}, u32[]{:S(2)}, u32[]{:S(2)}) collective-permute-start(f32[16,1024]{1,0:T(8,128)S(1)} %slice_add_fusion.9), channel_id=1, source_target_pairs={{0,4},{1,5},{2,6},{3,7},{4,0},{5,1},{6,2},{7,3},{8,12},{9,13},{10,... | collective-permute-start | bytes 196616 | tf_op jit(solution)/shard_map/ppermute | solution.py:312
  (5 other events, 27.6 us)

commit v3 on v2

--- a/solution.py
+++ b/solution.py
@@ -35,28 +35,52 @@
             (lambda x, rows: third[x, rows, :], HALO - 1))
 
 
+LAYERS = 3 * HALO - 1
+PACKED = LAYERS + 2
+
+
+def rounded(value):
+    return value.astype(jnp.bfloat16).astype(jnp.float32)
+
+
+def whole_tiles(rows):
+    return -(-rows // 16) * 16
+
+
 def plane_of(state, third, before, after, kind, plane, rows):
     read, depth = fields(state, third)[kind]
     length = state.shape[1]
     x = plane - HALO
     if x < -depth or x >= length + depth:
         return None
-    if x < 0:
-        return before[kind * HALO + depth + x, rows, :]
-    if x >= length:
-        return after[kind * HALO + x - length, rows, :]
-    return read(x, rows)
-
-
-def edge_rows_body(state, third, before, after, leading_ref, trailing_ref):
-    length, height = state.shape[1:3]
-    for plane in range(length + 2 * HALO):
-        for kind, depth in enumerate((HALO, HALO, HALO - 1)):
-            for out_ref, start in ((leading_ref, 0), (trailing_ref, height - depth)):
+    if 0 <= x < length:
+        return read(x, rows)
+    halo, layer = (before, kind * HALO + depth + x) if x < 0 else (after, kind * HALO + x - length)
+    value = halo[layer].astype(jnp.float32)
+    if kind < 2 and x in (-1, length):
+        value = value + halo[LAYERS + kind].astype(jnp.float32)
+    return value[rows]
+
+
+def edge_rows_body(state, third, before, after, leading_ref, trailing_ref, leading, trailing):
+    length, height, width = state.shape[1:]
+    planes = length + 2 * HALO
+    for side, start_of, nearest in ((leading, lambda depth: 0, 0), (trailing, lambda depth: height - depth, HALO - 1)):
+        for plane in range(planes):
+            for kind, depth in enumerate((HALO, HALO, HALO - 1)):
+                start, place = (start_of(depth), plane * PACKED)
                 value = plane_of(state, third, before, after, kind, plane, slice(start, start + depth))
                 if value is None:
-                    value = jnp.zeros((depth, state.shape[3]), jnp.float32)
-                out_ref[plane, kind * HALO:kind * HALO + depth, :] = value
+                    value = jnp.zeros((depth, width), jnp.float32)
+                side[place + kind * HALO:place + kind * HALO + depth, :] = value
+                if kind < 2:
+                    edge = value[nearest:nearest + 1]
+                    side[place + LAYERS + kind:place + LAYERS + kind + 1, :] = edge - rounded(edge)
+        filled = planes * PACKED
+        if filled < side.shape[0]:
+            side[filled:, :] = jnp.zeros((side.shape[0] - filled, width), jnp.float32)
+    leading_ref[...] = leading[...].astype(jnp.bfloat16)
+    trailing_ref[...] = trailing[...].astype(jnp.bfloat16)
 
 
 def strips_of(planes, width):
@@ -69,40 +93,66 @@
     return places, -(-len(places) // each)
 
 
-def assemble_body(state, third, before, after, below, above, whole_ref, strips_ref):
-    length, height, width = state.shape[1:]
-    planes = length + 2 * HALO
-    places, _ = strips_of(planes, width)
-    lanes = lax.broadcasted_iota(jnp.int32, whole_ref.shape[2:], 1)
+def assemble_body(state, third, before, after, below_ref, above_ref, whole_ref, strips_ref, below, above, strips):
+    _, height, width = state.shape[1:]
+    planes, rows = whole_ref.shape[1:3]
+    places, count = strips_of(planes, width)
+    lanes = lax.broadcasted_iota(jnp.int32, (rows, width), 1)
+    below[...] = below_ref[...].astype(jnp.float32)
+    above[...] = above_ref[...].astype(jnp.float32)
     tiles = {}
+
+    def gather_lanes(tile, value, shift, first, size):
+        turned = pltpu.roll(value, shift, axis=1)
+        here = (lanes >= first) & (lanes < first + size)
+        tiles[tile] = jnp.where(here, turned, tiles[tile]) if tile in tiles else turned
+
     for kind, depth in enumerate((HALO, HALO, HALO - 1)):
         for plane in range(planes):
             value = plane_of(state, third, before, after, kind, plane, slice(0, height))
             if value is None:
                 continue
-            held = slice(kind * HALO, kind * HALO + depth)
+            held = slice(plane * PACKED + kind * HALO, plane * PACKED + kind * HALO + depth)
             whole_ref[kind, plane, EDGE:EDGE + height, :] = value
-            whole_ref[kind, plane, EDGE - depth:EDGE, :] = below[plane, held, :]
-            whole_ref[kind, plane, EDGE + height:EDGE + height + depth, :] = above[plane, held, :]
+            whole_ref[kind, plane, EDGE - depth:EDGE, :] = below[held, :]
+            whole_ref[kind, plane, EDGE + height:EDGE + height + depth, :] = above[held, :]
+            if kind < 2:
+                rest = slice(plane * PACKED + LAYERS + kind, plane * PACKED + LAYERS + kind + 1)
+                whole_ref[kind, plane, EDGE - 1:EDGE, :] = below[held.stop - 1:held.stop, :] + below[rest, :]
+                whole_ref[kind, plane, EDGE + height:EDGE + height + 1, :] = (
+                    above[held.start:held.start + 1, :] + above[rest, :])
             tile, shift = places[kind, plane]
-            turned = pltpu.roll(whole_ref[kind, plane], (shift + HALO) % width, axis=1)
-            here = (lanes >= shift) & (lanes < shift + 2 * HALO)
-            tiles[tile] = jnp.where(here, turned, tiles[tile]) if tile in tiles else turned
+            value = whole_ref[kind, plane]
+            gather_lanes(tile, value, (shift + HALO) % width, shift, 2 * HALO)
+            if kind < 2:
+                first = 2 * (kind * planes + plane)
+                gather_lanes(count, value - rounded(value), first + 1, first, 2)
     for tile, value in tiles.items():
-        strips_ref[tile] = value
-
-
-def load_sides(whole, earlier, later, kind, target, places, first):
-    rows, width = whole.shape[2:]
+        strips[tile * rows:(tile + 1) * rows, :] = value
+    filled = len(tiles) * rows
+    if filled < strips.shape[0]:
+        strips[filled:, :] = jnp.zeros((strips.shape[0] - filled, width), jnp.float32)
+    strips_ref[...] = strips[...].astype(jnp.bfloat16)
+
+
+def load_sides(whole, earlier, later, kind, target, first):
+    planes, rows, width = whole.shape[1:]
+    places, count = strips_of(planes, width)
     lanes = lax.broadcasted_iota(jnp.int32, (rows, width), 1)
-    for plane in range(whole.shape[1]):
+
+    def both(tile, shift, size):
+        held = slice(tile * rows, (tile + 1) * rows)
+        after = (lanes >= shift + size) & (lanes < shift + 2 * size)
+        return pltpu.roll(jnp.where(after, later[held, :], earlier[held, :]), (2 * width - shift - size) % width, axis=1)
+
+    for plane in range(planes):
         if (kind, plane) not in places:
             continue
-        tile, shift = places[kind, plane]
-        back = (2 * width - shift - HALO) % width
-        beside = later[tile] if later is earlier else jnp.where(
-            (lanes >= shift + HALO) & (lanes < shift + 2 * HALO), later[tile], earlier[tile])
-        target[plane, first:first + rows, :] = pltpu.roll(beside, back, axis=1)
+        value = both(*places[kind, plane], HALO)
+        if kind < 2:
+            rest = both(count, 2 * (kind * planes + plane), 1)
+            value = value + jnp.where((lanes == 0) | (lanes == width - 1), rest, 0.0)
+        target[plane, first:first + rows, :] = value
 
 
 def one_step(source, target, fixed, planes, rows, sides):
@@ -138,10 +188,9 @@
 
 
 def run_steps(whole, earlier, later, fixed, now, then):
-    places, _ = strips_of(whole.shape[1], whole.shape[3])
     planes, rows = whole.shape[1:3]
     for kind, pair in enumerate(now):
-        load_sides(whole, earlier, later, kind, pair[1], places, 8)
+        load_sides(whole, earlier, later, kind, pair[1], 8)
         for plane in range(planes):
             pair[0][plane, 8:8 + rows, :] = whole[kind, plane]
     for step in range(HALO):
@@ -198,10 +247,12 @@
     return pairs[:2], pairs[2:]
 
 
-def first_steps_body(edge, whole, earlier, later, state_ref, inputs_ref, targets_ref, fixed_ref, *scratch):
-    *fields_now, side, column_ref, semaphores = scratch
+def first_steps_body(edge, whole, earlier_ref, later_ref, state_ref, inputs_ref, targets_ref, fixed_ref, *scratch):
+    *fields_now, side, earlier, later, column_ref, semaphores = scratch
     length, height, width = state_ref.shape[1:]
-    load_sides(whole, earlier, later, 2, side, strips_of(whole.shape[1], width)[0], 0)
+    earlier[...] = earlier_ref[...].astype(jnp.float32)
+    later[...] = later_ref[...].astype(jnp.float32)
+    load_sides(whole, earlier, later, 2, side, 0)
     copies = start_copies([(whole.at[2], fixed_ref.at[0]), (side, fixed_ref.at[1])], semaphores)
     now = run_steps(whole, earlier, later, [(whole.at[2], side)], *paired(fields_now))
     move, order = (move_order(width // edge, edge), cell_order(edge))
@@ -234,10 +285,12 @@
         field_ref[x, y:y + edge, :] = moved[number * edge:(number + 1) * edge, :]
 
 
-def last_steps_body(whole, earlier, later, fixed, state_ref, *scratch):
-    *fields_now, side = scratch
-    length, height, width = state_ref.shape[1:]
-    load_sides(whole, earlier, later, 2, side, strips_of(whole.shape[1], width)[0], 0)
+def last_steps_body(whole, earlier_ref, later_ref, fixed, state_ref, *scratch):
+    *fields_now, side, earlier, later = scratch
+    length, height, _ = state_ref.shape[1:]
+    earlier[...] = earlier_ref[...].astype(jnp.float32)
+    later[...] = later_ref[...].astype(jnp.float32)
+    load_sides(whole, earlier, later, 2, side, 0)
     both = [(fixed.at[0], fixed.at[1]), (whole.at[2], side)]
     now = run_steps(whole, earlier, later, both, *paired(fields_now))
     for species, field in enumerate(now):
@@ -261,8 +314,11 @@
     for kind, depth in enumerate((HALO, HALO, HALO - 1)):
         read = fields(state, third)[kind][0]
         for plane in range(depth):
-            leading_ref[kind * HALO + plane] = read(plane, slice(None))
-            trailing_ref[kind * HALO + plane] = read(length - depth + plane, slice(None))
+            for out_ref, x, nearest in ((leading_ref, plane, 0), (trailing_ref, length - depth + plane, length - 1)):
+                value = read(x, slice(None))
+                out_ref[kind * HALO + plane] = value.astype(jnp.bfloat16)
+                if kind < 2 and x == nearest:
+                    out_ref[LAYERS + kind] = (value - rounded(value)).astype(jnp.bfloat16)
 
 
 def first_faces_body(state_ref, third_ref, leading_ref, trailing_ref, state_out, third_out, semaphores):
@@ -277,7 +333,8 @@
 
 def edge_rows(state, third, before, after):
     planes = state.shape[1] + 2 * HALO
-    return kernel_call(edge_rows_body, [((planes, 3 * HALO - 1, state.shape[3]), jnp.float32)] * 2)(
+    packed = (whole_tiles(planes * PACKED), state.shape[3])
+    return kernel_call(edge_rows_body, [(packed, jnp.bfloat16)] * 2, scratch=[(packed, jnp.float32)] * 2)(
         state, third, before, after
     )
 
@@ -289,8 +346,10 @@
 def assemble(state, third, before, after, below, above):
     length, height, width = state.shape[1:]
     planes, rows = (length + 2 * HALO, height + 2 * EDGE)
-    outputs = [(3, planes, rows, width), (strips_of(planes, width)[1], rows, width)]
-    return kernel_call(assemble_body, [(shape, jnp.float32) for shape in outputs])(
+    strips = (whole_tiles((strips_of(planes, width)[1] + 1) * rows), width)
+    outputs = [((3, planes, rows, width), jnp.float32), (strips, jnp.bfloat16)]
+    scratch = [(shape, jnp.float32) for shape in (below.shape, above.shape, strips)]
+    return kernel_call(assemble_body, outputs, scratch=scratch)(
         state, third, before, after, below, above
     )
 
@@ -471,6 +530,7 @@
     planes, rows = (length + 2 * HALO, height + 2 * EDGE)
     fixed = ((2, planes, rows, width), f32)
     buffers = [((planes, 8 + rows + 8, width), f32)] * 8 + [((planes, rows, width), f32)]
+    buffers += [((whole_tiles((strips_of(planes, width)[1] + 1) * rows), width), f32)] * 2
     count = length * height * width // PATCH ** 3
     cells, hidden = weight_first.shape
     hidden_second = weight_middle.shape[1]
@@ -480,7 +540,7 @@
     stages = reduction_stages(mesh_sizes)
     big = 1 << 32
 
-    layers = ((3 * HALO - 1, height, width), f32)
+    layers = ((PACKED, height, width), bf16)
     leading, trailing, near_state, near_third = kernel_call(
         first_faces_body, [layers, layers, (concentrations.shape, f32), (diffusivity.shape, f32)],
         far=(0, 1), copies=2,

time: 72.7 us -> 70.2 us (0.966)
  waiting for transfers between devices: 18.2 us -> 15.4 us
    ppermute x10, waiting for transfers between devices: 10.4 us -> 7.76 us  [ring(): lax.ppermute(array, axis, [(i, (i + distance) % size) for i in range(size)])]
    ppermute x15, starting transfers between devices: 15 us -> 15.8 us  [exchange(): return lax.ppermute(array, ('gx', 'gy', 'row'), route)]
  transfers between devices with their start and end apart: 25 -> 25, of which waited for: 12 -> 11; matrix products, arithmetic and copies ran while one was open for 2% -> 3% of each run, Pallas kernels for 20% -> 20%
where the time goes in v3:
time: 70.2 us; the launch traced here: 70.1 us
  starting transfers between devices  30.4 us (43%)
  Pallas kernels  20.9 us (30%)
  waiting for transfers between devices  15.4 us (22%)
  other arithmetic  2.43 us (3%)
  between operations  0.83 us (1%)
    pallas_call x14, Pallas kernels, call(): pl.pallas_call(body, cost_estimate=pl.CostEstimate(flops=flops, transcend...  20.9 us
    ppermute x15, starting transfers between devices, exchange(): return lax.ppermute(array, ('gx', 'gy', 'row'), route)  15.8 us
    ppermute x10, starting transfers between devices, ring(): lax.ppermute(array, axis, [(i, (i + distance) % size) for i in range(size)])  14.6 us
    ppermute x10, waiting for transfers between devices, ring(): lax.ppermute(array, axis, [(i, (i + distance) % size) for i in range(size)])  7.76 us
    ppermute x15, waiting for transfers between devices, exchange(): return lax.ppermute(array, ('gx', 'gy', 'row'), route)  7.67 us
    add x3, other arithmetic, rest_halved(): return staying + arrived  1.97 us
  transfers between devices with their start and end apart: 25, of which 11 were waited for; matrix products, arithmetic and copies ran while one was open for 3% of the time, Pallas kernels for 20%

profile of v3, /device:TPU:0, one launch (start us, length us, event | category | flops | bytes accessed | tf_op | source)
XLA Modules:
  0.0 70.1 jit_solution(13453497273602154227)
XLA Ops:
  2.3 2.0 %collective-permute-start.1 = (bf16[10,32,128]{2,1,0:T(8,128)(2,1)S(1)}, bf16[10,32,128]{2,1,0:T(8,128)(2,1)S(1)}, u32[]{:S(2)}, u32[]{:S(2)}) collective-permute-start(bf16[10,32,128]{2,1,0:T(8,128)(2,1)S(1)} %get-tuple-element.45), channel_id=1, source_target_pairs={{0,24},{8,0},{16,8},{24,16},{1,25},{9,1},{17,9},{25,17},{2,26},{10... | collective-permute-start | bytes 245768 | tf_op jit(solution)/shard_map/ppermute | solution.py:20
  4.3 2.1 %collective-permute-done.before = bf16[10,32,128]{2,1,0:T(8,128)(2,1)S(1)} collective-permute-done((bf16[10,32,128]{2,1,0:T(8,128)(2,1)S(1)}, bf16[10,32,128]{2,1,0:T(8,128)(2,1)S(1)}, u32[]{:S(2)}, u32[]{:S(2)}) %collective-permute-start) | collective-permute-done | bytes 81952 | tf_op jit(solution)/shard_map/ppermute | solution.py:20
  7.1 1.7 %collective-permute-start.2 = (bf16[224,128]{1,0:T(8,128)(2,1)S(1)}, bf16[224,128]{1,0:T(8,128)(2,1)S(1)}, u32[]{:S(2)}, u32[]{:S(2)}) collective-permute-start(bf16[224,128]{1,0:T(8,128)(2,1)S(1)} %get-tuple-element.46), channel_id=1, source_target_pairs={{0,2},{2,4},{4,6},{6,0},{1,3},{3,5},{5,7},{7,1},{8,10},{10,12},{12... | collective-permute-start | bytes 172040 | tf_op jit(solution)/shard_map/ppermute | solution.py:20
  8.9 2.1 %collective-permute-start.3 = (bf16[224,128]{1,0:T(8,128)(2,1)S(1)}, bf16[224,128]{1,0:T(8,128)(2,1)S(1)}, u32[]{:S(2)}, u32[]{:S(2)}) collective-permute-start(bf16[224,128]{1,0:T(8,128)(2,1)S(1)} %get-tuple-element.47), channel_id=1, source_target_pairs={{0,6},{2,0},{4,2},{6,4},{1,7},{3,1},{5,3},{7,5},{8,14},{10,8},{12,... | collective-permute-start | bytes 172040 | tf_op jit(solution)/shard_map/ppermute | solution.py:20
  11.0 1.2 %shard_map.88.last_ref = bf16[1024,512]{1,0:T(8,128)(2,1)S(1)} custom-call(bf16[1024,512]{1,0:T(8,128)(2,1)} %weight_ref.2), custom_call_target="tpu_custom_call" | custom-call | flops 2147483648 | tf_op jit(solution)/shard_map/pallas_call | solution.py:509
  13.3 1.4 %collective-permute-done.3.above_ref = bf16[224,128]{1,0:T(8,128)(2,1)S(1)} collective-permute-done((bf16[224,128]{1,0:T(8,128)(2,1)S(1)}, bf16[224,128]{1,0:T(8,128)(2,1)S(1)}, u32[]{:S(2)}, u32[]{:S(2)}) %collective-permute-start.3) | collective-permute-done | bytes 57376 | tf_op jit(solution)/shard_map/ppermute | solution.py:20
  15.2 1.5 %collective-permute-start.4 = (bf16[208,128]{1,0:T(8,128)(2,1)S(1)}, bf16[208,128]{1,0:T(8,128)(2,1)S(1)}, u32[]{:S(2)}, u32[]{:S(2)}) collective-permute-start(bf16[208,128]{1,0:T(8,128)(2,1)S(1)} %get-tuple-element.49), channel_id=1, source_target_pairs={{0,1},{1,0},{2,3},{3,2},{4,5},{5,4},{6,7},{7,6},{8,9},{9,8},{10,11... | collective-permute-start | bytes 159752 | tf_op jit(solution)/shard_map/ppermute | solution.py:20
  16.8 2.5 %collective-permute-done.4.earlier_ref.later_ref = bf16[208,128]{1,0:T(8,128)(2,1)S(1)} collective-permute-done((bf16[208,128]{1,0:T(8,128)(2,1)S(1)}, bf16[208,128]{1,0:T(8,128)(2,1)S(1)}, u32[]{:S(2)}, u32[]{:S(2)}) %collective-permute-start.4) | collective-permute-done | bytes 53280 | tf_op jit(solution)/shard_map/ppermute | solution.py:20
  19.4 3.7 %shard_map.87 = (f32[2,16,32,128]{3,2,1,0:T(8,128)S(1)}, bf16[128,512]{1,0:T(8,128)(2,1)S(1)}, bf16[128,512]{1,0:T(8,128)(2,1)S(1)}, f32[2,22,40,128]{3,2,1,0:T(8,128)}) custom-call(f32[3,22,40,128]{3,2,1,0:T(8,128)S(1)} %get-tuple-element.48.whole, bf16[208,128]{1,0:T(8,128)(2,1)S(1)} %collective-permute-done.4.earlier_ref.later_ref, ...), custom_call_target="tpu_custom_call" | custom-call | flops 2147483648 | tf_op jit(solution)/shard_map/pallas_call | solution.py:509
  23.1 1.5 %collective-permute-start.7 = (bf16[128,512]{1,0:T(8,128)(2,1)S(1)}, bf16[128,512]{1,0:T(8,128)(2,1)S(1)}, u32[]{:S(2)}, u32[]{:S(2)}) collective-permute-start(bf16[128,512]{1,0:T(8,128)(2,1)S(1)} %get-tuple-element.54.inputs_ref.own_ref), channel_id=1, source_target_pairs={{0,1},{1,0},{2,3},{3,2},{4,5},{5,4},{6,7},{7,6},{8,9},{9,8},{10,11... | collective-permute-start | bytes 393224 | tf_op jit(solution)/shard_map/ppermute | solution.py:371
  26.7 1.5 %shard_map.89.third = f32[16,32,128]{2,1,0:T(8,128)S(1)} custom-call(bf16[128,512]{1,0:T(8,128)(2,1)S(1)} %get-tuple-element.54.inputs_ref.own_ref, bf16[512,1024]{1,0:T(8,128)(2,1)S(1)} %copy-done.1, bf16[1024,1024]{1,0:T(8,128)(2,1)S(1)} %copy-done, bf16[1024,512]{1,0:T(8,128)(2,1)S(1)} %shard_map.88.last_ref), custom_call_target="tpu_custom_call" | custom-call | flops 1073741824 | tf_op jit(solution)/shard_map/pallas_call | solution.py:509
  28.3 1.7 %collective-permute-start.6 = (bf16[10,32,128]{2,1,0:T(8,128)(2,1)S(1)}, bf16[10,32,128]{2,1,0:T(8,128)(2,1)S(1)}, u32[]{:S(2)}, u32[]{:S(2)}) collective-permute-start(bf16[10,32,128]{2,1,0:T(8,128)(2,1)S(1)} %get-tuple-element.53), channel_id=1, source_target_pairs={{0,24},{8,0},{16,8},{24,16},{1,25},{9,1},{17,9},{25,17},{2,26},{10... | collective-permute-start | bytes 245768 | tf_op jit(solution)/shard_map/ppermute | solution.py:20
  30.1 1.4 %collective-permute-start.11 = (bf16[128,512]{1,0:T(8,128)(2,1)S(1)}, bf16[128,512]{1,0:T(8,128)(2,1)S(1)}, u32[]{:S(2)}, u32[]{:S(2)}) collective-permute-start(bf16[128,512]{1,0:T(8,128)(2,1)S(1)} %get-tuple-element.61.own_ref), channel_id=1, source_target_pairs={{0,1},{1,0},{2,3},{3,2},{4,5},{5,4},{6,7},{7,6},{8,9},{9,8},{10,11... | collective-permute-start | bytes 393224 | tf_op jit(solution)/shard_map/ppermute | solution.py:371
  33.6 3.6 %shard_map.91 = (bf16[512,512]{1,0:T(8,128)(2,1)S(1)}, bf16[512,1024]{1,0:T(8,128)(2,1)S(1)}, f32[512,1024]{1,0:T(8,128)S(1)}, bf16[512,1024]{1,0:T(8,128)(2,1)S(1)}, f32[512,1024]{1,0:T(8,128)S(1)}) custom-call(bf16[128,512]{1,0:T(8,128)(2,1)S(1)} %get-tuple-element.54.inputs_ref.own_ref, bf16[128,512]{1,0:T(8,128)(2,1)S(1)} %collective-permute-done.7.a_ref, ...), custom_call_target="tpu_custom_call" | custom-call | flops 4294967296 | tf_op jit(solution)/shard_map/pallas_call | solution.py:509
  37.6 1.7 %collective-permute-done.13.c_ref = bf16[128,512]{1,0:T(8,128)(2,1)S(1)} collective-permute-done((bf16[128,512]{1,0:T(8,128)(2,1)S(1)}, bf16[128,512]{1,0:T(8,128)(2,1)S(1)}, u32[]{:S(2)}, u32[]{:S(2)}) %collective-permute-start.13) | collective-permute-done | bytes 131104 | tf_op jit(solution)/shard_map/ppermute | solution.py:371
  39.3 1.2 %shard_map.93 = (bf16[512,512]{1,0:T(8,128)(2,1)S(1)}, f32[128,512]{1,0:T(8,128)S(1)}, f32[128,512]{1,0:T(8,128)S(1)}) custom-call(bf16[512,1024]{1,0:T(8,128)(2,1)S(1)} %get-tuple-element.59.h2_ref, bf16[128,512]{1,0:T(8,128)(2,1)S(1)} %get-tuple-element.61.own_ref, bf16[128,512]{1,0:T(8,128)(2,1)S(1)} %collective-permute-done.11.a_ref, ...), custom_call_target="tpu_custom_call" | custom-call | flops 4294967296 | tf_op jit(solution)/shard_map/pallas_call | solution.py:509
  40.6 1.4 %shard_map.94 = (bf16[512,1024]{1,0:T(8,128)(2,1)S(1)}, f32[128,1024]{1,0:T(8,128)S(1)}, f32[128,1024]{1,0:T(8,128)S(1)}) custom-call(bf16[512,512]{1,0:T(8,128)(2,1)S(1)} %get-tuple-element.62.carried_ref, bf16[1024,512]{1,0:T(8,128)(2,1)S(1)} %copy-done.2, f32[512,1024]{1,0:T(8,128)S(1)} %get-tuple-element.63.slope_ref, ...), custom_call_target="tpu_custom_call" | custom-call | flops 2147483648 | tf_op jit(solution)/shard_map/pallas_call | solution.py:509
  44.5 3.0 %collective-permute-start.16 = (bf16[224,128]{1,0:T(8,128)(2,1)S(1)}, bf16[224,128]{1,0:T(8,128)(2,1)S(1)}, u32[]{:S(2)}, u32[]{:S(2)}) collective-permute-start(bf16[224,128]{1,0:T(8,128)(2,1)S(1)} %get-tuple-element.58), channel_id=1, source_target_pairs={{0,6},{2,0},{4,2},{6,4},{1,7},{3,1},{5,3},{7,5},{8,14},{10,8},{12,... | collective-permute-start | bytes 172040 | tf_op jit(solution)/shard_map/ppermute | solution.py:20
  48.1 2.1 %collective-permute-start.24 = (f32[32,512]{1,0:T(8,128)S(1)}, f32[32,512]{1,0:T(8,128)S(1)}, u32[]{:S(2)}, u32[]{:S(2)}) collective-permute-start(f32[32,512]{1,0:T(8,128)S(1)} %slice_add_fusion.11), channel_id=1, source_target_pairs={{0,4},{1,5},{2,6},{3,7},{4,0},{5,1},{6,2},{7,3},{8,12},{9,13},{10,... | collective-permute-start | bytes 196616 | tf_op jit(solution)/shard_map/ppermute | solution.py:371
  51.8 2.3 %shard_map.96 = (bf16[512,1024]{1,0:T(8,128)(2,1)}, f32[64,1024]{1,0:T(8,128)S(1)}, f32[64,1024]{1,0:T(8,128)S(1)}) custom-call(bf16[512,1024]{1,0:T(8,128)(2,1)S(1)} %get-tuple-element.73.carried_ref, bf16[1024,1024]{1,0:T(8,128)(2,1)S(1)} %copy-done, f32[512,1024]{1,0:T(8,128)S(1)} %get-tuple-element.74.slope_ref, ...), custom_call_target="tpu_custom_call" | custom-call | flops 2147483648 | tf_op jit(solution)/shard_map/pallas_call | solution.py:509
  55.8 1.6 %collective-permute-done.18 = f32[64,1024]{1,0:T(8,128)S(1)} collective-permute-done((f32[64,1024]{1,0:T(8,128)S(1)}, f32[64,1024]{1,0:T(8,128)S(1)}, u32[]{:S(2)}, u32[]{:S(2)}) %collective-permute-start.18) | collective-permute-done | bytes 262176 | tf_op jit(solution)/shard_map/ppermute | solution.py:371
  59.4 3.7 %shard_map.97 = f32[2,16,32,128]{3,2,1,0:T(8,128)} custom-call(f32[3,22,40,128]{3,2,1,0:T(8,128)S(1)} %get-tuple-element.78.whole, bf16[208,128]{1,0:T(8,128)(2,1)S(1)} %collective-permute-done.20.earlier_ref.later_ref, bf16[208,128]{1,0:T(8,128)(2,1)S(1)} %collective-permute-done.20.earlier_ref.later_ref, f32[2,22,40,128]{3,2,1,0:T(8,128)S(1)} %copy-done.3), custom_call_target="tpu_custom_call" | custom-call | flops 4294967296 | tf_op jit(solution)/shard_map/pallas_call | solution.py:509
  63.5 2.1 %collective-permute-start.22 = (f32[16,1024]{1,0:T(8,128)S(1)}, f32[16,1024]{1,0:T(8,128)S(1)}, u32[]{:S(2)}, u32[]{:S(2)}) collective-permute-start(f32[16,1024]{1,0:T(8,128)S(1)} %slice_add_fusion.9), channel_id=1, source_target_pairs={{0,4},{1,5},{2,6},{3,7},{4,0},{5,1},{6,2},{7,3},{8,12},{9,13},{10,... | collective-permute-start | bytes 196616 | tf_op jit(solution)/shard_map/ppermute | solution.py:371
  66.3 3.1 %collective-permute-done.22 = f32[16,1024]{1,0:T(8,128)S(1)} collective-permute-done((f32[16,1024]{1,0:T(8,128)S(1)}, f32[16,1024]{1,0:T(8,128)S(1)}, u32[]{:S(2)}, u32[]{:S(2)}) %collective-permute-start.22) | collective-permute-done | bytes 65568 | tf_op jit(solution)/shard_map/ppermute | solution.py:371
  (59 shorter events, 19.0 us)
Async XLA Ops:
  1.8 4.6 %collective-permute-start = (bf16[10,32,128]{2,1,0:T(8,128)(2,1)S(1)}, bf16[10,32,128]{2,1,0:T(8,128)(2,1)S(1)}, u32[]{:S(2)}, u32[]{:S(2)}) collective-permute-start(bf16[10,32,128]{2,1,0:T(8,128)(2,1)S(1)} %get-tuple-element.44), channel_id=1, source_target_pairs={{0,8},{8,16},{16,24},{24,0},{1,9},{9,17},{17,25},{25,1},{2,10},{10... | collective-permute-start | bytes 245768 | tf_op jit(solution)/shard_map/ppermute | solution.py:20
  2.3 4.7 %collective-permute-start.1 = (bf16[10,32,128]{2,1,0:T(8,128)(2,1)S(1)}, bf16[10,32,128]{2,1,0:T(8,128)(2,1)S(1)}, u32[]{:S(2)}, u32[]{:S(2)}) collective-permute-start(bf16[10,32,128]{2,1,0:T(8,128)(2,1)S(1)} %get-tuple-element.45), channel_id=1, source_target_pairs={{0,24},{8,0},{16,8},{24,16},{1,25},{9,1},{17,9},{25,17},{2,26},{10... | collective-permute-start | bytes 245768 | tf_op jit(solution)/shard_map/ppermute | solution.py:20
  7.1 6.1 %collective-permute-start.2 = (bf16[224,128]{1,0:T(8,128)(2,1)S(1)}, bf16[224,128]{1,0:T(8,128)(2,1)S(1)}, u32[]{:S(2)}, u32[]{:S(2)}) collective-permute-start(bf16[224,128]{1,0:T(8,128)(2,1)S(1)} %get-tuple-element.46), channel_id=1, source_target_pairs={{0,2},{2,4},{4,6},{6,0},{1,3},{3,5},{5,7},{7,1},{8,10},{10,12},{12... | collective-permute-start | bytes 172040 | tf_op jit(solution)/shard_map/ppermute | solution.py:20
  8.9 5.8 %collective-permute-start.3 = (bf16[224,128]{1,0:T(8,128)(2,1)S(1)}, bf16[224,128]{1,0:T(8,128)(2,1)S(1)}, u32[]{:S(2)}, u32[]{:S(2)}) collective-permute-start(bf16[224,128]{1,0:T(8,128)(2,1)S(1)} %get-tuple-element.47), channel_id=1, source_target_pairs={{0,6},{2,0},{4,2},{6,4},{1,7},{3,1},{5,3},{7,5},{8,14},{10,8},{12,... | collective-permute-start | bytes 172040 | tf_op jit(solution)/shard_map/ppermute | solution.py:20
  15.2 4.2 %collective-permute-start.4 = (bf16[208,128]{1,0:T(8,128)(2,1)S(1)}, bf16[208,128]{1,0:T(8,128)(2,1)S(1)}, u32[]{:S(2)}, u32[]{:S(2)}) collective-permute-start(bf16[208,128]{1,0:T(8,128)(2,1)S(1)} %get-tuple-element.49), channel_id=1, source_target_pairs={{0,1},{1,0},{2,3},{3,2},{4,5},{5,4},{6,7},{7,6},{8,9},{9,8},{10,11... | collective-permute-start | bytes 159752 | tf_op jit(solution)/shard_map/ppermute | solution.py:20
  23.1 6.9 %collective-permute-start.7 = (bf16[128,512]{1,0:T(8,128)(2,1)S(1)}, bf16[128,512]{1,0:T(8,128)(2,1)S(1)}, u32[]{:S(2)}, u32[]{:S(2)}) collective-permute-start(bf16[128,512]{1,0:T(8,128)(2,1)S(1)} %get-tuple-element.54.inputs_ref.own_ref), channel_id=1, source_target_pairs={{0,1},{1,0},{2,3},{3,2},{4,5},{5,4},{6,7},{7,6},{8,9},{9,8},{10,11... | collective-permute-start | bytes 393224 | tf_op jit(solution)/shard_map/ppermute | solution.py:371
  24.6 6.9 %collective-permute-start.8 = (bf16[128,512]{1,0:T(8,128)(2,1)S(1)}, bf16[128,512]{1,0:T(8,128)(2,1)S(1)}, u32[]{:S(2)}, u32[]{:S(2)}) collective-permute-start(bf16[128,512]{1,0:T(8,128)(2,1)S(1)} %get-tuple-element.54.inputs_ref.own_ref), channel_id=1, source_target_pairs={{0,2},{1,3},{2,0},{3,1},{4,6},{5,7},{6,4},{7,5},{8,10},{9,11},{10,... | collective-permute-start | bytes 393224 | tf_op jit(solution)/shard_map/ppermute | solution.py:371
  25.8 6.9 %collective-permute-start.9 = (bf16[128,512]{1,0:T(8,128)(2,1)S(1)}, bf16[128,512]{1,0:T(8,128)(2,1)S(1)}, u32[]{:S(2)}, u32[]{:S(2)}) collective-permute-start(bf16[128,512]{1,0:T(8,128)(2,1)S(1)} %get-tuple-element.54.inputs_ref.own_ref), channel_id=1, source_target_pairs={{0,3},{1,2},{2,1},{3,0},{4,7},{5,6},{6,5},{7,4},{8,11},{9,10},{10,... | collective-permute-start | bytes 393224 | tf_op jit(solution)/shard_map/ppermute | solution.py:371
  28.3 8.9 %collective-permute-start.5 = (bf16[10,32,128]{2,1,0:T(8,128)(2,1)S(1)}, bf16[10,32,128]{2,1,0:T(8,128)(2,1)S(1)}, u32[]{:S(2)}, u32[]{:S(2)}) collective-permute-start(bf16[10,32,128]{2,1,0:T(8,128)(2,1)S(1)} %get-tuple-element.52), channel_id=1, source_target_pairs={{0,8},{8,16},{16,24},{24,0},{1,9},{9,17},{17,25},{25,1},{2,10},{10... | collective-permute-start | bytes 245768 | tf_op jit(solution)/shard_map/ppermute | solution.py:20
  28.3 8.9 %collective-permute-start.6 = (bf16[10,32,128]{2,1,0:T(8,128)(2,1)S(1)}, bf16[10,32,128]{2,1,0:T(8,128)(2,1)S(1)}, u32[]{:S(2)}, u32[]{:S(2)}) collective-permute-start(bf16[10,32,128]{2,1,0:T(8,128)(2,1)S(1)} %get-tuple-element.53), channel_id=1, source_target_pairs={{0,24},{8,0},{16,8},{24,16},{1,25},{9,1},{17,9},{25,17},{2,26},{10... | collective-permute-start | bytes 245768 | tf_op jit(solution)/shard_map/ppermute | solution.py:20
  30.1 7.3 %collective-permute-start.11 = (bf16[128,512]{1,0:T(8,128)(2,1)S(1)}, bf16[128,512]{1,0:T(8,128)(2,1)S(1)}, u32[]{:S(2)}, u32[]{:S(2)}) collective-permute-start(bf16[128,512]{1,0:T(8,128)(2,1)S(1)} %get-tuple-element.61.own_ref), channel_id=1, source_target_pairs={{0,1},{1,0},{2,3},{3,2},{4,5},{5,4},{6,7},{7,6},{8,9},{9,8},{10,11... | collective-permute-start | bytes 393224 | tf_op jit(solution)/shard_map/ppermute | solution.py:371
  31.5 6.2 %collective-permute-start.12 = (bf16[128,512]{1,0:T(8,128)(2,1)S(1)}, bf16[128,512]{1,0:T(8,128)(2,1)S(1)}, u32[]{:S(2)}, u32[]{:S(2)}) collective-permute-start(bf16[128,512]{1,0:T(8,128)(2,1)S(1)} %get-tuple-element.61.own_ref), channel_id=1, source_target_pairs={{0,2},{1,3},{2,0},{3,1},{4,6},{5,7},{6,4},{7,5},{8,10},{9,11},{10,... | collective-permute-start | bytes 393224 | tf_op jit(solution)/shard_map/ppermute | solution.py:371
  32.6 6.7 %collective-permute-start.13 = (bf16[128,512]{1,0:T(8,128)(2,1)S(1)}, bf16[128,512]{1,0:T(8,128)(2,1)S(1)}, u32[]{:S(2)}, u32[]{:S(2)}) collective-permute-start(bf16[128,512]{1,0:T(8,128)(2,1)S(1)} %get-tuple-element.61.own_ref), channel_id=1, source_target_pairs={{0,3},{1,2},{2,1},{3,0},{4,7},{5,6},{6,5},{7,4},{8,11},{9,10},{10,... | collective-permute-start | bytes 393224 | tf_op jit(solution)/shard_map/ppermute | solution.py:371
  42.0 8.2 %collective-permute-start.15 = (f32[128,1024]{1,0:T(8,128)S(1)}, f32[128,1024]{1,0:T(8,128)S(1)}, u32[]{:S(2)}, u32[]{:S(2)}) collective-permute-start(f32[128,1024]{1,0:T(8,128)S(1)} %get-tuple-element.69), channel_id=1, source_target_pairs={{0,8},{1,9},{2,10},{3,11},{4,12},{5,13},{6,14},{7,15},{8,0},{9,1},... | collective-permute-start | bytes 1572872 | tf_op jit(solution)/shard_map/ppermute | solution.py:371
  42.6 5.5 %collective-permute-start.19 = (f32[64,512]{1,0:T(8,128)S(1)}, f32[64,512]{1,0:T(8,128)S(1)}, u32[]{:S(2)}, u32[]{:S(2)}) collective-permute-start(f32[64,512]{1,0:T(8,128)S(1)} %get-tuple-element.85), channel_id=1, source_target_pairs={{0,16},{1,17},{2,18},{3,19},{4,20},{5,21},{6,22},{7,23},{8,24},{9,... | collective-permute-start | bytes 393224 | tf_op jit(solution)/shard_map/ppermute | solution.py:371
  43.6 7.8 %collective-permute-start.10 = (bf16[224,128]{1,0:T(8,128)(2,1)S(1)}, bf16[224,128]{1,0:T(8,128)(2,1)S(1)}, u32[]{:S(2)}, u32[]{:S(2)}) collective-permute-start(bf16[224,128]{1,0:T(8,128)(2,1)S(1)} %get-tuple-element.57), channel_id=1, source_target_pairs={{0,2},{2,4},{4,6},{6,0},{1,3},{3,5},{5,7},{7,1},{8,10},{10,12},{12... | collective-permute-start | bytes 172040 | tf_op jit(solution)/shard_map/ppermute | solution.py:20
  44.5 6.8 %collective-permute-start.16 = (bf16[224,128]{1,0:T(8,128)(2,1)S(1)}, bf16[224,128]{1,0:T(8,128)(2,1)S(1)}, u32[]{:S(2)}, u32[]{:S(2)}) collective-permute-start(bf16[224,128]{1,0:T(8,128)(2,1)S(1)} %get-tuple-element.58), channel_id=1, source_target_pairs={{0,6},{2,0},{4,2},{6,4},{1,7},{3,1},{5,3},{7,5},{8,14},{10,8},{12,... | collective-permute-start | bytes 172040 | tf_op jit(solution)/shard_map/ppermute | solution.py:20
  48.1 6.1 %collective-permute-start.24 = (f32[32,512]{1,0:T(8,128)S(1)}, f32[32,512]{1,0:T(8,128)S(1)}, u32[]{:S(2)}, u32[]{:S(2)}) collective-permute-start(f32[32,512]{1,0:T(8,128)S(1)} %slice_add_fusion.11), channel_id=1, source_target_pairs={{0,4},{1,5},{2,6},{3,7},{4,0},{5,1},{6,2},{7,3},{8,12},{9,13},{10,... | collective-permute-start | bytes 196616 | tf_op jit(solution)/shard_map/ppermute | solution.py:371
  50.3 7.2 %collective-permute-start.18 = (f32[64,1024]{1,0:T(8,128)S(1)}, f32[64,1024]{1,0:T(8,128)S(1)}, u32[]{:S(2)}, u32[]{:S(2)}) collective-permute-start(f32[64,1024]{1,0:T(8,128)S(1)} %get-tuple-element.81), channel_id=1, source_target_pairs={{0,16},{1,17},{2,18},{3,19},{4,20},{5,21},{6,22},{7,23},{8,24},{9,... | collective-permute-start | bytes 786440 | tf_op jit(solution)/shard_map/ppermute | solution.py:371
  54.1 4.3 %collective-permute-start.17 = (f32[64,1024]{1,0:T(8,128)S(1)}, f32[64,1024]{1,0:T(8,128)S(1)}, u32[]{:S(2)}, u32[]{:S(2)}) collective-permute-start(f32[64,1024]{1,0:T(8,128)S(1)} %get-tuple-element.77), channel_id=1, source_target_pairs={{0,8},{1,9},{2,10},{3,11},{4,12},{5,13},{6,14},{7,15},{8,0},{9,1},... | collective-permute-start | bytes 786440 | tf_op jit(solution)/shard_map/ppermute | solution.py:371
  54.8 4.6 %collective-permute-start.20 = (bf16[208,128]{1,0:T(8,128)(2,1)S(1)}, bf16[208,128]{1,0:T(8,128)(2,1)S(1)}, u32[]{:S(2)}, u32[]{:S(2)}) collective-permute-start(bf16[208,128]{1,0:T(8,128)(2,1)S(1)} %get-tuple-element.72), channel_id=1, source_target_pairs={{0,1},{1,0},{2,3},{3,2},{4,5},{5,4},{6,7},{7,6},{8,9},{9,8},{10,11... | collective-permute-start | bytes 159752 | tf_op jit(solution)/shard_map/ppermute | solution.py:20
  57.4 8.1 %collective-permute-start.23 = (f32[32,1024]{1,0:T(8,128)S(1)}, f32[32,1024]{1,0:T(8,128)S(1)}, u32[]{:S(2)}, u32[]{:S(2)}) collective-permute-start(f32[32,1024]{1,0:T(8,128)S(1)} %slice_add_fusion.5), channel_id=1, source_target_pairs={{0,4},{1,5},{2,6},{3,7},{4,0},{5,1},{6,2},{7,3},{8,12},{9,13},{10,... | collective-permute-start | bytes 393224 | tf_op jit(solution)/shard_map/ppermute | solution.py:371
  58.4 5.0 %collective-permute-start.21 = (f32[32,1024]{1,0:T(8,128)S(1)}, f32[32,1024]{1,0:T(8,128)S(1)}, u32[]{:S(2)}, u32[]{:S(2)}) collective-permute-start(f32[32,1024]{1,0:T(8,128)S(1)} %get-tuple-element.83), channel_id=1, source_target_pairs={{0,16},{1,17},{2,18},{3,19},{4,20},{5,21},{6,22},{7,23},{8,24},{9,... | collective-permute-start | bytes 393224 | tf_op jit(solution)/shard_map/ppermute | solution.py:371
  63.5 5.9 %collective-permute-start.22 = (f32[16,1024]{1,0:T(8,128)S(1)}, f32[16,1024]{1,0:T(8,128)S(1)}, u32[]{:S(2)}, u32[]{:S(2)}) collective-permute-start(f32[16,1024]{1,0:T(8,128)S(1)} %slice_add_fusion.9), channel_id=1, source_target_pairs={{0,4},{1,5},{2,6},{3,7},{4,0},{5,1},{6,2},{7,3},{8,12},{9,13},{10,... | collective-permute-start | bytes 196616 | tf_op jit(solution)/shard_map/ppermute | solution.py:371
  (5 other events, 26.3 us)

commit v4 on v3

--- a/solution.py
+++ b/solution.py
@@ -155,7 +155,7 @@
         target[plane, first:first + rows, :] = value
 
 
-def one_step(source, target, fixed, planes, rows, sides):
+def one_step(source, target, fixed, planes, rows, sides, finished=None):
     def some_rows(plane, first):
         held, here = (slice(8 + first, 16 + first), slice(first, first + 8))
         around, centers = ([], [])
@@ -179,22 +179,21 @@
             for pair, value in zip(target, new):
                 pair[n][plane, held, :] = value
 
-    def one_plane(plane, carry):
+    for plane in range(*planes):
         for first in range(0, rows, 8):
             some_rows(plane, first)
-        return carry
-
-    lax.fori_loop(planes[0], planes[1], one_plane, 0, unroll=True)
-
-
-def run_steps(whole, earlier, later, fixed, now, then):
+        if finished is not None:
+            finished(plane, target)
+
+
+def run_steps(whole, earlier, later, fixed, now, then, finished=None):
     planes, rows = whole.shape[1:3]
     for kind, pair in enumerate(now):
         load_sides(whole, earlier, later, kind, pair[1], 8)
         for plane in range(planes):
             pair[0][plane, 8:8 + rows, :] = whole[kind, plane]
     for step in range(HALO):
-        one_step(now, then, fixed, (step + 1, planes - step - 1), rows, step < HALO - 1)
+        one_step(now, then, fixed, (step + 1, planes - step - 1), rows, step < HALO - 1, finished if step == HALO - 1 else None)
         now, then = then, now
     return now[0][0], now[1][0]
 
@@ -269,11 +268,12 @@
         copy.wait()
 
 
-def own_forward_body(edge, inputs_ref, first_ref, middle_ref, last_ref, field_ref):
+def own_forward_body(edge, scale, inputs_ref, targets_ref, first_ref, middle_ref, last_ref, field_ref, error_ref):
     length, height, width = field_ref.shape
     h1 = gelu_value(product(inputs_ref[...], first_ref[...])).astype(jnp.bfloat16)
     h2 = gelu_value(product(h1, middle_ref[...])).astype(jnp.bfloat16)
     forcing = product(h2, last_ref[...])
+    error_ref[...] = ((forcing - targets_ref[...].astype(jnp.float32)) * scale).astype(jnp.bfloat16)
     cells = lax.broadcasted_iota(jnp.int32, (edge ** 3, edge ** 3), 1)
     row = lax.broadcasted_iota(jnp.int32, (edge ** 3, edge ** 3), 0)
     square = edge * edge
@@ -286,16 +286,27 @@
 
 
 def last_steps_body(whole, earlier_ref, later_ref, fixed, state_ref, *scratch):
-    *fields_now, side, earlier, later = scratch
+    *fields_now, side, earlier, later, near, semaphores = scratch
     length, height, _ = state_ref.shape[1:]
+    group = length // semaphores.shape[0]
+    copies = []
+
+    def finished(plane, pairs):
+        x = plane - HALO
+        for species, pair in enumerate(pairs):
+            near[species, x] = pair[0][plane, 8 + EDGE:8 + EDGE + height, :]
+        if (x + 1) % group == 0:
+            held = slice(x + 1 - group, x + 1)
+            copies.append(pltpu.make_async_copy(near.at[:, held], state_ref.at[:, held], semaphores.at[x // group]))
+            copies[-1].start()
+
     earlier[...] = earlier_ref[...].astype(jnp.float32)
     later[...] = later_ref[...].astype(jnp.float32)
     load_sides(whole, earlier, later, 2, side, 0)
     both = [(fixed.at[0], fixed.at[1]), (whole.at[2], side)]
-    now = run_steps(whole, earlier, later, both, *paired(fields_now))
-    for species, field in enumerate(now):
-        for x in range(length):
-            state_ref[species, x] = field[x + HALO, 8 + EDGE:8 + EDGE + height, :]
+    run_steps(whole, earlier, later, both, *paired(fields_now), finished)
+    for copy in copies:
+        copy.wait()
 
 
 def start_copies(pairs, semaphores):
@@ -305,8 +316,10 @@
     return copies
 
 
-def bring_body(far_ref, near_ref, semaphores):
-    start_copies([(far_ref, near_ref)], semaphores)[0].wait()
+def bring_body(*refs):
+    count = len(refs) // 2
+    for copy in start_copies(zip(refs[:count], refs[count:-1]), refs[-1]):
+        copy.wait()
 
 
 def store_faces(state, third, leading_ref, trailing_ref):
@@ -321,10 +334,20 @@
                     out_ref[LAYERS + kind] = (value - rounded(value)).astype(jnp.bfloat16)
 
 
-def first_faces_body(state_ref, third_ref, leading_ref, trailing_ref, state_out, third_out, semaphores):
-    for copy in start_copies(((state_ref, state_out), (third_ref, third_out)), semaphores):
+def first_faces_body(state_ref, third_ref, leading_ref, trailing_ref, low, high, low_third, high_third, semaphores):
+    length = third_ref.shape[0]
+    for copy in start_copies((
+        (state_ref.at[:, :HALO], low), (state_ref.at[:, length - HALO:], high),
+        (third_ref.at[:HALO - 1], low_third), (third_ref.at[length - HALO + 1:], high_third),
+    ), semaphores):
         copy.wait()
-    store_faces(state_out, third_out, leading_ref, trailing_ref)
+    for kind, depth in enumerate((HALO, HALO, HALO - 1)):
+        for out_ref, near, third, nearest in ((leading_ref, low, low_third, 0), (trailing_ref, high, high_third, depth - 1)):
+            for plane in range(depth):
+                value = near[kind, plane] if kind < 2 else third[plane]
+                out_ref[kind * HALO + plane] = value.astype(jnp.bfloat16)
+                if kind < 2 and plane == nearest:
+                    out_ref[LAYERS + kind] = (value - rounded(value)).astype(jnp.bfloat16)
 
 
 def x_halos(leading, trailing):
@@ -420,8 +443,8 @@
     square = values * values
     bend = jnp.tanh(values * (root + (root * 0.044715) * square))
     cdf = 0.5 + 0.5 * bend
-    slope = cdf + (0.5 * values) * (1.0 - bend * bend) * (root + (3.0 * root * 0.044715) * square)
-    return values * cdf, slope
+    value = values * cdf
+    return value, cdf + (value - value * cdf) * (2.0 * root + (6.0 * root * 0.044715) * square)
 
 
 def gelu_value(values):
@@ -475,16 +498,11 @@
     activated(h1_ref[...], middle_ref, h2_ref, s2_ref)
 
 
-def forward_two_body(scale, h2_ref, own_ref, a_ref, b_ref, c_ref, last_ref, rows_ref, error_ref, leaving_ref, staying_ref):
+def forward_two_body(h2_ref, own_ref, a_ref, b_ref, c_ref, rows_ref, error_ref, leaving_ref, staying_ref):
     count = own_ref.shape[0]
-    h2 = h2_ref[...]
-    for columns in column_tiles(error_ref.shape[1]):
-        forcing = product(h2, last_ref[:, columns])
-        for number, part in enumerate((own_ref, a_ref, b_ref, c_ref)):
-            block = slice(number * count, (number + 1) * count)
-            target = part[:, columns].astype(jnp.float32)
-            error_ref[block, columns] = ((forcing[block] - target) * scale).astype(jnp.bfloat16)
-    chosen = transposed_choice(rows_ref[...], h2)
+    for number, part in enumerate((own_ref, a_ref, b_ref, c_ref)):
+        error_ref[number * count:(number + 1) * count, :] = part[...]
+    chosen = transposed_choice(rows_ref[...], h2_ref[...])
     for columns in column_tiles(error_ref.shape[1]):
         store_halves(product(chosen, error_ref[:, columns]), columns, leaving_ref, staying_ref)
 
@@ -541,12 +559,15 @@
     big = 1 << 32
 
     layers = ((PACKED, height, width), bf16)
-    leading, trailing, near_state, near_third = kernel_call(
-        first_faces_body, [layers, layers, (concentrations.shape, f32), (diffusivity.shape, f32)],
-        far=(0, 1), copies=2,
+    face, face_third = (((2, HALO, height, width), f32), ((HALO - 1, height, width), f32))
+    leading, trailing = kernel_call(
+        first_faces_body, [layers, layers], scratch=[face, face, face_third, face_third], far=(0, 1), copies=4
     )(concentrations, diffusivity)
     before, after = x_halos(leading, trailing)
-    (near_last,) = kernel_call(bring_body, [(weight_last.shape, bf16)], far=(0,), copies=1)(weight_last)
+    brought = (concentrations, diffusivity, weight_last)
+    near_state, near_third, near_last = kernel_call(
+        bring_body, [(array.shape, array.dtype) for array in brought], far=(0, 1, 2), copies=3
+    )(*brought)
     leading, trailing = edge_rows(near_state, near_third, before, after)
     below, above = y_halos(leading, trailing)
     whole, strips = assemble(near_state, near_third, before, after, below, above)
@@ -559,12 +580,13 @@
 
     gather = lambda array: [exchange(array, mesh_sizes, flips) for flips in ((0, 0, 1), (0, 1, 0), (0, 1, 1))]
     all_inputs = gather(inputs)
-    (field,) = kernel_call(functools.partial(own_forward_body, PATCH), [(diffusivity.shape, f32)],
+    field, own_error = kernel_call(
+        functools.partial(own_forward_body, PATCH, 1.0 / count), [(diffusivity.shape, f32), ((count, cells), bf16)],
         flops=big // 4,
     )(
-        inputs, weight_first, weight_middle, near_last
+        inputs, targets, weight_first, weight_middle, near_last
     )
-    all_targets = gather(tied(targets, field))
+    all_errors = gather(own_error)
     leading, trailing = kernel_call(store_faces, [layers, layers])(state, field)
     before, after = x_halos(leading, trailing)
     x, h1, s1, h2, s2 = kernel_call(
@@ -576,10 +598,8 @@
     leading, trailing = edge_rows(state, field, tied(before, h2), after)
     below, above = y_halos(leading, trailing)
     error, *last = kernel_call(
-        functools.partial(forward_two_body, 1.0 / count),
-        [((total, cells), bf16), half_of(rows_last, cells), half_of(rows_last, cells)],
-        flops=big,
-    )(tied(h2, leading, trailing), targets, *all_targets, weight_last, rows_last)
+        forward_two_body, [((total, cells), bf16), half_of(rows_last, cells), half_of(rows_last, cells)], flops=big
+    )(tied(h2, leading, trailing), own_error, *all_errors, rows_last)
     last = halved(*last, stages[0], mesh_sizes)
     back_second, *middle = kernel_call(
         backward_body,
@@ -597,7 +617,8 @@
     )(tied(back_second, strips), weight_middle, s1, x, rows_first)
     first = halved(*first, stages[0], mesh_sizes)
     middle = halved(*middle, stages[1], mesh_sizes)
-    (state,) = kernel_call(last_steps_body, [(state.shape, f32)], scratch=buffers, flops=big)(
+    (state,) = kernel_call(last_steps_body, [(state.shape, f32)], scratch=buffers + [(state.shape, f32)],
+                           flops=big, far_outputs=(0,), copies=4 if length % 4 == 0 else 1)(
         tied(whole, first[0], middle[0], last[0]), *z_strips(strips), diffusivity_fixed
     )
     grads = [rest_halved(*part, stages, done, mesh_sizes) for part, done in ((first, 1), (middle, 2), (last, 2))]

time: 70.2 us -> 68.8 us (0.980)
  Pallas kernels: 20.9 us -> 20.1 us
    pallas_call x14, Pallas kernels: 20.9 us -> 20.1 us  [call(): pl.pallas_call(body, cost_estimate=pl.CostEstimate(flops=flops, transcend...]
  transfers between devices with their start and end apart: 25 -> 25, of which waited for: 11 -> 11; matrix products, arithmetic and copies ran while one was open for 3% -> 3% of each run, Pallas kernels for 20% -> 21%
where the time goes in v4:
time: 68.8 us; the launch traced here: 68.7 us
  starting transfers between devices  30.4 us (44%)
  Pallas kernels  20.1 us (29%)
  waiting for transfers between devices  14.9 us (22%)
  other arithmetic  2.42 us (4%)
  between operations  0.84 us (1%)
    pallas_call x14, Pallas kernels, call(): pl.pallas_call(body, cost_estimate=pl.CostEstimate(flops=flops, transcend...  20.1 us
    ppermute x15, starting transfers between devices, exchange(): return lax.ppermute(array, ('gx', 'gy', 'row'), route)  15.7 us
    ppermute x10, starting transfers between devices, ring(): lax.ppermute(array, axis, [(i, (i + distance) % size) for i in range(size)])  14.7 us
    ppermute x10, waiting for transfers between devices, ring(): lax.ppermute(array, axis, [(i, (i + distance) % size) for i in range(size)])  7.5 us
    ppermute x15, waiting for transfers between devices, exchange(): return lax.ppermute(array, ('gx', 'gy', 'row'), route)  7.43 us
    add x3, other arithmetic, rest_halved(): return staying + arrived  1.97 us
  transfers between devices with their start and end apart: 25, of which 11 were waited for; matrix products, arithmetic and copies ran while one was open for 3% of the time, Pallas kernels for 21%

profile of v4, /device:TPU:0, one launch (start us, length us, event | category | flops | bytes accessed | tf_op | source)
XLA Modules:
  0.0 68.7 jit_solution(17330253451498602482)
XLA Ops:
  2.2 2.0 %collective-permute-start.1 = (bf16[10,32,128]{2,1,0:T(8,128)(2,1)S(1)}, bf16[10,32,128]{2,1,0:T(8,128)(2,1)S(1)}, u32[]{:S(2)}, u32[]{:S(2)}) collective-permute-start(bf16[10,32,128]{2,1,0:T(8,128)(2,1)S(1)} %get-tuple-element.47), channel_id=1, source_target_pairs={{0,24},{8,0},{16,8},{24,16},{1,25},{9,1},{17,9},{25,17},{2,26},{10... | collective-permute-start | bytes 245768 | tf_op jit(solution)/shard_map/ppermute | solution.py:20
  4.2 1.5 %shard_map.84 = (f32[2,16,32,128]{3,2,1,0:T(8,128)S(1)}, f32[16,32,128]{2,1,0:T(8,128)S(1)}, bf16[1024,512]{1,0:T(8,128)(2,1)S(1)}) custom-call(f32[2,16,32,128]{3,2,1,0:T(8,128)} %state_ref.1, f32[16,32,128]{2,1,0:T(8,128)} %third_ref.1, bf16[1024,512]{1,0:T(8,128)(2,1)} %weight_ref.2), custom_call_target="tpu_custom_call" | custom-call | flops 2147483648 | tf_op jit(solution)/shard_map/pallas_call | solution.py:527
  7.0 1.7 %collective-permute-start.2 = (bf16[224,128]{1,0:T(8,128)(2,1)S(1)}, bf16[224,128]{1,0:T(8,128)(2,1)S(1)}, u32[]{:S(2)}, u32[]{:S(2)}) collective-permute-start(bf16[224,128]{1,0:T(8,128)(2,1)S(1)} %get-tuple-element.48), channel_id=1, source_target_pairs={{0,2},{2,4},{4,6},{6,0},{1,3},{3,5},{5,7},{7,1},{8,10},{10,12},{12... | collective-permute-start | bytes 172040 | tf_op jit(solution)/shard_map/ppermute | solution.py:20
  8.7 2.1 %collective-permute-start.3 = (bf16[224,128]{1,0:T(8,128)(2,1)S(1)}, bf16[224,128]{1,0:T(8,128)(2,1)S(1)}, u32[]{:S(2)}, u32[]{:S(2)}) collective-permute-start(bf16[224,128]{1,0:T(8,128)(2,1)S(1)} %get-tuple-element.49), channel_id=1, source_target_pairs={{0,6},{2,0},{4,2},{6,4},{1,7},{3,1},{5,3},{7,5},{8,14},{10,8},{12,... | collective-permute-start | bytes 172040 | tf_op jit(solution)/shard_map/ppermute | solution.py:20
  10.9 2.2 %collective-permute-done.2.below_ref = bf16[224,128]{1,0:T(8,128)(2,1)S(1)} collective-permute-done((bf16[224,128]{1,0:T(8,128)(2,1)S(1)}, bf16[224,128]{1,0:T(8,128)(2,1)S(1)}, u32[]{:S(2)}, u32[]{:S(2)}) %collective-permute-start.2) | collective-permute-done | bytes 57376 | tf_op jit(solution)/shard_map/ppermute | solution.py:20
  13.1 1.4 %collective-permute-done.3.above_ref = bf16[224,128]{1,0:T(8,128)(2,1)S(1)} collective-permute-done((bf16[224,128]{1,0:T(8,128)(2,1)S(1)}, bf16[224,128]{1,0:T(8,128)(2,1)S(1)}, u32[]{:S(2)}, u32[]{:S(2)}) %collective-permute-start.3) | collective-permute-done | bytes 57376 | tf_op jit(solution)/shard_map/ppermute | solution.py:20
  15.0 1.5 %collective-permute-start.4 = (bf16[208,128]{1,0:T(8,128)(2,1)S(1)}, bf16[208,128]{1,0:T(8,128)(2,1)S(1)}, u32[]{:S(2)}, u32[]{:S(2)}) collective-permute-start(bf16[208,128]{1,0:T(8,128)(2,1)S(1)} %get-tuple-element.51), channel_id=1, source_target_pairs={{0,1},{1,0},{2,3},{3,2},{4,5},{5,4},{6,7},{7,6},{8,9},{9,8},{10,11... | collective-permute-start | bytes 159752 | tf_op jit(solution)/shard_map/ppermute | solution.py:20
  16.7 2.5 %collective-permute-done.4.earlier_ref.later_ref = bf16[208,128]{1,0:T(8,128)(2,1)S(1)} collective-permute-done((bf16[208,128]{1,0:T(8,128)(2,1)S(1)}, bf16[208,128]{1,0:T(8,128)(2,1)S(1)}, u32[]{:S(2)}, u32[]{:S(2)}) %collective-permute-start.4) | collective-permute-done | bytes 53280 | tf_op jit(solution)/shard_map/ppermute | solution.py:20
  19.2 3.6 %shard_map.88 = (f32[2,16,32,128]{3,2,1,0:T(8,128)S(1)}, bf16[128,512]{1,0:T(8,128)(2,1)S(1)}, bf16[128,512]{1,0:T(8,128)(2,1)S(1)}, f32[2,22,40,128]{3,2,1,0:T(8,128)}) custom-call(f32[3,22,40,128]{3,2,1,0:T(8,128)S(1)} %get-tuple-element.50.whole, bf16[208,128]{1,0:T(8,128)(2,1)S(1)} %collective-permute-done.4.earlier_ref.later_ref, ...), custom_call_target="tpu_custom_call" | custom-call | flops 2147483648 | tf_op jit(solution)/shard_map/pallas_call | solution.py:527
  22.8 1.5 %collective-permute-start.7 = (bf16[128,512]{1,0:T(8,128)(2,1)S(1)}, bf16[128,512]{1,0:T(8,128)(2,1)S(1)}, u32[]{:S(2)}, u32[]{:S(2)}) collective-permute-start(bf16[128,512]{1,0:T(8,128)(2,1)S(1)} %get-tuple-element.59.inputs_ref.own_ref), channel_id=1, source_target_pairs={{0,1},{1,0},{2,3},{3,2},{4,5},{5,4},{6,7},{7,6},{8,9},{9,8},{10,11... | collective-permute-start | bytes 393224 | tf_op jit(solution)/shard_map/ppermute | solution.py:394
  26.4 1.6 %shard_map.89 = (f32[16,32,128]{2,1,0:T(8,128)S(1)}, bf16[128,512]{1,0:T(8,128)(2,1)S(1)}) custom-call(bf16[128,512]{1,0:T(8,128)(2,1)S(1)} %get-tuple-element.59.inputs_ref.own_ref, bf16[128,512]{1,0:T(8,128)(2,1)S(1)} %get-tuple-element.54.targets_ref, bf16[512,1024]{1,0:T(8,128)(2,1)S(1)} %copy-done.1, bf16[1024,1024]{1,0:T(8,128)(2,1)S(1)} %copy-done, ...), custom_call_target="tpu_custom_call" | custom-call | flops 1073741824 | tf_op jit(solution)/shard_map/pallas_call | solution.py:527
  28.1 1.7 %collective-permute-start.6 = (bf16[10,32,128]{2,1,0:T(8,128)(2,1)S(1)}, bf16[10,32,128]{2,1,0:T(8,128)(2,1)S(1)}, u32[]{:S(2)}, u32[]{:S(2)}) collective-permute-start(bf16[10,32,128]{2,1,0:T(8,128)(2,1)S(1)} %get-tuple-element.58), channel_id=1, source_target_pairs={{0,24},{8,0},{16,8},{24,16},{1,25},{9,1},{17,9},{25,17},{2,26},{10... | collective-permute-start | bytes 245768 | tf_op jit(solution)/shard_map/ppermute | solution.py:20
  29.8 1.4 %collective-permute-start.11 = (bf16[128,512]{1,0:T(8,128)(2,1)S(1)}, bf16[128,512]{1,0:T(8,128)(2,1)S(1)}, u32[]{:S(2)}, u32[]{:S(2)}) collective-permute-start(bf16[128,512]{1,0:T(8,128)(2,1)S(1)} %get-tuple-element.65.own_ref), channel_id=1, source_target_pairs={{0,1},{1,0},{2,3},{3,2},{4,5},{5,4},{6,7},{7,6},{8,9},{9,8},{10,11... | collective-permute-start | bytes 393224 | tf_op jit(solution)/shard_map/ppermute | solution.py:394
  33.3 3.3 %shard_map.91 = (bf16[512,512]{1,0:T(8,128)(2,1)S(1)}, bf16[512,1024]{1,0:T(8,128)(2,1)S(1)}, f32[512,1024]{1,0:T(8,128)S(1)}, bf16[512,1024]{1,0:T(8,128)(2,1)S(1)}, f32[512,1024]{1,0:T(8,128)S(1)}) custom-call(bf16[128,512]{1,0:T(8,128)(2,1)S(1)} %get-tuple-element.59.inputs_ref.own_ref, bf16[128,512]{1,0:T(8,128)(2,1)S(1)} %collective-permute-done.7.a_ref, ...), custom_call_target="tpu_custom_call" | custom-call | flops 4294967296 | tf_op jit(solution)/shard_map/pallas_call | solution.py:527
  37.4 1.7 %collective-permute-done.13.c_ref = bf16[128,512]{1,0:T(8,128)(2,1)S(1)} collective-permute-done((bf16[128,512]{1,0:T(8,128)(2,1)S(1)}, bf16[128,512]{1,0:T(8,128)(2,1)S(1)}, u32[]{:S(2)}, u32[]{:S(2)}) %collective-permute-start.13) | collective-permute-done | bytes 131104 | tf_op jit(solution)/shard_map/ppermute | solution.py:394
  39.9 1.4 %shard_map.94 = (bf16[512,1024]{1,0:T(8,128)(2,1)S(1)}, f32[128,1024]{1,0:T(8,128)S(1)}, f32[128,1024]{1,0:T(8,128)S(1)}) custom-call(bf16[512,512]{1,0:T(8,128)(2,1)S(1)} %get-tuple-element.66.carried_ref, bf16[1024,512]{1,0:T(8,128)(2,1)S(1)} %copy-done.2, f32[512,1024]{1,0:T(8,128)S(1)} %get-tuple-element.67.slope_ref, ...), custom_call_target="tpu_custom_call" | custom-call | flops 2147483648 | tf_op jit(solution)/shard_map/pallas_call | solution.py:527
  43.8 3.0 %collective-permute-start.16 = (bf16[224,128]{1,0:T(8,128)(2,1)S(1)}, bf16[224,128]{1,0:T(8,128)(2,1)S(1)}, u32[]{:S(2)}, u32[]{:S(2)}) collective-permute-start(bf16[224,128]{1,0:T(8,128)(2,1)S(1)} %get-tuple-element.63), channel_id=1, source_target_pairs={{0,6},{2,0},{4,2},{6,4},{1,7},{3,1},{5,3},{7,5},{8,14},{10,8},{12,... | collective-permute-start | bytes 172040 | tf_op jit(solution)/shard_map/ppermute | solution.py:20
  47.4 2.1 %collective-permute-start.24 = (f32[32,512]{1,0:T(8,128)S(1)}, f32[32,512]{1,0:T(8,128)S(1)}, u32[]{:S(2)}, u32[]{:S(2)}) collective-permute-start(f32[32,512]{1,0:T(8,128)S(1)} %slice_add_fusion.11), channel_id=1, source_target_pairs={{0,4},{1,5},{2,6},{3,7},{4,0},{5,1},{6,2},{7,3},{8,12},{9,13},{10,... | collective-permute-start | bytes 196616 | tf_op jit(solution)/shard_map/ppermute | solution.py:394
  51.0 2.3 %shard_map.96 = (bf16[512,1024]{1,0:T(8,128)(2,1)}, f32[64,1024]{1,0:T(8,128)S(1)}, f32[64,1024]{1,0:T(8,128)S(1)}) custom-call(bf16[512,1024]{1,0:T(8,128)(2,1)S(1)} %get-tuple-element.77.carried_ref, bf16[1024,1024]{1,0:T(8,128)(2,1)S(1)} %copy-done, f32[512,1024]{1,0:T(8,128)S(1)} %get-tuple-element.78.slope_ref, ...), custom_call_target="tpu_custom_call" | custom-call | flops 2147483648 | tf_op jit(solution)/shard_map/pallas_call | solution.py:527
  54.0 1.2 %collective-permute-start.20 = (bf16[208,128]{1,0:T(8,128)(2,1)S(1)}, bf16[208,128]{1,0:T(8,128)(2,1)S(1)}, u32[]{:S(2)}, u32[]{:S(2)}) collective-permute-start(bf16[208,128]{1,0:T(8,128)(2,1)S(1)} %get-tuple-element.76), channel_id=1, source_target_pairs={{0,1},{1,0},{2,3},{3,2},{4,5},{5,4},{6,7},{7,6},{8,9},{9,8},{10,11... | collective-permute-start | bytes 159752 | tf_op jit(solution)/shard_map/ppermute | solution.py:20
  55.1 1.6 %collective-permute-done.18 = f32[64,1024]{1,0:T(8,128)S(1)} collective-permute-done((f32[64,1024]{1,0:T(8,128)S(1)}, f32[64,1024]{1,0:T(8,128)S(1)}, u32[]{:S(2)}, u32[]{:S(2)}) %collective-permute-start.18) | collective-permute-done | bytes 262176 | tf_op jit(solution)/shard_map/ppermute | solution.py:394
  58.7 3.6 %shard_map.97 = f32[2,16,32,128]{3,2,1,0:T(8,128)} custom-call(f32[3,22,40,128]{3,2,1,0:T(8,128)S(1)} %get-tuple-element.82.whole, bf16[208,128]{1,0:T(8,128)(2,1)S(1)} %collective-permute-done.20.earlier_ref.later_ref, bf16[208,128]{1,0:T(8,128)(2,1)S(1)} %collective-permute-done.20.earlier_ref.later_ref, f32[2,22,40,128]{3,2,1,0:T(8,128)S(1)} %copy-done.3), custom_call_target="tpu_custom_call" | custom-call | flops 4294967296 | tf_op jit(solution)/shard_map/pallas_call | solution.py:527
  62.8 2.1 %collective-permute-start.22 = (f32[16,1024]{1,0:T(8,128)S(1)}, f32[16,1024]{1,0:T(8,128)S(1)}, u32[]{:S(2)}, u32[]{:S(2)}) collective-permute-start(f32[16,1024]{1,0:T(8,128)S(1)} %slice_add_fusion.9), channel_id=1, source_target_pairs={{0,4},{1,5},{2,6},{3,7},{4,0},{5,1},{6,2},{7,3},{8,12},{9,13},{10,... | collective-permute-start | bytes 196616 | tf_op jit(solution)/shard_map/ppermute | solution.py:394
  65.6 2.4 %collective-permute-done.22 = f32[16,1024]{1,0:T(8,128)S(1)} collective-permute-done((f32[16,1024]{1,0:T(8,128)S(1)}, f32[16,1024]{1,0:T(8,128)S(1)}, u32[]{:S(2)}, u32[]{:S(2)}) %collective-permute-start.22) | collective-permute-done | bytes 65568 | tf_op jit(solution)/shard_map/ppermute | solution.py:394
  (59 shorter events, 18.3 us)
Async XLA Ops:
  1.6 4.6 %collective-permute-start = (bf16[10,32,128]{2,1,0:T(8,128)(2,1)S(1)}, bf16[10,32,128]{2,1,0:T(8,128)(2,1)S(1)}, u32[]{:S(2)}, u32[]{:S(2)}) collective-permute-start(bf16[10,32,128]{2,1,0:T(8,128)(2,1)S(1)} %get-tuple-element.46), channel_id=1, source_target_pairs={{0,8},{8,16},{16,24},{24,0},{1,9},{9,17},{17,25},{25,1},{2,10},{10... | collective-permute-start | bytes 245768 | tf_op jit(solution)/shard_map/ppermute | solution.py:20
  2.2 4.7 %collective-permute-start.1 = (bf16[10,32,128]{2,1,0:T(8,128)(2,1)S(1)}, bf16[10,32,128]{2,1,0:T(8,128)(2,1)S(1)}, u32[]{:S(2)}, u32[]{:S(2)}) collective-permute-start(bf16[10,32,128]{2,1,0:T(8,128)(2,1)S(1)} %get-tuple-element.47), channel_id=1, source_target_pairs={{0,24},{8,0},{16,8},{24,16},{1,25},{9,1},{17,9},{25,17},{2,26},{10... | collective-permute-start | bytes 245768 | tf_op jit(solution)/shard_map/ppermute | solution.py:20
  7.0 6.1 %collective-permute-start.2 = (bf16[224,128]{1,0:T(8,128)(2,1)S(1)}, bf16[224,128]{1,0:T(8,128)(2,1)S(1)}, u32[]{:S(2)}, u32[]{:S(2)}) collective-permute-start(bf16[224,128]{1,0:T(8,128)(2,1)S(1)} %get-tuple-element.48), channel_id=1, source_target_pairs={{0,2},{2,4},{4,6},{6,0},{1,3},{3,5},{5,7},{7,1},{8,10},{10,12},{12... | collective-permute-start | bytes 172040 | tf_op jit(solution)/shard_map/ppermute | solution.py:20
  8.7 5.8 %collective-permute-start.3 = (bf16[224,128]{1,0:T(8,128)(2,1)S(1)}, bf16[224,128]{1,0:T(8,128)(2,1)S(1)}, u32[]{:S(2)}, u32[]{:S(2)}) collective-permute-start(bf16[224,128]{1,0:T(8,128)(2,1)S(1)} %get-tuple-element.49), channel_id=1, source_target_pairs={{0,6},{2,0},{4,2},{6,4},{1,7},{3,1},{5,3},{7,5},{8,14},{10,8},{12,... | collective-permute-start | bytes 172040 | tf_op jit(solution)/shard_map/ppermute | solution.py:20
  15.0 4.2 %collective-permute-start.4 = (bf16[208,128]{1,0:T(8,128)(2,1)S(1)}, bf16[208,128]{1,0:T(8,128)(2,1)S(1)}, u32[]{:S(2)}, u32[]{:S(2)}) collective-permute-start(bf16[208,128]{1,0:T(8,128)(2,1)S(1)} %get-tuple-element.51), channel_id=1, source_target_pairs={{0,1},{1,0},{2,3},{3,2},{4,5},{5,4},{6,7},{7,6},{8,9},{9,8},{10,11... | collective-permute-start | bytes 159752 | tf_op jit(solution)/shard_map/ppermute | solution.py:20
  22.8 7.0 %collective-permute-start.7 = (bf16[128,512]{1,0:T(8,128)(2,1)S(1)}, bf16[128,512]{1,0:T(8,128)(2,1)S(1)}, u32[]{:S(2)}, u32[]{:S(2)}) collective-permute-start(bf16[128,512]{1,0:T(8,128)(2,1)S(1)} %get-tuple-element.59.inputs_ref.own_ref), channel_id=1, source_target_pairs={{0,1},{1,0},{2,3},{3,2},{4,5},{5,4},{6,7},{7,6},{8,9},{9,8},{10,11... | collective-permute-start | bytes 393224 | tf_op jit(solution)/shard_map/ppermute | solution.py:394
  24.3 6.9 %collective-permute-start.8 = (bf16[128,512]{1,0:T(8,128)(2,1)S(1)}, bf16[128,512]{1,0:T(8,128)(2,1)S(1)}, u32[]{:S(2)}, u32[]{:S(2)}) collective-permute-start(bf16[128,512]{1,0:T(8,128)(2,1)S(1)} %get-tuple-element.59.inputs_ref.own_ref), channel_id=1, source_target_pairs={{0,2},{1,3},{2,0},{3,1},{4,6},{5,7},{6,4},{7,5},{8,10},{9,11},{10,... | collective-permute-start | bytes 393224 | tf_op jit(solution)/shard_map/ppermute | solution.py:394
  25.4 6.9 %collective-permute-start.9 = (bf16[128,512]{1,0:T(8,128)(2,1)S(1)}, bf16[128,512]{1,0:T(8,128)(2,1)S(1)}, u32[]{:S(2)}, u32[]{:S(2)}) collective-permute-start(bf16[128,512]{1,0:T(8,128)(2,1)S(1)} %get-tuple-element.59.inputs_ref.own_ref), channel_id=1, source_target_pairs={{0,3},{1,2},{2,1},{3,0},{4,7},{5,6},{6,5},{7,4},{8,11},{9,10},{10,... | collective-permute-start | bytes 393224 | tf_op jit(solution)/shard_map/ppermute | solution.py:394
  28.0 8.6 %collective-permute-start.5 = (bf16[10,32,128]{2,1,0:T(8,128)(2,1)S(1)}, bf16[10,32,128]{2,1,0:T(8,128)(2,1)S(1)}, u32[]{:S(2)}, u32[]{:S(2)}) collective-permute-start(bf16[10,32,128]{2,1,0:T(8,128)(2,1)S(1)} %get-tuple-element.57), channel_id=1, source_target_pairs={{0,8},{8,16},{16,24},{24,0},{1,9},{9,17},{17,25},{25,1},{2,10},{10... | collective-permute-start | bytes 245768 | tf_op jit(solution)/shard_map/ppermute | solution.py:20
  28.1 8.6 %collective-permute-start.6 = (bf16[10,32,128]{2,1,0:T(8,128)(2,1)S(1)}, bf16[10,32,128]{2,1,0:T(8,128)(2,1)S(1)}, u32[]{:S(2)}, u32[]{:S(2)}) collective-permute-start(bf16[10,32,128]{2,1,0:T(8,128)(2,1)S(1)} %get-tuple-element.58), channel_id=1, source_target_pairs={{0,24},{8,0},{16,8},{24,16},{1,25},{9,1},{17,9},{25,17},{2,26},{10... | collective-permute-start | bytes 245768 | tf_op jit(solution)/shard_map/ppermute | solution.py:20
  29.8 6.9 %collective-permute-start.11 = (bf16[128,512]{1,0:T(8,128)(2,1)S(1)}, bf16[128,512]{1,0:T(8,128)(2,1)S(1)}, u32[]{:S(2)}, u32[]{:S(2)}) collective-permute-start(bf16[128,512]{1,0:T(8,128)(2,1)S(1)} %get-tuple-element.65.own_ref), channel_id=1, source_target_pairs={{0,1},{1,0},{2,3},{3,2},{4,5},{5,4},{6,7},{7,6},{8,9},{9,8},{10,11... | collective-permute-start | bytes 393224 | tf_op jit(solution)/shard_map/ppermute | solution.py:394
  31.2 6.2 %collective-permute-start.12 = (bf16[128,512]{1,0:T(8,128)(2,1)S(1)}, bf16[128,512]{1,0:T(8,128)(2,1)S(1)}, u32[]{:S(2)}, u32[]{:S(2)}) collective-permute-start(bf16[128,512]{1,0:T(8,128)(2,1)S(1)} %get-tuple-element.65.own_ref), channel_id=1, source_target_pairs={{0,2},{1,3},{2,0},{3,1},{4,6},{5,7},{6,4},{7,5},{8,10},{9,11},{10,... | collective-permute-start | bytes 393224 | tf_op jit(solution)/shard_map/ppermute | solution.py:394
  32.4 6.7 %collective-permute-start.13 = (bf16[128,512]{1,0:T(8,128)(2,1)S(1)}, bf16[128,512]{1,0:T(8,128)(2,1)S(1)}, u32[]{:S(2)}, u32[]{:S(2)}) collective-permute-start(bf16[128,512]{1,0:T(8,128)(2,1)S(1)} %get-tuple-element.65.own_ref), channel_id=1, source_target_pairs={{0,3},{1,2},{2,1},{3,0},{4,7},{5,6},{6,5},{7,4},{8,11},{9,10},{10,... | collective-permute-start | bytes 393224 | tf_op jit(solution)/shard_map/ppermute | solution.py:394
  41.3 8.2 %collective-permute-start.15 = (f32[128,1024]{1,0:T(8,128)S(1)}, f32[128,1024]{1,0:T(8,128)S(1)}, u32[]{:S(2)}, u32[]{:S(2)}) collective-permute-start(f32[128,1024]{1,0:T(8,128)S(1)} %get-tuple-element.73), channel_id=1, source_target_pairs={{0,8},{1,9},{2,10},{3,11},{4,12},{5,13},{6,14},{7,15},{8,0},{9,1},... | collective-permute-start | bytes 1572872 | tf_op jit(solution)/shard_map/ppermute | solution.py:394
  41.9 5.5 %collective-permute-start.19 = (f32[64,512]{1,0:T(8,128)S(1)}, f32[64,512]{1,0:T(8,128)S(1)}, u32[]{:S(2)}, u32[]{:S(2)}) collective-permute-start(f32[64,512]{1,0:T(8,128)S(1)} %get-tuple-element.89), channel_id=1, source_target_pairs={{0,16},{1,17},{2,18},{3,19},{4,20},{5,21},{6,22},{7,23},{8,24},{9,... | collective-permute-start | bytes 393224 | tf_op jit(solution)/shard_map/ppermute | solution.py:394
  42.9 7.6 %collective-permute-start.10 = (bf16[224,128]{1,0:T(8,128)(2,1)S(1)}, bf16[224,128]{1,0:T(8,128)(2,1)S(1)}, u32[]{:S(2)}, u32[]{:S(2)}) collective-permute-start(bf16[224,128]{1,0:T(8,128)(2,1)S(1)} %get-tuple-element.62), channel_id=1, source_target_pairs={{0,2},{2,4},{4,6},{6,0},{1,3},{3,5},{5,7},{7,1},{8,10},{10,12},{12... | collective-permute-start | bytes 172040 | tf_op jit(solution)/shard_map/ppermute | solution.py:20
  43.8 6.7 %collective-permute-start.16 = (bf16[224,128]{1,0:T(8,128)(2,1)S(1)}, bf16[224,128]{1,0:T(8,128)(2,1)S(1)}, u32[]{:S(2)}, u32[]{:S(2)}) collective-permute-start(bf16[224,128]{1,0:T(8,128)(2,1)S(1)} %get-tuple-element.63), channel_id=1, source_target_pairs={{0,6},{2,0},{4,2},{6,4},{1,7},{3,1},{5,3},{7,5},{8,14},{10,8},{12,... | collective-permute-start | bytes 172040 | tf_op jit(solution)/shard_map/ppermute | solution.py:20
  47.4 5.9 %collective-permute-start.24 = (f32[32,512]{1,0:T(8,128)S(1)}, f32[32,512]{1,0:T(8,128)S(1)}, u32[]{:S(2)}, u32[]{:S(2)}) collective-permute-start(f32[32,512]{1,0:T(8,128)S(1)} %slice_add_fusion.11), channel_id=1, source_target_pairs={{0,4},{1,5},{2,6},{3,7},{4,0},{5,1},{6,2},{7,3},{8,12},{9,13},{10,... | collective-permute-start | bytes 196616 | tf_op jit(solution)/shard_map/ppermute | solution.py:394
  49.6 7.2 %collective-permute-start.18 = (f32[64,1024]{1,0:T(8,128)S(1)}, f32[64,1024]{1,0:T(8,128)S(1)}, u32[]{:S(2)}, u32[]{:S(2)}) collective-permute-start(f32[64,1024]{1,0:T(8,128)S(1)} %get-tuple-element.85), channel_id=1, source_target_pairs={{0,16},{1,17},{2,18},{3,19},{4,20},{5,21},{6,22},{7,23},{8,24},{9,... | collective-permute-start | bytes 786440 | tf_op jit(solution)/shard_map/ppermute | solution.py:394
  53.3 4.4 %collective-permute-start.17 = (f32[64,1024]{1,0:T(8,128)S(1)}, f32[64,1024]{1,0:T(8,128)S(1)}, u32[]{:S(2)}, u32[]{:S(2)}) collective-permute-start(f32[64,1024]{1,0:T(8,128)S(1)} %get-tuple-element.81), channel_id=1, source_target_pairs={{0,8},{1,9},{2,10},{3,11},{4,12},{5,13},{6,14},{7,15},{8,0},{9,1},... | collective-permute-start | bytes 786440 | tf_op jit(solution)/shard_map/ppermute | solution.py:394
  54.0 4.7 %collective-permute-start.20 = (bf16[208,128]{1,0:T(8,128)(2,1)S(1)}, bf16[208,128]{1,0:T(8,128)(2,1)S(1)}, u32[]{:S(2)}, u32[]{:S(2)}) collective-permute-start(bf16[208,128]{1,0:T(8,128)(2,1)S(1)} %get-tuple-element.76), channel_id=1, source_target_pairs={{0,1},{1,0},{2,3},{3,2},{4,5},{5,4},{6,7},{7,6},{8,9},{9,8},{10,11... | collective-permute-start | bytes 159752 | tf_op jit(solution)/shard_map/ppermute | solution.py:20
  56.7 8.1 %collective-permute-start.23 = (f32[32,1024]{1,0:T(8,128)S(1)}, f32[32,1024]{1,0:T(8,128)S(1)}, u32[]{:S(2)}, u32[]{:S(2)}) collective-permute-start(f32[32,1024]{1,0:T(8,128)S(1)} %slice_add_fusion.5), channel_id=1, source_target_pairs={{0,4},{1,5},{2,6},{3,7},{4,0},{5,1},{6,2},{7,3},{8,12},{9,13},{10,... | collective-permute-start | bytes 393224 | tf_op jit(solution)/shard_map/ppermute | solution.py:394
  57.7 5.0 %collective-permute-start.21 = (f32[32,1024]{1,0:T(8,128)S(1)}, f32[32,1024]{1,0:T(8,128)S(1)}, u32[]{:S(2)}, u32[]{:S(2)}) collective-permute-start(f32[32,1024]{1,0:T(8,128)S(1)} %get-tuple-element.87), channel_id=1, source_target_pairs={{0,16},{1,17},{2,18},{3,19},{4,20},{5,21},{6,22},{7,23},{8,24},{9,... | collective-permute-start | bytes 393224 | tf_op jit(solution)/shard_map/ppermute | solution.py:394
  62.8 5.2 %collective-permute-start.22 = (f32[16,1024]{1,0:T(8,128)S(1)}, f32[16,1024]{1,0:T(8,128)S(1)}, u32[]{:S(2)}, u32[]{:S(2)}) collective-permute-start(f32[16,1024]{1,0:T(8,128)S(1)} %slice_add_fusion.9), channel_id=1, source_target_pairs={{0,4},{1,5},{2,6},{3,7},{4,0},{5,1},{6,2},{7,3},{8,12},{9,13},{10,... | collective-permute-start | bytes 196616 | tf_op jit(solution)/shard_map/ppermute | solution.py:394
  (5 other events, 27.2 us)

commit v5 on v4

--- a/solution.py
+++ b/solution.py
@@ -12,6 +12,7 @@
 PATCH = 8
 HALO = STEPS // 2
 EDGE = 4
+AXES = ("gx", "gy", "row")
 VMEM_LIMIT = 20 << 20
 
 
@@ -391,7 +392,7 @@
                 here = (i * size_y + j) * size_r + k
                 there = ((i ^ flips[0]) * size_y + (j ^ flips[1])) * size_r + (k ^ flips[2])
                 route.append((here, there))
-    return lax.ppermute(array, ("gx", "gy", "row"), route)
+    return lax.ppermute(array, AXES, route)
 
 
 def reduction_stages(mesh_sizes):
@@ -542,7 +543,7 @@
 
 
 def all_steps(concentrations, diffusivity, weight_first, weight_middle, weight_last):
-    mesh_sizes = tuple(lax.axis_size(axis) for axis in ("gx", "gy", "row"))
+    mesh_sizes = tuple(lax.axis_size(axis) for axis in AXES)
     length, height, width = diffusivity.shape
     f32, bf16 = (jnp.float32, jnp.bfloat16)
     planes, rows = (length + 2 * HALO, height + 2 * EDGE)
@@ -626,11 +627,11 @@
 
 
 def solution(mesh):
-    in_specs = (P(None, "gx", "gy", "row"), P("gx", "gy", "row"), P(), P(), P())
+    in_specs = (P(None, *AXES), P(*AXES), P(), P(), P())
     out_specs = (
-        P(None, "gx", "gy", "row"),
-        P(("gx", "gy", "row"), None),
-        P(("gx", "gy", "row"), None),
-        P(("gx", "gy", "row"), None),
+        P(None, *AXES),
+        P(AXES, None),
+        P(AXES, None),
+        P(AXES, None),
     )
     return jax.shard_map(all_steps, mesh=mesh, in_specs=in_specs, out_specs=out_specs, check_vma=False)

time: 68.8 us -> 68.8 us (level)
  no operation moved by 1% of the time
where the time goes in v5:
time: 68.8 us; the launch traced here: 68.7 us
  starting transfers between devices  30.4 us (44%)
  Pallas kernels  20.1 us (29%)
  waiting for transfers between devices  14.9 us (22%)
  other arithmetic  2.42 us (4%)
  between operations  0.84 us (1%)
    pallas_call x14, Pallas kernels, call(): pl.pallas_call(body, cost_estimate=pl.CostEstimate(flops=flops, transcend...  20.1 us
    ppermute x15, starting transfers between devices, exchange(): return lax.ppermute(array, AXES, route)  15.7 us
    ppermute x10, starting transfers between devices, ring(): lax.ppermute(array, axis, [(i, (i + distance) % size) for i in range(size)])  14.7 us
    ppermute x10, waiting for transfers between devices, ring(): lax.ppermute(array, axis, [(i, (i + distance) % size) for i in range(size)])  7.5 us
    ppermute x15, waiting for transfers between devices, exchange(): return lax.ppermute(array, AXES, route)  7.43 us
    add x3, other arithmetic, rest_halved(): return staying + arrived  1.97 us
  transfers between devices with their start and end apart: 25, of which 11 were waited for; matrix products, arithmetic and copies ran while one was open for 3% of the time, Pallas kernels for 21%

profile of v5, /device:TPU:0, one launch (start us, length us, event | category | flops | bytes accessed | tf_op | source)
XLA Modules:
  0.0 68.7 jit_solution(17330253451498602482)
XLA Ops:
  2.2 2.0 %collective-permute-start.1 = (bf16[10,32,128]{2,1,0:T(8,128)(2,1)S(1)}, bf16[10,32,128]{2,1,0:T(8,128)(2,1)S(1)}, u32[]{:S(2)}, u32[]{:S(2)}) collective-permute-start(bf16[10,32,128]{2,1,0:T(8,128)(2,1)S(1)} %get-tuple-element.47), channel_id=1, source_target_pairs={{0,24},{8,0},{16,8},{24,16},{1,25},{9,1},{17,9},{25,17},{2,26},{10... | collective-permute-start | bytes 245768 | tf_op jit(solution)/shard_map/ppermute | solution.py:21
  4.2 1.5 %shard_map.84 = (f32[2,16,32,128]{3,2,1,0:T(8,128)S(1)}, f32[16,32,128]{2,1,0:T(8,128)S(1)}, bf16[1024,512]{1,0:T(8,128)(2,1)S(1)}) custom-call(f32[2,16,32,128]{3,2,1,0:T(8,128)} %state_ref.1, f32[16,32,128]{2,1,0:T(8,128)} %third_ref.1, bf16[1024,512]{1,0:T(8,128)(2,1)} %weight_ref.2), custom_call_target="tpu_custom_call" | custom-call | flops 2147483648 | tf_op jit(solution)/shard_map/pallas_call | solution.py:528
  7.0 1.7 %collective-permute-start.2 = (bf16[224,128]{1,0:T(8,128)(2,1)S(1)}, bf16[224,128]{1,0:T(8,128)(2,1)S(1)}, u32[]{:S(2)}, u32[]{:S(2)}) collective-permute-start(bf16[224,128]{1,0:T(8,128)(2,1)S(1)} %get-tuple-element.48), channel_id=1, source_target_pairs={{0,2},{2,4},{4,6},{6,0},{1,3},{3,5},{5,7},{7,1},{8,10},{10,12},{12... | collective-permute-start | bytes 172040 | tf_op jit(solution)/shard_map/ppermute | solution.py:21
  8.7 2.1 %collective-permute-start.3 = (bf16[224,128]{1,0:T(8,128)(2,1)S(1)}, bf16[224,128]{1,0:T(8,128)(2,1)S(1)}, u32[]{:S(2)}, u32[]{:S(2)}) collective-permute-start(bf16[224,128]{1,0:T(8,128)(2,1)S(1)} %get-tuple-element.49), channel_id=1, source_target_pairs={{0,6},{2,0},{4,2},{6,4},{1,7},{3,1},{5,3},{7,5},{8,14},{10,8},{12,... | collective-permute-start | bytes 172040 | tf_op jit(solution)/shard_map/ppermute | solution.py:21
  10.9 2.2 %collective-permute-done.2.below_ref = bf16[224,128]{1,0:T(8,128)(2,1)S(1)} collective-permute-done((bf16[224,128]{1,0:T(8,128)(2,1)S(1)}, bf16[224,128]{1,0:T(8,128)(2,1)S(1)}, u32[]{:S(2)}, u32[]{:S(2)}) %collective-permute-start.2) | collective-permute-done | bytes 57376 | tf_op jit(solution)/shard_map/ppermute | solution.py:21
  13.1 1.4 %collective-permute-done.3.above_ref = bf16[224,128]{1,0:T(8,128)(2,1)S(1)} collective-permute-done((bf16[224,128]{1,0:T(8,128)(2,1)S(1)}, bf16[224,128]{1,0:T(8,128)(2,1)S(1)}, u32[]{:S(2)}, u32[]{:S(2)}) %collective-permute-start.3) | collective-permute-done | bytes 57376 | tf_op jit(solution)/shard_map/ppermute | solution.py:21
  15.0 1.5 %collective-permute-start.4 = (bf16[208,128]{1,0:T(8,128)(2,1)S(1)}, bf16[208,128]{1,0:T(8,128)(2,1)S(1)}, u32[]{:S(2)}, u32[]{:S(2)}) collective-permute-start(bf16[208,128]{1,0:T(8,128)(2,1)S(1)} %get-tuple-element.51), channel_id=1, source_target_pairs={{0,1},{1,0},{2,3},{3,2},{4,5},{5,4},{6,7},{7,6},{8,9},{9,8},{10,11... | collective-permute-start | bytes 159752 | tf_op jit(solution)/shard_map/ppermute | solution.py:21
  16.7 2.5 %collective-permute-done.4.earlier_ref.later_ref = bf16[208,128]{1,0:T(8,128)(2,1)S(1)} collective-permute-done((bf16[208,128]{1,0:T(8,128)(2,1)S(1)}, bf16[208,128]{1,0:T(8,128)(2,1)S(1)}, u32[]{:S(2)}, u32[]{:S(2)}) %collective-permute-start.4) | collective-permute-done | bytes 53280 | tf_op jit(solution)/shard_map/ppermute | solution.py:21
  19.2 3.6 %shard_map.88 = (f32[2,16,32,128]{3,2,1,0:T(8,128)S(1)}, bf16[128,512]{1,0:T(8,128)(2,1)S(1)}, bf16[128,512]{1,0:T(8,128)(2,1)S(1)}, f32[2,22,40,128]{3,2,1,0:T(8,128)}) custom-call(f32[3,22,40,128]{3,2,1,0:T(8,128)S(1)} %get-tuple-element.50.whole, bf16[208,128]{1,0:T(8,128)(2,1)S(1)} %collective-permute-done.4.earlier_ref.later_ref, ...), custom_call_target="tpu_custom_call" | custom-call | flops 2147483648 | tf_op jit(solution)/shard_map/pallas_call | solution.py:528
  22.8 1.5 %collective-permute-start.7 = (bf16[128,512]{1,0:T(8,128)(2,1)S(1)}, bf16[128,512]{1,0:T(8,128)(2,1)S(1)}, u32[]{:S(2)}, u32[]{:S(2)}) collective-permute-start(bf16[128,512]{1,0:T(8,128)(2,1)S(1)} %get-tuple-element.59.inputs_ref.own_ref), channel_id=1, source_target_pairs={{0,1},{1,0},{2,3},{3,2},{4,5},{5,4},{6,7},{7,6},{8,9},{9,8},{10,11... | collective-permute-start | bytes 393224 | tf_op jit(solution)/shard_map/ppermute | solution.py:395
  26.4 1.6 %shard_map.89 = (f32[16,32,128]{2,1,0:T(8,128)S(1)}, bf16[128,512]{1,0:T(8,128)(2,1)S(1)}) custom-call(bf16[128,512]{1,0:T(8,128)(2,1)S(1)} %get-tuple-element.59.inputs_ref.own_ref, bf16[128,512]{1,0:T(8,128)(2,1)S(1)} %get-tuple-element.54.targets_ref, bf16[512,1024]{1,0:T(8,128)(2,1)S(1)} %copy-done.1, bf16[1024,1024]{1,0:T(8,128)(2,1)S(1)} %copy-done, ...), custom_call_target="tpu_custom_call" | custom-call | flops 1073741824 | tf_op jit(solution)/shard_map/pallas_call | solution.py:528
  28.1 1.7 %collective-permute-start.6 = (bf16[10,32,128]{2,1,0:T(8,128)(2,1)S(1)}, bf16[10,32,128]{2,1,0:T(8,128)(2,1)S(1)}, u32[]{:S(2)}, u32[]{:S(2)}) collective-permute-start(bf16[10,32,128]{2,1,0:T(8,128)(2,1)S(1)} %get-tuple-element.58), channel_id=1, source_target_pairs={{0,24},{8,0},{16,8},{24,16},{1,25},{9,1},{17,9},{25,17},{2,26},{10... | collective-permute-start | bytes 245768 | tf_op jit(solution)/shard_map/ppermute | solution.py:21
  29.8 1.4 %collective-permute-start.11 = (bf16[128,512]{1,0:T(8,128)(2,1)S(1)}, bf16[128,512]{1,0:T(8,128)(2,1)S(1)}, u32[]{:S(2)}, u32[]{:S(2)}) collective-permute-start(bf16[128,512]{1,0:T(8,128)(2,1)S(1)} %get-tuple-element.65.own_ref), channel_id=1, source_target_pairs={{0,1},{1,0},{2,3},{3,2},{4,5},{5,4},{6,7},{7,6},{8,9},{9,8},{10,11... | collective-permute-start | bytes 393224 | tf_op jit(solution)/shard_map/ppermute | solution.py:395
  33.3 3.3 %shard_map.91 = (bf16[512,512]{1,0:T(8,128)(2,1)S(1)}, bf16[512,1024]{1,0:T(8,128)(2,1)S(1)}, f32[512,1024]{1,0:T(8,128)S(1)}, bf16[512,1024]{1,0:T(8,128)(2,1)S(1)}, f32[512,1024]{1,0:T(8,128)S(1)}) custom-call(bf16[128,512]{1,0:T(8,128)(2,1)S(1)} %get-tuple-element.59.inputs_ref.own_ref, bf16[128,512]{1,0:T(8,128)(2,1)S(1)} %collective-permute-done.7.a_ref, ...), custom_call_target="tpu_custom_call" | custom-call | flops 4294967296 | tf_op jit(solution)/shard_map/pallas_call | solution.py:528
  37.4 1.7 %collective-permute-done.13.c_ref = bf16[128,512]{1,0:T(8,128)(2,1)S(1)} collective-permute-done((bf16[128,512]{1,0:T(8,128)(2,1)S(1)}, bf16[128,512]{1,0:T(8,128)(2,1)S(1)}, u32[]{:S(2)}, u32[]{:S(2)}) %collective-permute-start.13) | collective-permute-done | bytes 131104 | tf_op jit(solution)/shard_map/ppermute | solution.py:395
  39.9 1.4 %shard_map.94 = (bf16[512,1024]{1,0:T(8,128)(2,1)S(1)}, f32[128,1024]{1,0:T(8,128)S(1)}, f32[128,1024]{1,0:T(8,128)S(1)}) custom-call(bf16[512,512]{1,0:T(8,128)(2,1)S(1)} %get-tuple-element.66.carried_ref, bf16[1024,512]{1,0:T(8,128)(2,1)S(1)} %copy-done.2, f32[512,1024]{1,0:T(8,128)S(1)} %get-tuple-element.67.slope_ref, ...), custom_call_target="tpu_custom_call" | custom-call | flops 2147483648 | tf_op jit(solution)/shard_map/pallas_call | solution.py:528
  43.8 3.0 %collective-permute-start.16 = (bf16[224,128]{1,0:T(8,128)(2,1)S(1)}, bf16[224,128]{1,0:T(8,128)(2,1)S(1)}, u32[]{:S(2)}, u32[]{:S(2)}) collective-permute-start(bf16[224,128]{1,0:T(8,128)(2,1)S(1)} %get-tuple-element.63), channel_id=1, source_target_pairs={{0,6},{2,0},{4,2},{6,4},{1,7},{3,1},{5,3},{7,5},{8,14},{10,8},{12,... | collective-permute-start | bytes 172040 | tf_op jit(solution)/shard_map/ppermute | solution.py:21
  47.4 2.1 %collective-permute-start.24 = (f32[32,512]{1,0:T(8,128)S(1)}, f32[32,512]{1,0:T(8,128)S(1)}, u32[]{:S(2)}, u32[]{:S(2)}) collective-permute-start(f32[32,512]{1,0:T(8,128)S(1)} %slice_add_fusion.11), channel_id=1, source_target_pairs={{0,4},{1,5},{2,6},{3,7},{4,0},{5,1},{6,2},{7,3},{8,12},{9,13},{10,... | collective-permute-start | bytes 196616 | tf_op jit(solution)/shard_map/ppermute | solution.py:395
  51.0 2.3 %shard_map.96 = (bf16[512,1024]{1,0:T(8,128)(2,1)}, f32[64,1024]{1,0:T(8,128)S(1)}, f32[64,1024]{1,0:T(8,128)S(1)}) custom-call(bf16[512,1024]{1,0:T(8,128)(2,1)S(1)} %get-tuple-element.77.carried_ref, bf16[1024,1024]{1,0:T(8,128)(2,1)S(1)} %copy-done, f32[512,1024]{1,0:T(8,128)S(1)} %get-tuple-element.78.slope_ref, ...), custom_call_target="tpu_custom_call" | custom-call | flops 2147483648 | tf_op jit(solution)/shard_map/pallas_call | solution.py:528
  54.0 1.2 %collective-permute-start.20 = (bf16[208,128]{1,0:T(8,128)(2,1)S(1)}, bf16[208,128]{1,0:T(8,128)(2,1)S(1)}, u32[]{:S(2)}, u32[]{:S(2)}) collective-permute-start(bf16[208,128]{1,0:T(8,128)(2,1)S(1)} %get-tuple-element.76), channel_id=1, source_target_pairs={{0,1},{1,0},{2,3},{3,2},{4,5},{5,4},{6,7},{7,6},{8,9},{9,8},{10,11... | collective-permute-start | bytes 159752 | tf_op jit(solution)/shard_map/ppermute | solution.py:21
  55.1 1.6 %collective-permute-done.18 = f32[64,1024]{1,0:T(8,128)S(1)} collective-permute-done((f32[64,1024]{1,0:T(8,128)S(1)}, f32[64,1024]{1,0:T(8,128)S(1)}, u32[]{:S(2)}, u32[]{:S(2)}) %collective-permute-start.18) | collective-permute-done | bytes 262176 | tf_op jit(solution)/shard_map/ppermute | solution.py:395
  58.7 3.6 %shard_map.97 = f32[2,16,32,128]{3,2,1,0:T(8,128)} custom-call(f32[3,22,40,128]{3,2,1,0:T(8,128)S(1)} %get-tuple-element.82.whole, bf16[208,128]{1,0:T(8,128)(2,1)S(1)} %collective-permute-done.20.earlier_ref.later_ref, bf16[208,128]{1,0:T(8,128)(2,1)S(1)} %collective-permute-done.20.earlier_ref.later_ref, f32[2,22,40,128]{3,2,1,0:T(8,128)S(1)} %copy-done.3), custom_call_target="tpu_custom_call" | custom-call | flops 4294967296 | tf_op jit(solution)/shard_map/pallas_call | solution.py:528
  62.8 2.1 %collective-permute-start.22 = (f32[16,1024]{1,0:T(8,128)S(1)}, f32[16,1024]{1,0:T(8,128)S(1)}, u32[]{:S(2)}, u32[]{:S(2)}) collective-permute-start(f32[16,1024]{1,0:T(8,128)S(1)} %slice_add_fusion.9), channel_id=1, source_target_pairs={{0,4},{1,5},{2,6},{3,7},{4,0},{5,1},{6,2},{7,3},{8,12},{9,13},{10,... | collective-permute-start | bytes 196616 | tf_op jit(solution)/shard_map/ppermute | solution.py:395
  65.6 2.4 %collective-permute-done.22 = f32[16,1024]{1,0:T(8,128)S(1)} collective-permute-done((f32[16,1024]{1,0:T(8,128)S(1)}, f32[16,1024]{1,0:T(8,128)S(1)}, u32[]{:S(2)}, u32[]{:S(2)}) %collective-permute-start.22) | collective-permute-done | bytes 65568 | tf_op jit(solution)/shard_map/ppermute | solution.py:395
  (59 shorter events, 18.3 us)
Async XLA Ops:
  1.6 4.6 %collective-permute-start = (bf16[10,32,128]{2,1,0:T(8,128)(2,1)S(1)}, bf16[10,32,128]{2,1,0:T(8,128)(2,1)S(1)}, u32[]{:S(2)}, u32[]{:S(2)}) collective-permute-start(bf16[10,32,128]{2,1,0:T(8,128)(2,1)S(1)} %get-tuple-element.46), channel_id=1, source_target_pairs={{0,8},{8,16},{16,24},{24,0},{1,9},{9,17},{17,25},{25,1},{2,10},{10... | collective-permute-start | bytes 245768 | tf_op jit(solution)/shard_map/ppermute | solution.py:21
  2.2 4.7 %collective-permute-start.1 = (bf16[10,32,128]{2,1,0:T(8,128)(2,1)S(1)}, bf16[10,32,128]{2,1,0:T(8,128)(2,1)S(1)}, u32[]{:S(2)}, u32[]{:S(2)}) collective-permute-start(bf16[10,32,128]{2,1,0:T(8,128)(2,1)S(1)} %get-tuple-element.47), channel_id=1, source_target_pairs={{0,24},{8,0},{16,8},{24,16},{1,25},{9,1},{17,9},{25,17},{2,26},{10... | collective-permute-start | bytes 245768 | tf_op jit(solution)/shard_map/ppermute | solution.py:21
  7.0 6.1 %collective-permute-start.2 = (bf16[224,128]{1,0:T(8,128)(2,1)S(1)}, bf16[224,128]{1,0:T(8,128)(2,1)S(1)}, u32[]{:S(2)}, u32[]{:S(2)}) collective-permute-start(bf16[224,128]{1,0:T(8,128)(2,1)S(1)} %get-tuple-element.48), channel_id=1, source_target_pairs={{0,2},{2,4},{4,6},{6,0},{1,3},{3,5},{5,7},{7,1},{8,10},{10,12},{12... | collective-permute-start | bytes 172040 | tf_op jit(solution)/shard_map/ppermute | solution.py:21
  8.7 5.8 %collective-permute-start.3 = (bf16[224,128]{1,0:T(8,128)(2,1)S(1)}, bf16[224,128]{1,0:T(8,128)(2,1)S(1)}, u32[]{:S(2)}, u32[]{:S(2)}) collective-permute-start(bf16[224,128]{1,0:T(8,128)(2,1)S(1)} %get-tuple-element.49), channel_id=1, source_target_pairs={{0,6},{2,0},{4,2},{6,4},{1,7},{3,1},{5,3},{7,5},{8,14},{10,8},{12,... | collective-permute-start | bytes 172040 | tf_op jit(solution)/shard_map/ppermute | solution.py:21
  15.0 4.2 %collective-permute-start.4 = (bf16[208,128]{1,0:T(8,128)(2,1)S(1)}, bf16[208,128]{1,0:T(8,128)(2,1)S(1)}, u32[]{:S(2)}, u32[]{:S(2)}) collective-permute-start(bf16[208,128]{1,0:T(8,128)(2,1)S(1)} %get-tuple-element.51), channel_id=1, source_target_pairs={{0,1},{1,0},{2,3},{3,2},{4,5},{5,4},{6,7},{7,6},{8,9},{9,8},{10,11... | collective-permute-start | bytes 159752 | tf_op jit(solution)/shard_map/ppermute | solution.py:21
  22.8 7.0 %collective-permute-start.7 = (bf16[128,512]{1,0:T(8,128)(2,1)S(1)}, bf16[128,512]{1,0:T(8,128)(2,1)S(1)}, u32[]{:S(2)}, u32[]{:S(2)}) collective-permute-start(bf16[128,512]{1,0:T(8,128)(2,1)S(1)} %get-tuple-element.59.inputs_ref.own_ref), channel_id=1, source_target_pairs={{0,1},{1,0},{2,3},{3,2},{4,5},{5,4},{6,7},{7,6},{8,9},{9,8},{10,11... | collective-permute-start | bytes 393224 | tf_op jit(solution)/shard_map/ppermute | solution.py:395
  24.3 6.9 %collective-permute-start.8 = (bf16[128,512]{1,0:T(8,128)(2,1)S(1)}, bf16[128,512]{1,0:T(8,128)(2,1)S(1)}, u32[]{:S(2)}, u32[]{:S(2)}) collective-permute-start(bf16[128,512]{1,0:T(8,128)(2,1)S(1)} %get-tuple-element.59.inputs_ref.own_ref), channel_id=1, source_target_pairs={{0,2},{1,3},{2,0},{3,1},{4,6},{5,7},{6,4},{7,5},{8,10},{9,11},{10,... | collective-permute-start | bytes 393224 | tf_op jit(solution)/shard_map/ppermute | solution.py:395
  25.4 6.9 %collective-permute-start.9 = (bf16[128,512]{1,0:T(8,128)(2,1)S(1)}, bf16[128,512]{1,0:T(8,128)(2,1)S(1)}, u32[]{:S(2)}, u32[]{:S(2)}) collective-permute-start(bf16[128,512]{1,0:T(8,128)(2,1)S(1)} %get-tuple-element.59.inputs_ref.own_ref), channel_id=1, source_target_pairs={{0,3},{1,2},{2,1},{3,0},{4,7},{5,6},{6,5},{7,4},{8,11},{9,10},{10,... | collective-permute-start | bytes 393224 | tf_op jit(solution)/shard_map/ppermute | solution.py:395
  28.0 8.6 %collective-permute-start.5 = (bf16[10,32,128]{2,1,0:T(8,128)(2,1)S(1)}, bf16[10,32,128]{2,1,0:T(8,128)(2,1)S(1)}, u32[]{:S(2)}, u32[]{:S(2)}) collective-permute-start(bf16[10,32,128]{2,1,0:T(8,128)(2,1)S(1)} %get-tuple-element.57), channel_id=1, source_target_pairs={{0,8},{8,16},{16,24},{24,0},{1,9},{9,17},{17,25},{25,1},{2,10},{10... | collective-permute-start | bytes 245768 | tf_op jit(solution)/shard_map/ppermute | solution.py:21
  28.1 8.6 %collective-permute-start.6 = (bf16[10,32,128]{2,1,0:T(8,128)(2,1)S(1)}, bf16[10,32,128]{2,1,0:T(8,128)(2,1)S(1)}, u32[]{:S(2)}, u32[]{:S(2)}) collective-permute-start(bf16[10,32,128]{2,1,0:T(8,128)(2,1)S(1)} %get-tuple-element.58), channel_id=1, source_target_pairs={{0,24},{8,0},{16,8},{24,16},{1,25},{9,1},{17,9},{25,17},{2,26},{10... | collective-permute-start | bytes 245768 | tf_op jit(solution)/shard_map/ppermute | solution.py:21
  29.8 6.9 %collective-permute-start.11 = (bf16[128,512]{1,0:T(8,128)(2,1)S(1)}, bf16[128,512]{1,0:T(8,128)(2,1)S(1)}, u32[]{:S(2)}, u32[]{:S(2)}) collective-permute-start(bf16[128,512]{1,0:T(8,128)(2,1)S(1)} %get-tuple-element.65.own_ref), channel_id=1, source_target_pairs={{0,1},{1,0},{2,3},{3,2},{4,5},{5,4},{6,7},{7,6},{8,9},{9,8},{10,11... | collective-permute-start | bytes 393224 | tf_op jit(solution)/shard_map/ppermute | solution.py:395
  31.2 6.2 %collective-permute-start.12 = (bf16[128,512]{1,0:T(8,128)(2,1)S(1)}, bf16[128,512]{1,0:T(8,128)(2,1)S(1)}, u32[]{:S(2)}, u32[]{:S(2)}) collective-permute-start(bf16[128,512]{1,0:T(8,128)(2,1)S(1)} %get-tuple-element.65.own_ref), channel_id=1, source_target_pairs={{0,2},{1,3},{2,0},{3,1},{4,6},{5,7},{6,4},{7,5},{8,10},{9,11},{10,... | collective-permute-start | bytes 393224 | tf_op jit(solution)/shard_map/ppermute | solution.py:395
  32.4 6.7 %collective-permute-start.13 = (bf16[128,512]{1,0:T(8,128)(2,1)S(1)}, bf16[128,512]{1,0:T(8,128)(2,1)S(1)}, u32[]{:S(2)}, u32[]{:S(2)}) collective-permute-start(bf16[128,512]{1,0:T(8,128)(2,1)S(1)} %get-tuple-element.65.own_ref), channel_id=1, source_target_pairs={{0,3},{1,2},{2,1},{3,0},{4,7},{5,6},{6,5},{7,4},{8,11},{9,10},{10,... | collective-permute-start | bytes 393224 | tf_op jit(solution)/shard_map/ppermute | solution.py:395
  41.3 8.2 %collective-permute-start.15 = (f32[128,1024]{1,0:T(8,128)S(1)}, f32[128,1024]{1,0:T(8,128)S(1)}, u32[]{:S(2)}, u32[]{:S(2)}) collective-permute-start(f32[128,1024]{1,0:T(8,128)S(1)} %get-tuple-element.73), channel_id=1, source_target_pairs={{0,8},{1,9},{2,10},{3,11},{4,12},{5,13},{6,14},{7,15},{8,0},{9,1},... | collective-permute-start | bytes 1572872 | tf_op jit(solution)/shard_map/ppermute | solution.py:395
  41.9 5.5 %collective-permute-start.19 = (f32[64,512]{1,0:T(8,128)S(1)}, f32[64,512]{1,0:T(8,128)S(1)}, u32[]{:S(2)}, u32[]{:S(2)}) collective-permute-start(f32[64,512]{1,0:T(8,128)S(1)} %get-tuple-element.89), channel_id=1, source_target_pairs={{0,16},{1,17},{2,18},{3,19},{4,20},{5,21},{6,22},{7,23},{8,24},{9,... | collective-permute-start | bytes 393224 | tf_op jit(solution)/shard_map/ppermute | solution.py:395
  42.9 7.6 %collective-permute-start.10 = (bf16[224,128]{1,0:T(8,128)(2,1)S(1)}, bf16[224,128]{1,0:T(8,128)(2,1)S(1)}, u32[]{:S(2)}, u32[]{:S(2)}) collective-permute-start(bf16[224,128]{1,0:T(8,128)(2,1)S(1)} %get-tuple-element.62), channel_id=1, source_target_pairs={{0,2},{2,4},{4,6},{6,0},{1,3},{3,5},{5,7},{7,1},{8,10},{10,12},{12... | collective-permute-start | bytes 172040 | tf_op jit(solution)/shard_map/ppermute | solution.py:21
  43.8 6.7 %collective-permute-start.16 = (bf16[224,128]{1,0:T(8,128)(2,1)S(1)}, bf16[224,128]{1,0:T(8,128)(2,1)S(1)}, u32[]{:S(2)}, u32[]{:S(2)}) collective-permute-start(bf16[224,128]{1,0:T(8,128)(2,1)S(1)} %get-tuple-element.63), channel_id=1, source_target_pairs={{0,6},{2,0},{4,2},{6,4},{1,7},{3,1},{5,3},{7,5},{8,14},{10,8},{12,... | collective-permute-start | bytes 172040 | tf_op jit(solution)/shard_map/ppermute | solution.py:21
  47.4 5.9 %collective-permute-start.24 = (f32[32,512]{1,0:T(8,128)S(1)}, f32[32,512]{1,0:T(8,128)S(1)}, u32[]{:S(2)}, u32[]{:S(2)}) collective-permute-start(f32[32,512]{1,0:T(8,128)S(1)} %slice_add_fusion.11), channel_id=1, source_target_pairs={{0,4},{1,5},{2,6},{3,7},{4,0},{5,1},{6,2},{7,3},{8,12},{9,13},{10,... | collective-permute-start | bytes 196616 | tf_op jit(solution)/shard_map/ppermute | solution.py:395
  49.6 7.2 %collective-permute-start.18 = (f32[64,1024]{1,0:T(8,128)S(1)}, f32[64,1024]{1,0:T(8,128)S(1)}, u32[]{:S(2)}, u32[]{:S(2)}) collective-permute-start(f32[64,1024]{1,0:T(8,128)S(1)} %get-tuple-element.85), channel_id=1, source_target_pairs={{0,16},{1,17},{2,18},{3,19},{4,20},{5,21},{6,22},{7,23},{8,24},{9,... | collective-permute-start | bytes 786440 | tf_op jit(solution)/shard_map/ppermute | solution.py:395
  53.3 4.4 %collective-permute-start.17 = (f32[64,1024]{1,0:T(8,128)S(1)}, f32[64,1024]{1,0:T(8,128)S(1)}, u32[]{:S(2)}, u32[]{:S(2)}) collective-permute-start(f32[64,1024]{1,0:T(8,128)S(1)} %get-tuple-element.81), channel_id=1, source_target_pairs={{0,8},{1,9},{2,10},{3,11},{4,12},{5,13},{6,14},{7,15},{8,0},{9,1},... | collective-permute-start | bytes 786440 | tf_op jit(solution)/shard_map/ppermute | solution.py:395
  54.0 4.7 %collective-permute-start.20 = (bf16[208,128]{1,0:T(8,128)(2,1)S(1)}, bf16[208,128]{1,0:T(8,128)(2,1)S(1)}, u32[]{:S(2)}, u32[]{:S(2)}) collective-permute-start(bf16[208,128]{1,0:T(8,128)(2,1)S(1)} %get-tuple-element.76), channel_id=1, source_target_pairs={{0,1},{1,0},{2,3},{3,2},{4,5},{5,4},{6,7},{7,6},{8,9},{9,8},{10,11... | collective-permute-start | bytes 159752 | tf_op jit(solution)/shard_map/ppermute | solution.py:21
  56.7 8.1 %collective-permute-start.23 = (f32[32,1024]{1,0:T(8,128)S(1)}, f32[32,1024]{1,0:T(8,128)S(1)}, u32[]{:S(2)}, u32[]{:S(2)}) collective-permute-start(f32[32,1024]{1,0:T(8,128)S(1)} %slice_add_fusion.5), channel_id=1, source_target_pairs={{0,4},{1,5},{2,6},{3,7},{4,0},{5,1},{6,2},{7,3},{8,12},{9,13},{10,... | collective-permute-start | bytes 393224 | tf_op jit(solution)/shard_map/ppermute | solution.py:395
  57.7 5.0 %collective-permute-start.21 = (f32[32,1024]{1,0:T(8,128)S(1)}, f32[32,1024]{1,0:T(8,128)S(1)}, u32[]{:S(2)}, u32[]{:S(2)}) collective-permute-start(f32[32,1024]{1,0:T(8,128)S(1)} %get-tuple-element.87), channel_id=1, source_target_pairs={{0,16},{1,17},{2,18},{3,19},{4,20},{5,21},{6,22},{7,23},{8,24},{9,... | collective-permute-start | bytes 393224 | tf_op jit(solution)/shard_map/ppermute | solution.py:395
  62.8 5.2 %collective-permute-start.22 = (f32[16,1024]{1,0:T(8,128)S(1)}, f32[16,1024]{1,0:T(8,128)S(1)}, u32[]{:S(2)}, u32[]{:S(2)}) collective-permute-start(f32[16,1024]{1,0:T(8,128)S(1)} %slice_add_fusion.9), channel_id=1, source_target_pairs={{0,4},{1,5},{2,6},{3,7},{4,0},{5,1},{6,2},{7,3},{8,12},{9,13},{10,... | collective-permute-start | bytes 196616 | tf_op jit(solution)/shard_map/ppermute | solution.py:395
  (5 other events, 27.2 us)
